TPU v7x, 128 devices: a whole 4x4x4 slice. The times are simulated.
128 devices in a mesh: fsdp: 2 (over core), ep: 64 (over z, y, x).
Axes of the slice: x: 4, y: 4, z: 4, core: 2. Of those that a mesh axis runs over, the one named last changes fastest.
Arguments:
- x_tok: bfloat16 [262144, 512], P(('fsdp', 'ep'))
- dy_tok: bfloat16 [262144, 512], P(('fsdp', 'ep'))
- expert_ids: int32 [262144, 2], P(('fsdp', 'ep'))
- route_w: float32 [262144, 2], P(('fsdp', 'ep'))
- w_gate: bfloat16 [128, 512, 512], P('ep', 'fsdp')
- w_up: bfloat16 [128, 512, 512], P('ep', 'fsdp')
- w_down: bfloat16 [128, 512, 512], P('ep', None, 'fsdp')
Outputs:
- output 1: bfloat16 [262144, 512], P(('fsdp', 'ep'))
- output 2: float32 [262144, 2], P(('fsdp', 'ep'))
- output 3: float32 [128, 512, 512], P('ep', 'fsdp')
- output 4: float32 [128, 512, 512], P('ep', 'fsdp')
- output 5: float32 [128, 512, 512], P('ep', None, 'fsdp')
All inputs are finite; a program needn't handle non-finite values.
Results may differ from a plain program's by a relative error of at most 0.001.
Values are sent between devices in bfloat16 or wider.
A program may use at most 1 GiB of HBM per device.

v0:
```python
import jax
import jax.numpy as jnp
from jax import lax
from jax.sharding import PartitionSpec as P

CAP_FACTOR = 3


def capacity_of(tok_dev, top_k, experts):
    return max(8, ((CAP_FACTOR * tok_dev * top_k // experts + 7) // 8) * 8)


def route_slots(ids_dev, experts, capacity):
    n_pairs = ids_dev.shape[0]
    n_slots = experts * capacity
    onehot = (ids_dev[:, None] == jnp.arange(experts, dtype=jnp.int32)[None, :]).astype(jnp.int32)
    before = jnp.cumsum(onehot, axis=0) - onehot
    position = jnp.sum(before * onehot, axis=1)
    dest_slot = jnp.where(position < capacity, ids_dev * capacity + position, n_slots)
    held = jax.ops.segment_sum(jnp.arange(1, n_pairs + 1, dtype=jnp.int32), dest_slot, num_segments=n_slots + 1)[:n_slots]
    slot_src = jnp.where(held > 0, held - 1, n_pairs)
    return dest_slot, slot_src


def swiglu_grads(pre_gate, pre_up, grad_hidden):
    sigma = jax.nn.sigmoid(pre_gate)
    grad_gate = grad_hidden * pre_up * sigma * (1.0 + pre_gate * (1.0 - sigma))
    grad_up = grad_hidden * pre_gate * sigma
    return grad_gate.astype(jnp.bfloat16), grad_up.astype(jnp.bfloat16)


def expert_backward(x_rows, dy_rows, gate_rows, w_gate_full, w_up_full, w_down_full):
    pre_gate = jnp.einsum("secd,edf->secf", x_rows, w_gate_full, preferred_element_type=jnp.float32)
    pre_up = jnp.einsum("secd,edf->secf", x_rows, w_up_full, preferred_element_type=jnp.float32)
    hidden = (jax.nn.silu(pre_gate) * pre_up).astype(jnp.bfloat16)
    y_rows = jnp.einsum("secf,efd->secd", hidden, w_down_full, preferred_element_type=jnp.float32)
    dy_wide = dy_rows.astype(jnp.float32)
    scaled_dy = (gate_rows[..., None] * dy_wide).astype(jnp.bfloat16)
    dr_rows = jnp.sum(dy_wide * y_rows, axis=-1)
    grad_hidden = jnp.einsum("secd,efd->secf", scaled_dy, w_down_full, preferred_element_type=jnp.float32)
    grad_gate, grad_up = swiglu_grads(pre_gate, pre_up, grad_hidden)
    dx_rows = (jnp.einsum("secf,edf->secd", grad_gate, w_gate_full, preferred_element_type=jnp.float32)
               + jnp.einsum("secf,edf->secd", grad_up, w_up_full, preferred_element_type=jnp.float32)).astype(jnp.bfloat16)
    dw_gate = jnp.einsum("secd,secf->edf", x_rows, grad_gate, preferred_element_type=jnp.float32)
    dw_up = jnp.einsum("secd,secf->edf", x_rows, grad_up, preferred_element_type=jnp.float32)
    dw_down = jnp.einsum("secf,secd->efd", hidden, scaled_dy, preferred_element_type=jnp.float32)
    return dx_rows, dr_rows, dw_gate, dw_up, dw_down


def take_rows(rows, row_ids):
    return jnp.take(rows, row_ids, axis=0, mode="fill", fill_value=0)


def solution(mesh):
    n_ep = mesh.shape["ep"]
    tok_spec = P(("fsdp", "ep"), None)
    spec_in = P("ep", "fsdp", None)
    spec_out = P("ep", None, "fsdp")

    def per_device(x_tok, dy_tok, expert_ids, route_w, w_gate, w_up, w_down):
        tok_dev, top_k = expert_ids.shape
        exp_local = w_gate.shape[0]
        d_model = x_tok.shape[1]
        experts = exp_local * n_ep
        capacity = capacity_of(tok_dev, top_k, experts)
        dest_slot, slot_src = route_slots(expert_ids.reshape(-1), experts, capacity)
        tok_of_slot = slot_src // top_k
        x_send = take_rows(x_tok, tok_of_slot)
        dy_send = take_rows(dy_tok, tok_of_slot)
        gate_send = take_rows(route_w.reshape(-1), slot_src)
        x_recv = lax.all_to_all(x_send, "ep", 0, 0, tiled=True).reshape(n_ep, exp_local, capacity, d_model)
        dy_recv = lax.all_to_all(dy_send, "ep", 0, 0, tiled=True).reshape(n_ep, exp_local, capacity, d_model)
        gate_recv = lax.all_to_all(gate_send, "ep", 0, 0, tiled=True).reshape(n_ep, exp_local, capacity)
        w_gate_full = lax.all_gather(w_gate, "fsdp", axis=1, tiled=True)
        w_up_full = lax.all_gather(w_up, "fsdp", axis=1, tiled=True)
        w_down_full = lax.all_gather(w_down, "fsdp", axis=2, tiled=True)
        dx_rows, dr_rows, dw_gate, dw_up, dw_down = expert_backward(
            x_recv, dy_recv, gate_recv, w_gate_full, w_up_full, w_down_full)
        dx_back = lax.all_to_all(dx_rows.reshape(n_ep * exp_local * capacity, d_model), "ep", 0, 0, tiled=True)
        dr_back = lax.all_to_all(dr_rows.reshape(-1), "ep", 0, 0, tiled=True)
        dx_pairs = take_rows(dx_back, dest_slot).reshape(tok_dev, top_k, d_model)
        grad_x = jnp.sum(dx_pairs.astype(jnp.float32), axis=1).astype(jnp.bfloat16)
        route_grad = take_rows(dr_back, dest_slot).reshape(tok_dev, top_k)
        grad_w_gate = lax.psum_scatter(dw_gate, "fsdp", scatter_dimension=1, tiled=True)
        grad_w_up = lax.psum_scatter(dw_up, "fsdp", scatter_dimension=1, tiled=True)
        grad_w_down = lax.psum_scatter(dw_down, "fsdp", scatter_dimension=2, tiled=True)
        return grad_x, route_grad, grad_w_gate, grad_w_up, grad_w_down

    return jax.shard_map(
        per_device, mesh=mesh,
        in_specs=(tok_spec, tok_spec, tok_spec, tok_spec, spec_in, spec_in, spec_out),
        out_specs=(tok_spec, tok_spec, spec_in, spec_in, spec_out),
        check_vma=False)
```

profile of v0, /device:TPU:32, one launch (start us, length us, event | category | flops | bytes accessed | tf_op | source)
XLA Modules:
  0.0 1005.5 jit_solution(191149440614518836)
XLA Ops:
  14.3 2.5 copy.47
  18.7 2.5 fusion.27
  21.9 21.9 %scatter_custom_fusion = s32[12289]{0:T(1024)S(1)} fusion(s32[4096]{0:T(1024)S(1)} %bitcast.111, s32[4096]{0:T(1024)S(1)} %iota_add_fusion, s32[]{:T(128)} %constant.58.clone.1), kind=kCustom, calls=%fused_computation.82 | custom fusion | flops 4096 | bytes 49160 | tf_op jit(solution)/shard_map/scatter-add | solution.py:20
  46.9 68.0 %gather_fusion = f32[12288]{0:T(1024)S(1)} fusion(f32[4096]{0:T(1024)S(1)} %reshape.171, s32[12288]{0:T(1024)S(1)} %get-tuple-element.30), kind=kCustom, calls=%fused_computation.2 | custom fusion | bytes 147456 | tf_op jit(solution)/shard_map/jit(_take)/gather | solution.py:51
  115.8 11.1 %all-to-all-start = ((f32[64,192,1]{1,2,0:T(1,128)}), f32[64,192,1]{1,2,0:T(1,128)S(1)}, u32[]{:S(2)}, u32[]{:S(2)}) async-start(f32[64,192,1]{1,2,0:T(1,128)} %copy.50), calls=%async_computation | async-start | bytes 131072 | tf_op jit(solution)/shard_map/all_to_all | solution.py:73
  127.0 50.0 %gather_fusion.3 = bf16[12288,512]{1,0:T(8,128)(2,1)} fusion(bf16[2048,512]{1,0:T(8,128)(2,1)S(1)} %copy-done, s32[12288]{0:T(1024)S(1)} %get-tuple-element.29), kind=kCustom, calls=%fused_computation.clone | custom fusion | bytes 25214976 | tf_op jit(solution)/shard_map/jit(_take)/gather | solution.py:51
  177.0 52.2 %gather_fusion.4 = bf16[12288,512]{1,0:T(8,128)(2,1)} fusion(bf16[2048,512]{1,0:T(8,128)(2,1)} %param.9, s32[12288]{0:T(1024)S(1)} %get-tuple-element.29), kind=kCustom, calls=%fused_computation.1.clone | custom fusion | bytes 25214976 | tf_op jit(solution)/shard_map/jit(_take)/gather | solution.py:51
  229.2 17.2 %broadcast_select_fusion.1 = (bf16[12288,512]{1,0:T(8,128)(2,1)}, bf16[12288,512]{1,0:T(8,128)(2,1)}) fusion(bf16[12288,512]{1,0:T(8,128)(2,1)} %gather_fusion.3, pred[12288]{0:T(1024)(128)(4,1)S(1)} %compare_and_fusion.1, bf16[12288,512]{1,0:T(8,128)(2,1)} %gather_fusion.4), kind=kLoop, calls=%fused_computation.32 | loop fusion | flops 12582912 | bytes 50343936 | tf_op jit(solution)/shard_map/jit(_take)/select_n | solution.py:51
  246.4 172.5 %all_to_all.49 = bf16[64,192,512]{2,1,0:T(8,128)(2,1)} all-to-all(bf16[64,192,512]{2,1,0:T(8,128)(2,1)} %bitcast.105), channel_id=1, replica_groups=mesh['fsdp'=2,'ep'=64] {'ep'}, dimensions={0} | all-to-all | bytes 25165824 | tf_op jit(solution)/shard_map/all_to_all | solution.py:72
  418.9 17.4 %all-to-all-start.2 = ((bf16[64,192,512]{2,1,0:T(8,128)(2,1)}), bf16[64,192,512]{2,1,0:T(8,128)(2,1)}, u32[]{:S(2)}, u32[]{:S(2)}) async-start(bf16[64,192,512]{2,1,0:T(8,128)(2,1)} %bitcast.104), calls=%async_computation.2 | async-start | bytes 25165824 | tf_op jit(solution)/shard_map/all_to_all | solution.py:71
  438.8 12.7 %all-gather.4.cloned.1.call-done = bf16[2,512,512]{2,1,0:T(8,128)(2,1)} async-done(((bf16[2,512,256]{2,1,0:T(8,128)(2,1)}), bf16[2,512,512]{2,1,0:T(8,128)(2,1)}) %all-gather.4.cloned.1.call-update) | async-done | bytes 1048592 | tf_op jit(solution)/shard_map/all_gather | solution.py:76
  451.6 16.3 %fusion.23 = f32[2,64,96,512]{3,2,1,0:T(8,128)} fusion(bf16[2,512,512]{2,1,0:T(8,128)(2,1)} %all-gather.4.cloned.1.call-done, f32[64,2,96]{2,1,0:T(2,128)S(1)} %mul.65, bf16[64,2,96,512]{3,2,1,0:T(8,128)(2,1)} %bitcast.106), kind=kOutput, calls=%fused_computation.39 | convolution fusion | flops 6461325312 | bytes 38846464 | tf_op jit(solution)/shard_map/secd,efd->secf/dot_general | solution.py:40
  467.9 158.4 %all-to-all-done.2 = bf16[64,192,512]{2,1,0:T(8,128)(2,1)} async-done(((bf16[64,192,512]{2,1,0:T(8,128)(2,1)}), bf16[64,192,512]{2,1,0:T(8,128)(2,1)}, u32[]{:S(2)}, u32[]{:S(2)}) %all-to-all-start.2) | async-done | bytes 12582944 | tf_op jit(solution)/shard_map/all_to_all | solution.py:71
  626.3 14.8 %fusion.19 = f32[2,64,96,512]{3,2,1,0:T(8,128)} fusion(bf16[64,2,96,512]{3,2,1,0:T(8,128)(2,1)} %bitcast.11, bf16[2,512,512]{2,1,0:T(8,128)(2,1)} %all-gather.6.cloned.1.call-done), kind=kOutput, calls=%fused_computation.35 | convolution fusion | flops 6442450944 | bytes 38797312 | tf_op jit(solution)/shard_map/secd,edf->secf/dot_general | solution.py:34
  641.1 35.0 %fusion.10 = (bf16[64,2,96,512]{3,2,0,1:T(8,128)(2,1)}, bf16[64,2,96,512]{3,2,0,1:T(8,128)(2,1)}, bf16[64,2,96,512]{3,2,0,1:T(8,128)(2,1)}) fusion(f32[2,64,96,512]{3,2,1,0:T(8,128)} %fusion.19, f32[2,64,96,512]{3,2,1,0:T(8,128)} %fusion.23, bf16[2,512,512]{2,1,0:T(8,128)(2,1)} %all-gather.8.cloned.1.call-done, bf16[64,2,96,512]{3,2,1,0:T(8,128)(2,1)} %bitcast.11), kind=kOutput, calls=%fused_computation.21 | convolution fusion | flops 6543114240 | bytes 101711872 | tf_op jit(solution)/shard_map/secd,edf->secf/dot_general | solution.py:33
  676.1 12.3 %fusion = f32[64,2,96]{2,0,1:T(8,128)S(1)} fusion(bf16[64,2,96,512]{3,2,0,1:T(8,128)(2,1)} %get-tuple-element.25, bf16[2,512,512]{2,1,0:T(8,128)(2,1)S(1)} %copy-done.13, bf16[64,2,96,512]{3,2,1,0:T(8,128)(2,1)} %bitcast.107), kind=kOutput, calls=%fused_computation.7 | convolution fusion | flops 6461313024 | bytes 26263552 | tf_op jit(solution)/shard_map/secf,efd->secd/dot_general | solution.py:36
  689.2 17.4 %all-to-all-start.4 = ((f32[64,192,1]{1,2,0:T(1,128)}), f32[64,192,1]{1,2,0:T(1,128)S(1)}, u32[]{:S(2)}, u32[]{:S(2)}) async-start(f32[64,192,1]{1,2,0:T(1,128)} %all_to_all.43), calls=%async_computation.4 | async-start | bytes 131072 | tf_op jit(solution)/shard_map/all_to_all | solution.py:80
  706.6 14.6 %fusion.39 = f32[2,64,96,512]{3,2,1,0:T(8,128)} fusion(bf16[64,2,96,512]{3,2,0,1:T(8,128)(2,1)} %get-tuple-element.26, bf16[2,512,512]{2,1,0:T(8,128)(2,1)S(1)} %copy-done.6), kind=kOutput, calls=%fused_computation.54 | convolution fusion | flops 6442450944 | bytes 38797312 | tf_op jit(solution)/shard_map/secf,edf->secd/dot_general | solution.py:42
  721.2 18.8 %fusion.12 = bf16[64,2,96,512]{3,2,0,1:T(8,128)(2,1)} fusion(f32[2,64,96,512]{3,2,1,0:T(8,128)} %fusion.39, bf16[64,2,96,512]{3,2,0,1:T(8,128)(2,1)} %get-tuple-element.27, bf16[2,512,512]{2,1,0:T(8,128)(2,1)S(1)} %copy-done.5), kind=kOutput, calls=%fused_computation.26 | convolution fusion | flops 6455033856 | bytes 51380224 | tf_op jit(solution)/shard_map/secf,edf->secd/dot_general | solution.py:43
  740.0 10.9 %copy.54 = bf16[64,2,96,512]{3,2,1,0:T(8,128)(2,1)} copy(bf16[64,2,96,512]{3,2,0,1:T(8,128)(2,1)} %fusion.12) | data formatting | bytes 25165824 | tf_op jit(solution)/shard_map/convert_element_type | solution.py:43
  750.9 10.6 %all-to-all-start.3 = ((bf16[64,192,512]{2,1,0:T(8,128)(2,1)}), bf16[64,192,512]{2,1,0:T(8,128)(2,1)}, u32[]{:S(2)}, u32[]{:S(2)}) async-start(bf16[64,192,512]{2,1,0:T(8,128)(2,1)} %bitcast.103), calls=%async_computation.3 | async-start | bytes 25165824 | tf_op jit(solution)/shard_map/all_to_all | solution.py:79
  761.6 13.4 %fusion.30 = f32[2,512,512]{2,1,0:T(8,128)} fusion(bf16[64,2,96,512]{3,2,0,1:T(8,128)(2,1)} %get-tuple-element.25, f32[64,2,96]{2,1,0:T(2,128)S(1)} %copy-done.10, bf16[64,2,96,512]{3,2,1,0:T(8,128)(2,1)} %bitcast.108), kind=kOutput, calls=%fused_computation.51 | convolution fusion | flops 6461325312 | bytes 27312128 | tf_op jit(solution)/shard_map/secf,secd->efd/dot_general | solution.py:46
  775.1 14.5 %fusion.33 = f32[2,512,512]{2,1,0:T(8,128)} fusion(bf16[64,2,96,512]{3,2,1,0:T(8,128)(2,1)} %bitcast.11, bf16[64,2,96,512]{3,2,0,1:T(8,128)(2,1)} %get-tuple-element.26), kind=kOutput, calls=%fused_computation.52 | convolution fusion | flops 6442450944 | bytes 27262976 | tf_op jit(solution)/shard_map/secd,secf->edf/dot_general | solution.py:44
  789.7 14.3 %fusion.36 = f32[2,512,512]{2,1,0:T(8,128)} fusion(bf16[64,2,96,512]{3,2,1,0:T(8,128)(2,1)} %bitcast.11, bf16[64,2,96,512]{3,2,0,1:T(8,128)(2,1)} %get-tuple-element.27), kind=kOutput, calls=%fused_computation.53 | convolution fusion | flops 6442450944 | bytes 27262976 | tf_op jit(solution)/shard_map/secd,secf->edf/dot_general | solution.py:45
  805.3 23.0 %gather_fusion.2 = f32[4096]{0:T(1024)S(1)} fusion(f32[12288]{0:T(1024)S(1)} %all_to_all.42, s32[4096]{0:T(1024)S(1)} %broadcast_clamp_fusion.1), kind=kCustom, calls=%fused_computation.4 | custom fusion | bytes 49152 | tf_op jit(solution)/shard_map/jit(_take)/gather | solution.py:51
  828.4 2.0 gather.26
  830.4 2.6 broadcast_select_fusion.3
  833.0 2.2 copy.61
  835.1 116.4 %all-to-all-done.3 = bf16[64,192,512]{2,1,0:T(8,128)(2,1)} async-done(((bf16[64,192,512]{2,1,0:T(8,128)(2,1)}), bf16[64,192,512]{2,1,0:T(8,128)(2,1)}, u32[]{:S(2)}, u32[]{:S(2)}) %all-to-all-start.3) | async-done | bytes 12582944 | tf_op jit(solution)/shard_map/all_to_all | solution.py:79
  951.5 23.8 %gather_fusion.1 = bf16[4096,512]{1,0:T(8,128)(2,1)} fusion(bf16[12288,512]{1,0:T(8,128)(2,1)} %bitcast.21, s32[4096]{0:T(1024)S(1)} %broadcast_clamp_fusion.1), kind=kCustom, calls=%fused_computation.3 | custom fusion | bytes 8404992 | tf_op jit(solution)/shard_map/jit(_take)/gather | solution.py:51
  975.3 7.2 gather.24
  982.5 15.9 %fusion.25 = bf16[2048,512]{1,0:T(8,128)(2,1)} fusion(bf16[2048,2,512]{2,1,0:T(2,128)(2,1)} %gather.24, pred[2048,2]{1,0:T(8,128)(4,1)S(1)} %get-tuple-element.22), kind=kLoop, calls=%fused_computation.42 | loop fusion | flops 3145728 | bytes 6295552 | tf_op jit(solution)/shard_map/reduce_sum | solution.py:82
  (76 shorter events, 18.4 us)
Async XLA Ops:
  7.2 119.8 %copy-start = (bf16[2048,512]{1,0:T(8,128)(2,1)S(1)}, bf16[2048,512]{1,0:T(8,128)(2,1)}, u32[]{:S(2)}) copy-start(bf16[2048,512]{1,0:T(8,128)(2,1)} %param.10) | copy-start | bytes 6291460
  7.2 36.7 %copy-start.12 = (f32[2048,2]{0,1:T(2,128)S(1)}, f32[2048,2]{0,1:T(2,128)}, u32[]{:S(2)}) copy-start(f32[2048,2]{0,1:T(2,128)} %param.12) | copy-start | bytes 49156
  8.4 35.4 %copy-start.2 = (s32[2048,2]{1,0:T(8,128)}, s32[2048,2]{1,0:T(8,128)S(1)}, u32[]{:S(2)}) copy-start(s32[2048,2]{1,0:T(8,128)S(1)} %copy.44) | copy-start | bytes 49156
  11.1 1.3 copy-start.4
  21.2 0.7 copy-start.7
  115.8 130.6 %all-to-all-start = ((f32[64,192,1]{1,2,0:T(1,128)}), f32[64,192,1]{1,2,0:T(1,128)S(1)}, u32[]{:S(2)}, u32[]{:S(2)}) async-start(f32[64,192,1]{1,2,0:T(1,128)} %copy.50), calls=%async_computation | async-start | bytes 131072 | tf_op jit(solution)/shard_map/all_to_all | solution.py:73
  418.9 207.3 %all-to-all-start.2 = ((bf16[64,192,512]{2,1,0:T(8,128)(2,1)}), bf16[64,192,512]{2,1,0:T(8,128)(2,1)}, u32[]{:S(2)}, u32[]{:S(2)}) async-start(bf16[64,192,512]{2,1,0:T(8,128)(2,1)} %bitcast.104), calls=%async_computation.2 | async-start | bytes 25165824 | tf_op jit(solution)/shard_map/all_to_all | solution.py:71
  436.3 15.2 %all-gather.4.cloned.1.call-start = ((), (), s32[]{:S(2)}) async-start(), calls=%async_computation.8 | async-start | bytes 1572864 | tf_op jit(solution)/shard_map/all_gather | solution.py:76
  437.1 30.8 %all-gather.6.cloned.1.call-start = ((), (), s32[]{:S(2)}) async-start(), calls=%async_computation.9 | async-start | bytes 1572864 | tf_op jit(solution)/shard_map/all_gather | solution.py:75
  437.8 203.3 %all-gather.8.cloned.1.call-start = ((), (), s32[]{:S(2)}) async-start(), calls=%async_computation.10 | async-start | bytes 1572864 | tf_op jit(solution)/shard_map/all_gather | solution.py:74
  438.8 29.1 %copy-start.9 = (f32[64,2,96]{2,1,0:T(2,128)}, f32[64,2,96]{2,1,0:T(2,128)S(1)}, u32[]{:S(2)}) copy-start(f32[64,2,96]{2,1,0:T(2,128)S(1)} %mul.65) | copy-start | bytes 147460
  641.1 35.0 %copy-start.13 = (bf16[2,512,512]{2,1,0:T(8,128)(2,1)S(1)}, bf16[2,512,512]{2,1,0:T(8,128)(2,1)}, u32[]{:S(2)}) copy-start(bf16[2,512,512]{2,1,0:T(8,128)(2,1)} %all-gather.4.cloned.1.call-done) | copy-start | bytes 3145732
  676.1 30.5 %copy-start.6 = (bf16[2,512,512]{2,1,0:T(8,128)(2,1)S(1)}, bf16[2,512,512]{2,1,0:T(8,128)(2,1)}, u32[]{:S(2)}) copy-start(bf16[2,512,512]{2,1,0:T(8,128)(2,1)} %all-gather.8.cloned.1.call-done) | copy-start | bytes 3145732
  689.2 61.7 %all-to-all-start.4 = ((f32[64,192,1]{1,2,0:T(1,128)}), f32[64,192,1]{1,2,0:T(1,128)S(1)}, u32[]{:S(2)}, u32[]{:S(2)}) async-start(f32[64,192,1]{1,2,0:T(1,128)} %all_to_all.43), calls=%async_computation.4 | async-start | bytes 131072 | tf_op jit(solution)/shard_map/all_to_all | solution.py:80
  706.6 14.6 %copy-start.5 = (bf16[2,512,512]{2,1,0:T(8,128)(2,1)S(1)}, bf16[2,512,512]{2,1,0:T(8,128)(2,1)}, u32[]{:S(2)}) copy-start(bf16[2,512,512]{2,1,0:T(8,128)(2,1)} %all-gather.6.cloned.1.call-done) | copy-start | bytes 3145732
  750.9 10.7 %copy-start.10 = (f32[64,2,96]{2,1,0:T(2,128)S(1)}, f32[64,2,96]{2,1,0:T(2,128)}, u32[]{:S(2)}) copy-start(f32[64,2,96]{2,1,0:T(2,128)} %copy-done.9) | copy-start | bytes 147460
  750.9 200.7 %all-to-all-start.3 = ((bf16[64,192,512]{2,1,0:T(8,128)(2,1)}), bf16[64,192,512]{2,1,0:T(8,128)(2,1)}, u32[]{:S(2)}, u32[]{:S(2)}) async-start(bf16[64,192,512]{2,1,0:T(8,128)(2,1)} %bitcast.103), calls=%async_computation.3 | async-start | bytes 25165824 | tf_op jit(solution)/shard_map/all_to_all | solution.py:79
  761.5 236.9 %reduce-scatter.8.cloned.1.call-start = ((), (), s32[]{:S(2)}) async-start(), calls=%async_computation.13 | async-start | bytes 3145728 | tf_op jit(solution)/shard_map/reduce_scatter | solution.py:86
  775.0 223.4 %reduce-scatter.4.cloned.1.call-start = ((), (), s32[]{:S(2)}) async-start(), calls=%async_computation.11 | async-start | bytes 3145728 | tf_op jit(solution)/shard_map/reduce_scatter | solution.py:84
  789.6 14.4 %copy-start.8 = (s32[4096]{0:T(1024)S(1)}, s32[4096]{0:T(1024)}, u32[]{:S(2)}) copy-start(s32[4096]{0:T(1024)} %copy-done.7) | copy-start | bytes 49156
  789.6 15.4 %copy-start.11 = (s32[4096,1]{0,1:T(1,128)S(1)}, s32[4096,1]{0,1:T(1,128)}, u32[]{:S(2)}) copy-start(s32[4096,1]{0,1:T(1,128)} %get-tuple-element.23) | copy-start | bytes 49156
  789.6 208.8 %reduce-scatter.6.cloned.1.call-start = ((), (), s32[]{:S(2)}) async-start(), calls=%async_computation.12 | async-start | bytes 3145728 | tf_op jit(solution)/shard_map/reduce_scatter | solution.py:85
  804.0 26.4 %copy-start.3 = (s32[2048,2]{1,0:T(8,128)S(1)}, s32[2048,2]{1,0:T(8,128)}, u32[]{:S(2)}) copy-start(s32[2048,2]{1,0:T(8,128)} %copy-done.2) | copy-start | bytes 49156
  951.5 46.9 %copy-start.1 = (bf16[2048,512]{1,0:T(8,128)(2,1)S(1)}, bf16[2048,512]{1,0:T(8,128)(2,1)}, u32[]{:S(2)}) copy-start(bf16[2048,512]{1,0:T(8,128)(2,1)} %param.10) | copy-start | bytes 6291460
Sparse Core Ops, SparseCore 0:
  438.8 12.7 all-gather.3
  453.2 12.9 all-gather.5
  467.8 12.9 all-gather.7
  775.1 13.2 reduce-scatter.7
  791.2 13.2 reduce-scatter.3
  807.3 13.2 reduce-scatter.5
where the time goes:
time: 1010 us
  waiting for transfers between devices  290 us (29%)
  local copies, waits for them, and re-layouts  253 us (25%)
  blocking collectives  173 us (17%)
  matrix products  154 us (15%)
  other arithmetic  64.8 us (6%)
  starting transfers between devices  56.7 us (6%)
  between operations  14.6 us (1%)
    gather x8, local copies, waits for them, and re-layouts, take_rows(): return jnp.take(rows, row_ids, axis=0, mode='fill', fill_value=0)  226 us
    all_to_all x1, blocking collectives, per_device(): lax.all_to_all(dy_send, 'ep', 0, 0, tiled=True)  173 us
    all_to_all x1, waiting for transfers between devices, per_device(): lax.all_to_all(x_send, 'ep', 0, 0, tiled=True)  158 us
    all_to_all x1, waiting for transfers between devices, per_device(): lax.all_to_all(dx_rows.reshape(n_ep * exp_local * capacity, d_model), 'ep...  116 us
    dot_general x1, matrix products, expert_backward(): jnp.einsum('secd,edf->secf', x_rows, w_gate_full, preferred_element_type=...  35 us
    scatter-add x1, other arithmetic, route_slots(): jax.ops.segment_sum(jnp.arange(1, n_pairs + 1, dtype=jnp.int32), dest_slo...  21.9 us
    select_n x4, other arithmetic, take_rows(): return jnp.take(rows, row_ids, axis=0, mode='fill', fill_value=0)  20.5 us
  transfers between devices with their start and end apart: 10, of which 3 were waited for; matrix products, arithmetic and copies ran while one was open for 31% of the time, Pallas kernels for 0%

commit v1 on v0

v1 whole, which is shorter than its diff:
```python
import functools

import jax
import jax.numpy as jnp
from jax import lax
from jax.experimental import pallas as pl
from jax.experimental.pallas import tpu as pltpu
from jax.sharding import PartitionSpec as P

CAP_FACTOR = 3
LANES = 128
ROWS_G = 256
FAR = 1 << 20
f32, bf16, i32 = jnp.float32, jnp.bfloat16, jnp.int32


def capacity_of(tok_dev, top_k, experts):
    return max(8, ((CAP_FACTOR * tok_dev * top_k // experts + 7) // 8) * 8)


def iota(shape, dim):
    return lax.broadcasted_iota(i32, shape, dim)


def nn(a, b):
    return jnp.dot(a, b, preferred_element_type=f32)


def nt(a, b):
    return lax.dot_general(a, b, (((1,), (1,)), ((), ())), preferred_element_type=f32)


def tn(a, b):
    return lax.dot_general(a, b, (((0,), (0,)), ((), ())), preferred_element_type=f32)


def split3(v):
    hi = v.astype(bf16)
    rest = v - hi.astype(f32)
    mid = rest.astype(bf16)
    lo = (rest - mid.astype(f32)).astype(bf16)
    return hi, mid, lo


def add3(v, n):
    return v[:, :n] + v[:, n:2 * n] + v[:, 2 * n:]


def exact(a, b):
    return jnp.dot(a, b, preferred_element_type=f32, precision=lax.Precision.HIGHEST)


def route_kernel(capacity, rows, span, ids_ref, rw_ref, q_ref, msg_ref):
    experts, chunk = LANES, 256
    tokens = ids_ref.shape[1]
    n_dest = msg_ref.shape[0]
    before = (iota((chunk, chunk), 0) < iota((chunk, chunk), 1)).astype(bf16)
    expert_id = iota((experts, chunk), 0)
    slot_id = iota((span, chunk), 0)
    half_id = iota((n_dest, chunk), 0) * 2
    seen = jnp.zeros((experts, 1), f32)
    gates = [jnp.zeros((3 * n_dest, span), f32) for _ in range(2)]
    for c in range(tokens // chunk):
        at = slice(c * chunk, (c + 1) * chunk)
        id_rows = [ids_ref[j:j + 1, at] for j in range(2)]
        hits = [expert_id == row for row in id_rows]
        member = jnp.where(hits[0] | hits[1], 1.0, 0.0)
        earlier = nn(member.astype(bf16), before) + seen
        seen = seen + jnp.sum(member, axis=1, keepdims=True)
        for j in range(2):
            place = jnp.sum(jnp.where(hits[j], earlier, 0.0), axis=0, keepdims=True).astype(i32)
            slot = jnp.where(id_rows[j] % 2 == 0, place, rows - 1 - place)
            slot = jnp.where(place < capacity, slot, FAR)
            q_ref[j:j + 1, at] = jnp.where(place < capacity, (id_rows[j] // 2) * rows + slot, FAR)
            slot_hot = jnp.where(slot_id == slot, 1.0, 0.0).astype(bf16)
            weight = rw_ref[j:j + 1, at]
            for par in range(2):
                mine = jnp.where(half_id + par == id_rows[j], weight, 0.0)
                gates[par] = gates[par] + nt(jnp.concatenate(split3(mine), axis=0), slot_hot)
    kept = jnp.broadcast_to(jnp.minimum(seen, float(capacity)), (experts, LANES)).astype(bf16)
    owner = (iota((n_dest, experts), 1) // 2 == iota((n_dest, experts), 0)).astype(bf16)
    over = jnp.where(nn(owner, kept) > float(rows), 1.0, 0.0)
    for par in range(2):
        g = gates[par]
        msg_ref[:, par * span:(par + 1) * span] = g[:n_dest] + g[n_dest:2 * n_dest] + g[2 * n_dest:]
    msg_ref[:, 2 * span:] = jnp.broadcast_to(jnp.max(over, axis=0, keepdims=True), (n_dest, LANES))


def pack_kernel(q_ref, x_ref, dy_ref, out_ref):
    d = x_ref.shape[1]
    row = iota((ROWS_G, q_ref.shape[1]), 0) + pl.program_id(0) * ROWS_G
    pick = jnp.where((q_ref[0:1, :] == row) | (q_ref[1:2, :] == row), 1.0, 0.0).astype(bf16)
    out_ref[:, :d] = nn(pick, x_ref[...]).astype(bf16)
    out_ref[:, d:] = nn(pick, dy_ref[...]).astype(bf16)


def expert_kernel(depth, span, xdy_ref, rec_ref, wg_ref, wu_ref, wd_ref,
                  dx_ref, dr_ref, dwg_ref, dwu_ref, dwd_ref, w2_ref):
    step = pl.program_id(0)
    group, rows, width = xdy_ref.shape
    n_src = rec_ref.shape[0]
    d = width // 2
    half = wg_ref.shape[2]
    m = group * depth

    @pl.when(step == 0)
    def _():
        for ref in (dr_ref, dwg_ref, dwu_ref, dwd_ref):
            ref[...] = jnp.zeros_like(ref)
        for k in range(2):
            for i in range(2):
                w2_ref[k, :, i * half:(i + 1) * half] = wd_ref[i, k]

    local = iota((m, n_src), 0) // depth + step * group
    src_hot = jnp.where(local == iota((m, n_src), 1), 1.0, 0.0).astype(bf16)
    within = iota((m, span), 0) % depth
    outs = []
    for k in range(2):
        first = 0 if k == 0 else rows - depth
        slot_hot = iota((m, span), 1) == within + first
        gate_parts = jnp.concatenate(split3(rec_ref[:, k * span:(k + 1) * span]), axis=1)
        weight = jnp.sum(jnp.where(slot_hot, add3(nn(src_hot, gate_parts), span), 0.0), axis=1, keepdims=True)
        x = xdy_ref[:, first:first + depth, :d].reshape(m, d)
        dy = xdy_ref[:, first:first + depth, d:].reshape(m, d).astype(f32)
        w1 = wg_ref[:, k].reshape(d, wg_ref.shape[3])
        w3 = wu_ref[:, k].reshape(d, wu_ref.shape[3])
        w2 = w2_ref[k]
        h1 = nn(x, w1)
        h3 = nn(x, w3)
        s = jax.nn.sigmoid(h1)
        hidden = (h1 * s * h3).astype(bf16)
        dr = jnp.sum(dy * nn(hidden, w2), axis=1, keepdims=True)
        g = (weight * dy).astype(bf16)
        da = nt(g, w2)
        dh1 = (da * h3 * s * (1.0 + h1 * (1.0 - s))).astype(bf16)
        dh3 = (da * h1 * s).astype(bf16)
        outs.append((nt(dh1, w1) + nt(dh3, w3)).reshape(group, depth, d))
        dwg_ref[k] += tn(x, dh1)
        dwu_ref[k] += tn(x, dh3)
        dwd_ref[k] += tn(hidden, g)
        parts = jnp.concatenate(split3(jnp.where(slot_hot, dr, 0.0)), axis=1)
        dr_ref[:, k * span:(k + 1) * span] += add3(tn(src_hot, parts), span)
    low = rows - depth
    dx_ref[:, :low] = outs[0][:, :low].astype(bf16)
    if depth > low:
        dx_ref[:, low:depth] = (outs[0][:, low:] + outs[1][:, :depth - low]).astype(bf16)
    dx_ref[:, depth:] = outs[1][:, depth - low:].astype(bf16)


def dr_kernel(rows, span, ids_ref, q_ref, back_ref, out_ref):
    n_src = back_ref.shape[0]
    tokens = ids_ref.shape[1]
    table = back_ref[...].T
    chunk = 512
    for c in range(tokens // chunk):
        at = slice(c * chunk, (c + 1) * chunk)
        for j in range(2):
            ids = ids_ref[j:j + 1, at]
            q = q_ref[j:j + 1, at]
            owner = jnp.where(iota((n_src, chunk), 0) == ids // 2, 1.0, 0.0)
            column = exact(table, owner)
            want = jnp.where(q < FAR, (ids % 2) * span + q - (ids // 2) * rows, FAR)
            out_ref[j:j + 1, at] = jnp.sum(
                jnp.where(iota((2 * span, chunk), 0) == want, column, 0.0), axis=0, keepdims=True)


def combine_kernel(q_ref, back_ref, out_ref):
    rows, depth = q_ref.shape[0], 512
    q0, q1 = q_ref[:, 0:1], q_ref[:, 1:2]

    def body(i, acc):
        at = i * depth
        column = iota((rows, depth), 1) + at
        pick = jnp.where((q0 == column) | (q1 == column), 1.0, 0.0).astype(bf16)
        return acc + nn(pick, back_ref[pl.ds(pl.multiple_of(at, depth), depth), :])

    steps = back_ref.shape[0] // depth
    out_ref[...] = lax.fori_loop(0, steps, body, jnp.zeros(out_ref.shape, f32)).astype(bf16)


def vmem():
    return pl.BlockSpec(memory_space=pltpu.VMEM)


def whole(shape):
    return pl.BlockSpec(shape, lambda i: (0,) * len(shape))


PARAMS = pltpu.CompilerParams(vmem_limit_bytes=60 * 1024 * 1024)


def exchange(v):
    return lax.all_to_all(v, "ep", 0, 0, tiled=True)


class Plan:
    def __init__(self, rows, depth, group, capacity, n_ep):
        self.rows, self.depth, self.group, self.capacity, self.n_ep = rows, depth, group, capacity, n_ep
        self.span = -(-rows // LANES) * LANES

    def forward(self, x_tok, dy_tok, ids_t, rw_t, weights):
        tok_dev, d = x_tok.shape
        n_ep, rows, span = self.n_ep, self.rows, self.span
        q_t, msg = pl.pallas_call(
            functools.partial(route_kernel, self.capacity, rows, span),
            out_shape=(jax.ShapeDtypeStruct((2, tok_dev), i32), jax.ShapeDtypeStruct((n_ep, 2 * span + LANES), f32)),
            in_specs=[vmem(), vmem()], out_specs=(vmem(),) * 2, compiler_params=PARAMS, name="route",
        )(ids_t, rw_t)
        rec = exchange(msg)
        packed = pl.pallas_call(
            pack_kernel,
            out_shape=jax.ShapeDtypeStruct((n_ep * rows, 2 * d), bf16),
            grid=(n_ep * rows // ROWS_G,),
            in_specs=[whole((2, tok_dev)), whole((tok_dev, d)), whole((tok_dev, d))],
            out_specs=pl.BlockSpec((ROWS_G, 2 * d), lambda i: (i, 0)),
            compiler_params=PARAMS, name="pack",
        )(q_t, x_tok, dy_tok)
        xdy = exchange(packed.reshape(n_ep, rows, 2 * d))
        dx, dr, dwg, dwu, dwd = self.experts(xdy, rec, weights)
        dx_back = exchange(dx).reshape(n_ep * rows, d)
        dr_back = exchange(dr)
        dr_t = pl.pallas_call(
            functools.partial(dr_kernel, rows, span),
            out_shape=jax.ShapeDtypeStruct((2, tok_dev), f32),
            in_specs=[vmem()] * 3, out_specs=vmem(), compiler_params=PARAMS, name="route_grad",
        )(ids_t, q_t, dr_back)
        return rec[:, 2 * span:], q_t, dx_back, dr_t, (dwg, dwu, dwd)

    def experts(self, xdy, rec, weights):
        n_ep, rows, width = xdy.shape
        d, group, span = width // 2, self.group, self.span
        wg, wu, wd = weights
        ff = wg.shape[3]
        return pl.pallas_call(
            functools.partial(expert_kernel, self.depth, span),
            out_shape=(jax.ShapeDtypeStruct((n_ep, rows, d), bf16),
                       jax.ShapeDtypeStruct((n_ep, 2 * span), f32),
                       jax.ShapeDtypeStruct((2, d, ff), f32),
                       jax.ShapeDtypeStruct((2, d, ff), f32),
                       jax.ShapeDtypeStruct((2, ff, d), f32)),
            grid=(n_ep // group,),
            in_specs=[pl.BlockSpec((group, rows, width), lambda i: (i, 0, 0)),
                      whole(rec.shape), whole(wg.shape), whole(wu.shape), whole(wd.shape)],
            out_specs=(pl.BlockSpec((group, rows, d), lambda i: (i, 0, 0)),
                       whole((n_ep, 2 * span)), whole((2, d, ff)), whole((2, d, ff)), whole((2, ff, d))),
            scratch_shapes=[pltpu.VMEM((2, ff, d), bf16)],
            compiler_params=PARAMS, name="experts",
        )(xdy, rec, wg, wu, wd)

    def combine(self, q_t, dx_back):
        tok_dev, (slots, d), tile = q_t.shape[1], dx_back.shape, 256
        return pl.pallas_call(
            combine_kernel,
            out_shape=jax.ShapeDtypeStruct((tok_dev, d), bf16),
            grid=(tok_dev // tile,),
            in_specs=[pl.BlockSpec((tile, 2), lambda i: (i, 0)), whole((slots, d))],
            out_specs=pl.BlockSpec((tile, d), lambda i: (i, 0)),
            compiler_params=PARAMS, name="combine",
        )(q_t.T, dx_back)


def solution(mesh):
    n_ep = mesh.shape["ep"]
    tok_spec = P(("fsdp", "ep"), None)
    spec_in = P("ep", "fsdp", None)
    spec_out = P("ep", None, "fsdp")

    def per_device(x_tok, dy_tok, expert_ids, route_w, w_gate, w_up, w_down):
        tok_dev, top_k = expert_ids.shape
        capacity = capacity_of(tok_dev, top_k, w_gate.shape[0] * n_ep)
        part = lax.axis_index("fsdp")
        swap = [(0, 1), (1, 0)]
        weights = [lax.all_gather(w, "fsdp", axis=0) for w in (w_gate, w_up, w_down)]
        inputs = (x_tok, dy_tok, expert_ids.T, route_w.T, weights)

        def shard_halves(dws):
            out = []
            for dw, axis in zip(dws, (1, 1, 2)):
                size = dw.shape[axis] // 2
                keep = lax.dynamic_slice_in_dim(dw, part * size, size, axis)
                give = lax.dynamic_slice_in_dim(dw, (1 - part) * size, size, axis)
                out.append(keep + lax.ppermute(give, "fsdp", swap))
            return out

        quick = Plan(128, capacity, 4, capacity, n_ep)
        safe = Plan(2 * capacity, capacity, 4, capacity, n_ep)
        flags, q_t, dx_back, dr_t, dws = quick.forward(*inputs)
        bad = jnp.max(flags).reshape(1, 1)
        bad = jnp.maximum(bad, lax.ppermute(bad, "fsdp", swap))

        def fits():
            return (quick.combine(q_t, dx_back), dr_t.T, *shard_halves(dws))

        def general():
            _, q_all, dx_all, dr_all, dw_all = safe.forward(*inputs)
            return (safe.combine(q_all, dx_all), dr_all.T, *shard_halves(dw_all))

        return lax.cond(bad[0, 0] == 0.0, fits, general)

    return jax.shard_map(
        per_device, mesh=mesh,
        in_specs=(tok_spec, tok_spec, tok_spec, tok_spec, spec_in, spec_in, spec_out),
        out_specs=(tok_spec, tok_spec, spec_in, spec_in, spec_out),
        check_vma=False)
```

time: 1010 us -> 665 us (0.66)
  local copies, waits for them, and re-layouts: 253 us -> 10.1 us
  Pallas kernels: 0 us -> 194 us
  matrix products: 154 us -> 0 us
  blocking collectives: 173 us -> 34 us
  waiting for transfers between devices: 290 us -> 367 us
  other arithmetic: 64.8 us -> 8.97 us
  starting transfers between devices: 56.7 us -> 29.5 us
    gather x8 -> x0, local copies, waits for them, and re-layouts: 226 us -> none  [take_rows(): return jnp.take(rows, row_ids, axis=0, mode='fill', fill_value=0)]
    pallas_call x0 -> x5, Pallas kernels: none -> 194 us  [the longest x1 82.4 us: experts(): pl.pallas_call(functools.partial(expert_kernel, self.depth, span), out_sh...]
    dot_general x9 -> x0, matrix products: 154 us -> none  [the longest x1 35 us: expert_backward(): jnp.einsum('secd,edf->secf', x_rows, w_gate_full, preferred_element_type=...]
    all_to_all x1, blocking collectives: 173 us -> 34 us  [exchange(): return lax.all_to_all(v, 'ep', 0, 0, tiled=True)]
    all_to_all x4 -> x3, waiting for transfers between devices: 275 us -> 322 us  [exchange(): return lax.all_to_all(v, 'ep', 0, 0, tiled=True)]
    all_gather x3, waiting for transfers between devices: 12.7 us -> 41.8 us  [per_device(): lax.all_gather(w, 'fsdp', axis=0)]
    all_to_all x4 -> x3, starting transfers between devices: 56.5 us -> 28.8 us  [exchange(): return lax.all_to_all(v, 'ep', 0, 0, tiled=True)]
    scatter-add x1 -> x0, other arithmetic: 21.9 us -> none  [route_slots(): jax.ops.segment_sum(jnp.arange(1, n_pairs + 1, dtype=jnp.int32), dest_slo...]
  transfers between devices with their start and end apart: 10 -> 10, of which waited for: 3 -> 6; matrix products, arithmetic and copies ran while one was open for 31% -> 2% of each run, Pallas kernels for 0% -> 16%
where the time goes in v1:
time: 665 us; the launch traced here: 659 us
  waiting for transfers between devices  367 us (55%)
  Pallas kernels  194 us (29%)
  blocking collectives  34 us (5%)
  starting transfers between devices  29.5 us (4%)
  between operations  15.1 us (2%)
  local copies, waits for them, and re-layouts  10.1 us (2%)
  other arithmetic  8.97 us (1%)
    all_to_all x3, waiting for transfers between devices, exchange(): return lax.all_to_all(v, 'ep', 0, 0, tiled=True)  322 us
    pallas_call x1, Pallas kernels, experts(): pl.pallas_call(functools.partial(expert_kernel, self.depth, span), out_sh...  82.4 us
    pallas_call x1, Pallas kernels, combine(): pl.pallas_call(combine_kernel, out_shape=jax.ShapeDtypeStruct((tok_dev, d...  58.6 us
    pallas_call x1, Pallas kernels, forward(): pl.pallas_call(pack_kernel, out_shape=jax.ShapeDtypeStruct((n_ep * rows,...  43.7 us
    all_gather x3, waiting for transfers between devices, per_device(): lax.all_gather(w, 'fsdp', axis=0)  41.8 us
    all_to_all x1, blocking collectives, exchange(): return lax.all_to_all(v, 'ep', 0, 0, tiled=True)  34 us
    all_to_all x3, starting transfers between devices, exchange(): return lax.all_to_all(v, 'ep', 0, 0, tiled=True)  28.8 us
  transfers between devices with their start and end apart: 10, of which 6 were waited for; matrix products, arithmetic and copies ran while one was open for 2% of the time, Pallas kernels for 16%

profile of v1, /device:TPU:32, one launch (start us, length us, event | category | flops | bytes accessed | tf_op | source)
XLA Modules:
  0.0 658.9 jit_solution(5363307598560756763)
XLA Ops:
  7.2 4.2 route.3
  11.4 1.6 copy.27
  13.0 11.1 %all-to-all-start.4 = ((f32[64,1,384]{2,1,0:T(1,128)}), f32[64,1,384]{2,1,0:T(1,128)S(1)}, u32[]{:S(2)}, u32[]{:S(2)}) async-start(f32[64,1,384]{2,1,0:T(1,128)} %copy.27), calls=%async_computation.4 | async-start | bytes 196608 | tf_op jit(solution)/shard_map/all_to_all | solution.py:193
  24.1 43.7 %pack.3 = bf16[8192,1024]{1,0:T(8,128)(2,1)} custom-call(s32[2,2048]{1,0:T(2,128)S(1)} %get-tuple-element.108.q_ref, bf16[2048,512]{1,0:T(8,128)(2,1)} %x_ref.1, bf16[2048,512]{1,0:T(8,128)(2,1)} %dy_ref.1), custom_call_target="tpu_custom_call" | custom-call | tf_op jit(solution)/shard_map/pack/pallas_call | solution.py:210
  67.9 10.5 %all-to-all-start.5 = ((bf16[64,128,1024]{2,1,0:T(8,128)(2,1)}), bf16[64,128,1024]{2,1,0:T(8,128)(2,1)}, u32[]{:S(2)}, u32[]{:S(2)}) async-start(bf16[64,128,1024]{2,1,0:T(8,128)(2,1)} %bitcast.32), calls=%async_computation.5 | async-start | bytes 33554432 | tf_op jit(solution)/shard_map/all_to_all | solution.py:193
  78.5 0.7 all-gather.7.cloned.1.call-update
  79.2 0.7 all-gather.9.cloned.1.call-update
  79.9 0.7 all-gather.11.cloned.1.call-update
  80.6 0.6 copy.40
  81.3 12.6 %all-gather.7.cloned.1.call-done = bf16[4,256,512]{2,1,0:T(8,128)(2,1)} async-done(((bf16[2,256,512]{2,1,0:T(8,128)(2,1)}), bf16[4,256,512]{2,1,0:T(8,128)(2,1)}) %all-gather.7.cloned.1.call-update) | async-done | bytes 1048592 | tf_op jit(solution)/shard_map/all_gather | solution.py:273
  93.8 14.6 %all-gather.9.cloned.1.call-done = bf16[4,256,512]{2,1,0:T(8,128)(2,1)} async-done(((bf16[2,256,512]{2,1,0:T(8,128)(2,1)}), bf16[4,256,512]{2,1,0:T(8,128)(2,1)}) %all-gather.9.cloned.1.call-update) | async-done | bytes 1048592 | tf_op jit(solution)/shard_map/all_gather | solution.py:273
  108.5 14.6 %all-gather.11.cloned.1.call-done = bf16[4,512,256]{2,1,0:T(8,128)(2,1)} async-done(((bf16[2,512,256]{2,1,0:T(8,128)(2,1)}), bf16[4,512,256]{2,1,0:T(8,128)(2,1)}) %all-gather.11.cloned.1.call-update) | async-done | bytes 1048592 | tf_op jit(solution)/shard_map/all_gather | solution.py:273
  123.1 216.2 %all-to-all-done.5.xdy_ref = bf16[64,128,1024]{2,1,0:T(8,128)(2,1)} async-done(((bf16[64,128,1024]{2,1,0:T(8,128)(2,1)}), bf16[64,128,1024]{2,1,0:T(8,128)(2,1)}, u32[]{:S(2)}, u32[]{:S(2)}) %all-to-all-start.5) | async-done | bytes 16777248 | tf_op jit(solution)/shard_map/all_to_all | solution.py:193
  339.3 82.4 %experts.3 = (bf16[64,128,512]{2,1,0:T(8,128)(2,1)}, f32[64,256]{1,0:T(8,128)}, f32[2,512,512]{2,1,0:T(8,128)}, f32[2,512,512]{2,1,0:T(8,128)}, f32[2,512,512]{2,1,0:T(8,128)}) custom-call(bf16[64,128,1024]{2,1,0:T(8,128)(2,1)} %all-to-all-done.5.xdy_ref, f32[64,384]{1,0:T(8,128)} %bitcast.42, bf16[2,2,256,512]{3,2,1,0:T(8,128)(2,1)} %bitcast.33, ...), custom_call_target="tpu_custom_call" | custom-call | tf_op jit(solution)/shard_map/experts/pallas_call | solution.py:234
  421.7 0.9 copy.28
  422.6 34.0 %all_to_all.57 = f32[64,1,256]{2,1,0:T(1,128)S(1)} all-to-all(f32[64,1,256]{2,1,0:T(1,128)S(1)} %copy.28), channel_id=1, replica_groups=mesh['fsdp'=2,'ep'=64] {'ep'}, dimensions={0} | all-to-all | bytes 131072 | tf_op jit(solution)/shard_map/all_to_all | solution.py:193
  456.6 7.2 %all-to-all-start.6 = ((bf16[64,128,512]{2,1,0:T(8,128)(2,1)}), bf16[64,128,512]{2,1,0:T(8,128)(2,1)}, u32[]{:S(2)}, u32[]{:S(2)}) async-start(bf16[64,128,512]{2,1,0:T(8,128)(2,1)} %get-tuple-element.67), calls=%async_computation.6 | async-start | bytes 16777216 | tf_op jit(solution)/shard_map/all_to_all | solution.py:193
  463.9 1.4 slice_reduce_fusion
  465.3 1.1 collective-permute-done.6
  467.6 0.6 copy.41
  468.3 4.9 route_grad.3
  473.2 105.9 %all-to-all-done.6 = bf16[64,128,512]{2,1,0:T(8,128)(2,1)} async-done(((bf16[64,128,512]{2,1,0:T(8,128)(2,1)}), bf16[64,128,512]{2,1,0:T(8,128)(2,1)}, u32[]{:S(2)}, u32[]{:S(2)}) %all-to-all-start.6) | async-done | bytes 8388640 | tf_op jit(solution)/shard_map/all_to_all | solution.py:193
  579.1 1.3 copy.53
  580.4 71.9 %conditional.1 = (bf16[2048,512]{1,0:T(8,128)(2,1)}, f32[2048,2]{0,1:T(2,128)}, f32[2,256,512]{2,1,0:T(8,128)}, f32[2,256,512]{2,1,0:T(8,128)}, f32[2,512,256]{2,1,0:T(8,128)}) conditional(s32[]{:T(128)} %bitcast.13, (s32[2,2048]{1,0:T(2,128)S(1)}, f32[2,2048]{1,0:T(2,128)S(1)}, bf16[2048,512]{1,0:T(8,128)(2,1)S(1)}, bf16[2048,512]{1,0:T(8,128)(2,1)}, ...), branch_computations={%region_1.0_spmd, %region_2.0_spmd} | conditional | flops 786441 | bytes 168755712 | solution.py:298
  580.6 2.4 constant_dynamic-slice_fusion.3
  583.0 1.0 constant_dynamic-slice_fusion.4
  584.1 0.5 collective-permute-start.4
  584.8 1.3 copy.29
  586.1 58.6 %combine.3 = bf16[2048,512]{1,0:T(8,128)(2,1)} custom-call(s32[2048,2]{1,0:T(8,128)} %bitcast.39, bf16[8192,512]{1,0:T(8,128)(2,1)} %bitcast.7.back_ref), custom_call_target="tpu_custom_call" | custom-call | tf_op jit(solution)/shard_map/cond/branch_1_fun/combine/pallas_call | solution.py:252
  644.8 2.8 dynamic-slice_add_fusion.3
  647.6 2.4 dynamic-slice_add_fusion.4
  650.0 2.4 dynamic-slice_add_fusion.5
  (25 shorter events, 0.3 us)
Async XLA Ops:
  13.0 54.8 %all-to-all-start.4 = ((f32[64,1,384]{2,1,0:T(1,128)}), f32[64,1,384]{2,1,0:T(1,128)S(1)}, u32[]{:S(2)}, u32[]{:S(2)}) async-start(f32[64,1,384]{2,1,0:T(1,128)} %copy.27), calls=%async_computation.4 | async-start | bytes 196608 | tf_op jit(solution)/shard_map/all_to_all | solution.py:193
  67.9 271.4 %all-to-all-start.5 = ((bf16[64,128,1024]{2,1,0:T(8,128)(2,1)}), bf16[64,128,1024]{2,1,0:T(8,128)(2,1)}, u32[]{:S(2)}, u32[]{:S(2)}) async-start(bf16[64,128,1024]{2,1,0:T(8,128)(2,1)} %bitcast.32), calls=%async_computation.5 | async-start | bytes 33554432 | tf_op jit(solution)/shard_map/all_to_all | solution.py:193
  78.4 15.4 %all-gather.7.cloned.1.call-start = ((), (), s32[]{:S(2)}) async-start(), calls=%async_computation.8 | async-start | bytes 1572864 | tf_op jit(solution)/shard_map/all_gather | solution.py:273
  79.1 29.3 %all-gather.9.cloned.1.call-start = ((), (), s32[]{:S(2)}) async-start(), calls=%async_computation.9 | async-start | bytes 1572864 | tf_op jit(solution)/shard_map/all_gather | solution.py:273
  79.9 43.2 %all-gather.11.cloned.1.call-start = ((), (), s32[]{:S(2)}) async-start(), calls=%async_computation.10 | async-start | bytes 1572864 | tf_op jit(solution)/shard_map/all_gather | solution.py:273
  456.6 11.6 %copy-start.9 = (s32[2048,2]{0,1:T(2,128)S(1)}, s32[2048,2]{0,1:T(2,128)}, u32[]{:S(2)}) copy-start(s32[2048,2]{0,1:T(2,128)} %param.11) | copy-start | bytes 49156
  456.6 123.8 %copy-start = (bf16[2048,512]{1,0:T(8,128)(2,1)S(1)}, bf16[2048,512]{1,0:T(8,128)(2,1)}, u32[]{:S(2)}) copy-start(bf16[2048,512]{1,0:T(8,128)(2,1)} %x_ref.1) | copy-start | bytes 6291460
  456.6 123.8 %copy-start.1 = (bf16[4,256,512]{2,1,0:T(8,128)(2,1)S(1)}, bf16[4,256,512]{2,1,0:T(8,128)(2,1)}, u32[]{:S(2)}) copy-start(bf16[4,256,512]{2,1,0:T(8,128)(2,1)} %all-gather.7.cloned.1.call-done) | copy-start | bytes 3145732
  456.6 123.8 %copy-start.11 = (f32[2048,2]{0,1:T(2,128)S(1)}, f32[2048,2]{0,1:T(2,128)}, u32[]{:S(2)}) copy-start(f32[2048,2]{0,1:T(2,128)} %param.12) | copy-start | bytes 49156
  456.6 122.4 %all-to-all-start.6 = ((bf16[64,128,512]{2,1,0:T(8,128)(2,1)}), bf16[64,128,512]{2,1,0:T(8,128)(2,1)}, u32[]{:S(2)}, u32[]{:S(2)}) async-start(bf16[64,128,512]{2,1,0:T(8,128)(2,1)} %get-tuple-element.67), calls=%async_computation.6 | async-start | bytes 16777216 | tf_op jit(solution)/shard_map/all_to_all | solution.py:193
  465.2 1.1 collective-permute-start.6
  580.6 2.5 copy-start.5
  580.6 4.0 copy-start.4
  583.0 61.7 %collective-permute-start.5 = (f32[2,512,256]{2,1,0:T(8,128)}, f32[2,512,256]{2,1,0:T(8,128)}, u32[]{:S(2)}, u32[]{:S(2)}) collective-permute-start(f32[2,512,256]{2,1,0:T(8,128)} %constant_dynamic-slice_fusion.3), channel_id=1, source_target_pairs={{0,64},{64,0},{1,65},{65,1},{2,66},{66,2},{3,67},{67,3},{4,68},{68... | collective-permute-start | bytes 3145736 | tf_op jit(solution)/shard_map/cond/branch_1_fun/ppermute | solution.py:282
  584.1 63.5 %collective-permute-start.4 = (f32[2,256,512]{2,1,0:T(8,128)}, f32[2,256,512]{2,1,0:T(8,128)}, u32[]{:S(2)}, u32[]{:S(2)}) collective-permute-start(f32[2,256,512]{2,1,0:T(8,128)} %constant_dynamic-slice_fusion.4), channel_id=1, source_target_pairs={{0,64},{64,0},{1,65},{65,1},{2,66},{66,2},{3,67},{67,3},{4,68},{68... | collective-permute-start | bytes 3145736 | tf_op jit(solution)/shard_map/cond/branch_1_fun/ppermute | solution.py:282
  584.7 65.3 %collective-permute-start.3 = (f32[2,256,512]{2,1,0:T(8,128)S(1)}, f32[2,256,512]{2,1,0:T(8,128)}, u32[]{:S(2)}, u32[]{:S(2)}) collective-permute-start(f32[2,256,512]{2,1,0:T(8,128)S(1)} %constant_dynamic-slice_fusion.5), channel_id=1, source_target_pairs={{0,64},{64,0},{1,65},{65,1},{2,66},{66,2},{3,67},{67,3},{4,68},{68... | collective-permute-start | bytes 3145736 | tf_op jit(solution)/shard_map/cond/branch_1_fun/ppermute | solution.py:282
  644.8 2.8 copy-start.6
Sparse Core Ops, SparseCore 0:
  80.9 12.9 all-gather.6
  95.5 12.9 all-gather.8
  110.1 12.9 all-gather.10

commit v2 on v1

v2 whole, which is shorter than its diff:
```python
import functools

import jax
import jax.numpy as jnp
from jax import lax
from jax.experimental import pallas as pl
from jax.experimental.pallas import tpu as pltpu
from jax.sharding import PartitionSpec as P

CAP_FACTOR = 3
LANES = 128
FAR = 1 << 20
TAIL = 8
MESH = pl.DeviceIdType.MESH
f32, bf16, i32 = jnp.float32, jnp.bfloat16, jnp.int32


def capacity_of(tok_dev, top_k, experts):
    return max(8, ((CAP_FACTOR * tok_dev * top_k // experts + 7) // 8) * 8)


def iota(shape, dim):
    return lax.broadcasted_iota(i32, shape, dim)


def nn(a, b):
    return jnp.dot(a, b, preferred_element_type=f32)


def nt(a, b):
    return lax.dot_general(a, b, (((1,), (1,)), ((), ())), preferred_element_type=f32)


def tn(a, b):
    return lax.dot_general(a, b, (((0,), (0,)), ((), ())), preferred_element_type=f32)


def split3(v):
    hi = v.astype(bf16)
    rest = v - hi.astype(f32)
    mid = rest.astype(bf16)
    lo = (rest - mid.astype(f32)).astype(bf16)
    return hi, mid, lo


def add3(v, n):
    return v[:, :n] + v[:, n:2 * n] + v[:, 2 * n:]


def route_kernel(capacity, rows, depth, span, local_top, ids_ref, rw_ref, q_ref, pos_ref, msg_ref, top_ref, topw_ref):
    experts, chunk = LANES, 256
    tokens = ids_ref.shape[1]
    n_dest = msg_ref.shape[0]
    pitch = rows + TAIL
    before = (iota((chunk, chunk), 0) < iota((chunk, chunk), 1)).astype(bf16)
    expert_id = iota((experts, chunk), 0)
    slot_id = iota((span, chunk), 0)
    half_id = iota((n_dest, chunk), 0) * 2
    seen = jnp.zeros((experts, 1), f32)
    for c in range(tokens // chunk):
        at = slice(c * chunk, (c + 1) * chunk)
        hits = [expert_id == ids_ref[j:j + 1, at] for j in range(2)]
        member = jnp.where(hits[0] | hits[1], 1.0, 0.0)
        earlier = nn(member.astype(bf16), before) + seen
        seen = seen + jnp.sum(member, axis=1, keepdims=True)
        for j in range(2):
            pos_ref[j:j + 1, at] = jnp.sum(jnp.where(hits[j], earlier, 0.0), axis=0, keepdims=True).astype(i32)
    expert_col = iota((experts, 1), 0).astype(f32)
    kept = jnp.minimum(seen, float(capacity))
    if local_top:
        most = jnp.max(seen, axis=0, keepdims=True)
        top = jnp.min(jnp.where(seen == most, expert_col, float(experts)), axis=0, keepdims=True)
        kept = jnp.where(expert_col == top, 0.0, kept)
    else:
        top = jnp.full((1, 1), -1.0, f32)
    top_i = top.astype(i32)
    gates = [jnp.zeros((3 * n_dest, span), f32) for _ in range(2)]
    top_gates = jnp.zeros((24, LANES), f32)
    for c in range(tokens // chunk):
        at = slice(c * chunk, (c + 1) * chunk)
        for j in range(2):
            ids = ids_ref[j:j + 1, at]
            place = pos_ref[j:j + 1, at]
            weight = rw_ref[j:j + 1, at]
            keep = place < capacity
            slot = jnp.where(ids % 2 == 0, place, rows - 1 - place)
            q = (ids // 2) * pitch + slot
            if local_top:
                is_top = ids == top_i
                q = jnp.where(is_top, n_dest * pitch + place, q)
                slot = jnp.where(is_top, FAR, slot)
                top_hot = jnp.where((iota((LANES, chunk), 0) == place) & keep & is_top, 1.0, 0.0).astype(bf16)
                top_parts = [jnp.broadcast_to(p, (8, chunk)) for p in split3(weight)]
                top_gates = top_gates + nt(jnp.concatenate(top_parts, axis=0), top_hot)
            q_ref[j:j + 1, at] = jnp.where(keep, q, FAR)
            slot_hot = jnp.where(slot_id == jnp.where(keep, slot, FAR), 1.0, 0.0).astype(bf16)
            for par in range(2):
                mine = jnp.where(half_id + par == ids, weight, 0.0)
                gates[par] = gates[par] + nt(jnp.concatenate(split3(mine), axis=0), slot_hot)
    kept_wide = jnp.broadcast_to(kept, (experts, LANES)).astype(bf16)
    owner = (iota((n_dest, experts), 1) // 2 == iota((n_dest, experts), 0)).astype(bf16)
    over = jnp.max(jnp.where(nn(owner, kept_wide) > float(rows), 1.0, 0.0), axis=0, keepdims=True)
    over = jnp.maximum(over, jnp.max(jnp.where(kept > float(depth), 1.0, 0.0), axis=0, keepdims=True))
    for par in range(2):
        g = gates[par]
        msg_ref[:, par * span:(par + 1) * span] = g[:n_dest] + g[n_dest:2 * n_dest] + g[2 * n_dest:]
    note = jnp.where(iota((1, LANES), 1) == 1, top, over)
    msg_ref[:, 2 * span:] = jnp.broadcast_to(note, (n_dest, LANES))
    top_ref[...] = jnp.broadcast_to(top_i, (8, LANES))
    topw_ref[...] = top_gates[:8] + top_gates[8:16] + top_gates[16:]


def pack_kernel(group, rows, first, q_ref, x_ref, dy_ref, out_ref):
    d = x_ref.shape[1]
    count, tokens = group * rows, q_ref.shape[1]
    row = iota((count, tokens), 0)
    slot = row + (row // rows + pl.program_id(0) * group) * TAIL + pl.program_id(0) * count + first
    pick = jnp.where((q_ref[0:1, :] == slot) | (q_ref[1:2, :] == slot), 1.0, 0.0).astype(bf16)
    out_ref[:, :d] = nn(pick, x_ref[...]).astype(bf16)
    out_ref[:, d:] = nn(pick, dy_ref[...]).astype(bf16)


def swiglu_rows(x, dy, weight, w1, w3, w2):
    h1 = nn(x, w1)
    h3 = nn(x, w3)
    s = jax.nn.sigmoid(h1)
    hidden = (h1 * s * h3).astype(bf16)
    dr = jnp.sum(dy * nn(hidden, w2), axis=1, keepdims=True)
    g = (weight * dy).astype(bf16)
    da = nt(g, w2)
    dh1 = (da * h3 * s * (1.0 + h1 * (1.0 - s))).astype(bf16)
    dh3 = (da * h1 * s).astype(bf16)
    return hidden, g, dh1, dh3, nt(dh1, w1) + nt(dh3, w3), dr


def expert_kernel(depth, span, xdy_ref, rec_ref, wg_ref, wu_ref, wd_ref,
                  dx_ref, dwg_ref, dwu_ref, dwd_ref, w2_ref):
    step = pl.program_id(0)
    group, rows, width = xdy_ref.shape
    n_src = rec_ref.shape[0]
    d = width // 2
    half = wg_ref.shape[2]
    m = group * depth

    @pl.when(step == 0)
    def _():
        for ref in (dwg_ref, dwu_ref, dwd_ref):
            ref[...] = jnp.zeros_like(ref)
        for k in range(2):
            for i in range(2):
                w2_ref[k, :, i * half:(i + 1) * half] = wd_ref[i, k]

    local = iota((m, n_src), 0) // depth
    src_hot = jnp.where(local + step * group == iota((m, n_src), 1), 1.0, 0.0).astype(bf16)
    row_hot = jnp.where(iota((m, LANES), 0) // depth == iota((m, LANES), 1), 1.0, 0.0).astype(bf16)
    within = iota((m, span), 0) % depth
    outs, dr_slots = [], jnp.zeros((LANES, span), f32)
    for k in range(2):
        first = 0 if k == 0 else rows - depth
        slot_hot = iota((m, span), 1) == within + first
        gate_parts = jnp.concatenate(split3(rec_ref[:, k * span:(k + 1) * span]), axis=1)
        weight = jnp.sum(jnp.where(slot_hot, add3(nn(src_hot, gate_parts), span), 0.0), axis=1, keepdims=True)
        x = xdy_ref[:, first:first + depth, :d].reshape(m, d)
        dy = xdy_ref[:, first:first + depth, d:].reshape(m, d).astype(f32)
        w1 = wg_ref[:, k].reshape(d, wg_ref.shape[3])
        w3 = wu_ref[:, k].reshape(d, wu_ref.shape[3])
        hidden, g, dh1, dh3, dx, dr = swiglu_rows(x, dy, weight, w1, w3, w2_ref[k])
        outs.append(dx.reshape(group, depth, d))
        dwg_ref[k] += tn(x, dh1)
        dwu_ref[k] += tn(x, dh3)
        dwd_ref[k] += tn(hidden, g)
        parts = jnp.concatenate(split3(jnp.where(slot_hot & (weight > 0.0), dr, 0.0)), axis=1)
        dr_slots = dr_slots + add3(tn(row_hot, parts), span)
    low = rows - depth
    dx_ref[:, :low] = outs[0][:, :low].astype(bf16)
    if depth > low:
        dx_ref[:, low:depth] = (outs[0][:, low:] + outs[1][:, :depth - low]).astype(bf16)
    dx_ref[:, depth:rows] = outs[1][:, depth - low:].astype(bf16)
    parts = split3(dr_slots)
    for i in range(group):
        dx_ref[i, rows:, :] = jnp.zeros((TAIL, d), bf16)
        for n in range(3):
            dx_ref[i, rows + n:rows + n + 1, :span] = parts[n][i:i + 1, :]


def top_kernel(wm_ref, rows_ref, gate_ref, dx_ref, dr_ref, grad_ref,
               wbuf, wr0, wr1, wr2, wfull, gfull, gbuf, gpeer, gr0, gr1, gr2, ssem, rsem):
    me, part = lax.axis_index("ep"), lax.axis_index("fsdp")
    strides = (1, 4, 16)
    coord = [me % 4, (me // 4) % 4, me // 16]
    n_mat, total = wbuf.shape[0], wbuf.shape[1]
    levels = len(strides)

    def peer(axis, delta):
        return me + ((coord[axis] + delta) % 4 - coord[axis]) * strides[axis]

    barrier = pltpu.get_barrier_semaphore()
    for axis in range(3):
        for delta in (1, 2, 3):
            pl.semaphore_signal(barrier, inc=1, device_id={"ep": peer(axis, delta)}, device_id_type=MESH)
    pl.semaphore_signal(barrier, inc=1, device_id={"fsdp": 1 - part}, device_id_type=MESH)
    pl.semaphore_wait(barrier, 10)

    def at(base, size):
        return pl.ds(pl.multiple_of(base, 16), size)

    def all_reduce(which, buf, recvs, put):
        base = [0] * n_mat
        sizes, starts = [], []
        for level in range(levels):
            size = total // 4 ** (level + 1)
            copies = []
            for c in range(n_mat):
                axis = (c + level) % 3
                for delta in (1, 2, 3):
                    to = (coord[axis] + delta) % 4
                    copies.append(pltpu.make_async_remote_copy(
                        src_ref=buf.at[c, at(base[c] + to * size, size)],
                        dst_ref=recvs[level].at[c, 3 - delta],
                        send_sem=ssem.at[which, 0, level, c, delta - 1], recv_sem=rsem.at[which, 0, level, c, 3 - delta],
                        device_id={"ep": peer(axis, delta)}, device_id_type=MESH))
            for copy in copies:
                copy.start()
            for copy in copies:
                copy.wait()
            starts.append(list(base))
            sizes.append(size)
            for c in range(n_mat):
                base[c] = base[c] + coord[(c + level) % 3] * size
                mine = at(base[c], size)
                got = [recvs[level][c, i].astype(f32) for i in range(3)]
                buf[c, mine] = (buf[c, mine].astype(f32) + got[0] + got[1] + got[2]).astype(buf.dtype)
        for c in range(n_mat):
            put(c, at(base[c], sizes[-1]))[...] = buf[c, at(base[c], sizes[-1])]
        for level in reversed(range(levels)):
            copies = []
            for c in range(n_mat):
                axis = (c + level) % 3
                mine = at(starts[level][c] + coord[axis] * sizes[level], sizes[level])
                for delta in (1, 2, 3):
                    copies.append(pltpu.make_async_remote_copy(
                        src_ref=put(c, mine), dst_ref=put(c, mine),
                        send_sem=ssem.at[which, 1, level, c, delta - 1], recv_sem=rsem.at[which, 1, level, c, 3 - delta],
                        device_id={"ep": peer(axis, delta)}, device_id_type=MESH))
            for copy in copies:
                copy.start()
            for copy in copies:
                copy.wait()

    wbuf[...] = wm_ref[...]
    all_reduce(0, wbuf, (wr0, wr1, wr2), lambda c, s: wfull.at[part, c, s])
    swap = pltpu.make_async_remote_copy(
        src_ref=wfull.at[part], dst_ref=wfull.at[part], send_sem=ssem.at[0, 2, 0, 0, 0], recv_sem=rsem.at[0, 2, 0, 0, 0],
        device_id={"fsdp": 1 - part}, device_id_type=MESH)
    swap.start()
    swap.wait()

    d = dx_ref.shape[1]
    half = d // 2
    wide = d // LANES
    mats = []
    for i in range(2):
        mats.append(jnp.concatenate([jnp.concatenate(
            [wfull[f, i, b * half:(b + 1) * half, :] for b in range(wide)], axis=1) for f in range(2)], axis=0))
    w2 = jnp.concatenate([wfull[f, 2, b * d:(b + 1) * d, :] for f in range(2) for b in range(wide // 2)], axis=1)
    n = rows_ref.shape[0]
    x = rows_ref[:, :d]
    dy = rows_ref[:, d:].astype(f32)
    eye = iota((n, n), 0) == iota((n, n), 1)
    weight = jnp.sum(jnp.where(eye, gate_ref[0:1, :], 0.0), axis=1, keepdims=True)
    hidden, g, dh1, dh3, dx, dr = swiglu_rows(x, dy, weight, mats[0], mats[1], w2)
    dx_ref[...] = dx.astype(bf16)
    dr_ref[...] = jnp.broadcast_to(dr, dr_ref.shape)
    for i, dh in enumerate((dh1, dh3)):
        dw = tn(x, dh)
        for f in range(2):
            for b in range(wide):
                gfull[f, i, b * half:(b + 1) * half, :] = dw[f * half:(f + 1) * half, b * LANES:(b + 1) * LANES]
    dw = tn(hidden, g)
    for f in range(2):
        for b in range(wide // 2):
            lane = f * half + b * LANES
            gfull[f, 2, b * d:(b + 1) * d, :] = dw[:, lane:lane + LANES]

    swap = pltpu.make_async_remote_copy(
        src_ref=gfull.at[1 - part], dst_ref=gpeer, send_sem=ssem.at[1, 2, 0, 0, 0], recv_sem=rsem.at[1, 2, 0, 0, 0],
        device_id={"fsdp": 1 - part}, device_id_type=MESH)
    swap.start()
    swap.wait()
    gbuf[...] = gfull[part] + gpeer[...]
    all_reduce(1, gbuf, (gr0, gr1, gr2), lambda c, s: grad_ref.at[c, s])


def dr_kernel(rows, span, ids_ref, q_ref, pos_ref, back_ref, top_dr_ref, out_ref):
    n_src = back_ref.shape[0]
    tokens = ids_ref.shape[1]
    pitch = rows + TAIL
    chunk = 512
    tables = [back_ref[:, n, :span].T for n in range(3)]
    for c in range(tokens // chunk):
        at = slice(c * chunk, (c + 1) * chunk)
        for j in range(2):
            block = ids_ref[j:j + 1, at] // 2
            q = q_ref[j:j + 1, at]
            owner = jnp.where(iota((n_src, chunk), 0) == block, 1.0, 0.0).astype(bf16)
            column = nn(tables[0], owner) + nn(tables[1], owner) + nn(tables[2], owner)
            far = q >= n_src * pitch
            want = jnp.where(far, FAR, q - block * pitch)
            picked = jnp.sum(jnp.where(iota((span, chunk), 0) == want, column, 0.0), axis=0, keepdims=True)
            if top_dr_ref is not None:
                want = jnp.where(far, q - n_src * pitch, FAR)
                picked = picked + jnp.sum(
                    jnp.where(iota((LANES, chunk), 0) == want, top_dr_ref[:, 0:1], 0.0), axis=0, keepdims=True)
            out_ref[j:j + 1, at] = picked


def combine_kernel(q_ref, back_ref, *rest):
    top_ref, out_ref = rest if len(rest) == 2 else (None, rest[0])
    rows, slots = q_ref.shape[0], back_ref.shape[0]
    q0, q1 = q_ref[:, 0:1], q_ref[:, 1:2]
    acc = jnp.zeros(out_ref.shape, f32)
    for at in range(0, slots, 512):
        depth = min(512, slots - at)
        column = iota((rows, depth), 1) + at
        pick = jnp.where((q0 == column) | (q1 == column), 1.0, 0.0).astype(bf16)
        acc = acc + nn(pick, back_ref[at:at + depth, :])
    if top_ref is not None:
        column = iota((rows, LANES), 1) + slots
        pick = jnp.where((q0 == column) | (q1 == column), 1.0, 0.0).astype(bf16)
        acc = acc + nn(pick, top_ref[...])
    out_ref[...] = acc.astype(bf16)


def vmem():
    return pl.BlockSpec(memory_space=pltpu.VMEM)


def whole(shape):
    return pl.BlockSpec(shape, lambda i: (0,) * len(shape))


PARAMS = pltpu.CompilerParams(vmem_limit_bytes=60 * 1024 * 1024)


def exchange(v):
    return lax.all_to_all(v, "ep", 0, 0, tiled=True)


def top_serve(w_mine, rows, gate, d):
    n_mat, total = 3, w_mine.shape[1]
    scratch = []
    for dtype in (bf16, f32):
        recvs = [pltpu.VMEM((n_mat, 3, total // 4 ** (i + 1), LANES), dtype) for i in range(3)]
        if dtype == bf16:
            scratch += [pltpu.VMEM((n_mat, total, LANES), dtype), *recvs, pltpu.VMEM((2, n_mat, total, LANES), dtype)]
        else:
            scratch += [pltpu.VMEM((2, n_mat, total, LANES), dtype), pltpu.VMEM((n_mat, total, LANES), dtype),
                        pltpu.VMEM((n_mat, total, LANES), dtype), *recvs]
    scratch += [pltpu.SemaphoreType.DMA((2, 3, 3, n_mat, 3)), pltpu.SemaphoreType.DMA((2, 3, 3, n_mat, 3))]
    return pl.pallas_call(
        top_kernel,
        out_shape=(jax.ShapeDtypeStruct((rows.shape[0], d), bf16),
                   jax.ShapeDtypeStruct((rows.shape[0], LANES), f32),
                   jax.ShapeDtypeStruct((n_mat, total, LANES), f32)),
        in_specs=[vmem()] * 3, out_specs=(vmem(),) * 3, scratch_shapes=scratch,
        compiler_params=pltpu.CompilerParams(
            vmem_limit_bytes=48 * 1024 * 1024, collective_id=0, has_side_effects=True),
        cost_estimate=pl.CostEstimate(flops=40_000_000_000, bytes_accessed=8_000_000, transcendentals=0),
        name="top",
    )(w_mine, rows, gate)


class Plan:
    def __init__(self, rows, depth, pack_group, group, capacity, n_ep, local_top):
        self.rows, self.depth, self.pack_group, self.group = rows, depth, pack_group, group
        self.capacity, self.n_ep, self.local_top = capacity, n_ep, local_top
        self.span = -(-rows // LANES) * LANES

    def pack(self, q_t, x_tok, dy_tok, group, rows, steps, first):
        tok_dev, d = x_tok.shape
        return pl.pallas_call(
            functools.partial(pack_kernel, group, rows, first),
            out_shape=jax.ShapeDtypeStruct((steps * group * rows, 2 * d), bf16),
            grid=(steps,),
            in_specs=[whole((2, tok_dev)), whole((tok_dev, d)), whole((tok_dev, d))],
            out_specs=pl.BlockSpec((group * rows, 2 * d), lambda i: (i, 0)),
            compiler_params=PARAMS, name="pack",
        )(q_t, x_tok, dy_tok)

    def forward(self, me, x_tok, dy_tok, ids_t, rw_t, weights, own):
        tok_dev, d = x_tok.shape
        n_ep, rows, span = self.n_ep, self.rows, self.span
        q_t, pos_t, msg, top, top_gate = pl.pallas_call(
            functools.partial(route_kernel, self.capacity, rows, self.depth, span, self.local_top),
            out_shape=(jax.ShapeDtypeStruct((2, tok_dev), i32), jax.ShapeDtypeStruct((2, tok_dev), i32),
                       jax.ShapeDtypeStruct((n_ep, 2 * span + LANES), f32),
                       jax.ShapeDtypeStruct((8, LANES), i32), jax.ShapeDtypeStruct((8, LANES), f32)),
            in_specs=[vmem(), vmem()], out_specs=(vmem(),) * 5, compiler_params=PARAMS, name="route",
        )(ids_t, rw_t)
        rec = exchange(msg)
        packed = self.pack(q_t, x_tok, dy_tok, self.pack_group, rows, n_ep // self.pack_group, 0)
        top_out = None
        if self.local_top:
            top_rows = self.pack(q_t, x_tok, dy_tok, 1, LANES, 1, n_ep * (rows + TAIL))
            top_id = top[0, 0]
            mine = top_id // 2 == me
            flat = []
            for w in own:
                one = lax.dynamic_index_in_dim(w, top_id % 2, 0, keepdims=False)
                one = jnp.where(mine, one, jnp.zeros_like(one))
                flat.append(one.reshape(one.shape[0], -1, LANES).transpose(1, 0, 2).reshape(-1, LANES))
            packed, top_rows = lax.optimization_barrier((packed, top_rows))
            top_out = (top_id, *top_serve(jnp.stack(flat), top_rows, top_gate, d))
        xdy = exchange(packed.reshape(n_ep, rows, 2 * d))
        dx, dwg, dwu, dwd = self.experts(xdy, rec, weights)
        back = exchange(dx)
        return rec[:, 2 * span:], q_t, back, top_out, (dwg, dwu, dwd)

    def experts(self, xdy, rec, weights):
        n_ep, rows, width = xdy.shape
        d, group, span = width // 2, self.group, self.span
        wg, wu, wd = weights
        ff = wg.shape[3]
        return pl.pallas_call(
            functools.partial(expert_kernel, self.depth, span),
            out_shape=(jax.ShapeDtypeStruct((n_ep, rows + TAIL, d), bf16),
                       jax.ShapeDtypeStruct((2, d, ff), f32),
                       jax.ShapeDtypeStruct((2, d, ff), f32),
                       jax.ShapeDtypeStruct((2, ff, d), f32)),
            grid=(n_ep // group,),
            in_specs=[pl.BlockSpec((group, rows, width), lambda i: (i, 0, 0)),
                      whole(rec.shape), whole(wg.shape), whole(wu.shape), whole(wd.shape)],
            out_specs=(pl.BlockSpec((group, rows + TAIL, d), lambda i: (i, 0, 0)),
                       whole((2, d, ff)), whole((2, d, ff)), whole((2, ff, d))),
            scratch_shapes=[pltpu.VMEM((2, ff, d), bf16)],
            compiler_params=PARAMS, name="experts",
        )(xdy, rec, wg, wu, wd)

    def finish(self, ids_t, q_t, back, top_out):
        tok_dev, (n_ep, pitch, d), tile = q_t.shape[1], back.shape, 256
        tail = back[:, self.rows:, :]
        dr_args = [ids_t, q_t, q_t, tail] + ([top_out[2]] if top_out else [])
        kernel = functools.partial(dr_kernel, self.rows, self.span)
        if not top_out:
            inner = kernel
            kernel = lambda a, b, c, e, out: inner(a, b, c, e, None, out)
        dr_t = pl.pallas_call(
            kernel, out_shape=jax.ShapeDtypeStruct((2, tok_dev), f32),
            in_specs=[vmem()] * len(dr_args), out_specs=vmem(), compiler_params=PARAMS, name="route_grad",
        )(*dr_args)
        slots = n_ep * pitch
        args = [q_t.T, back.reshape(slots, d)] + ([top_out[1]] if top_out else [])
        grad_x = pl.pallas_call(
            combine_kernel,
            out_shape=jax.ShapeDtypeStruct((tok_dev, d), bf16),
            grid=(tok_dev // tile,),
            in_specs=[pl.BlockSpec((tile, 2), lambda i: (i, 0))] + [whole(v.shape) for v in args[1:]],
            out_specs=pl.BlockSpec((tile, d), lambda i: (i, 0)),
            compiler_params=PARAMS, name="combine",
        )(*args)
        return grad_x, dr_t.T


def solution(mesh):
    n_ep = mesh.shape["ep"]
    tok_spec = P(("fsdp", "ep"), None)
    spec_in = P("ep", "fsdp", None)
    spec_out = P("ep", None, "fsdp")

    def per_device(x_tok, dy_tok, expert_ids, route_w, w_gate, w_up, w_down):
        tok_dev, top_k = expert_ids.shape
        capacity = capacity_of(tok_dev, top_k, w_gate.shape[0] * n_ep)
        me, part = lax.axis_index("ep").astype(i32), lax.axis_index("fsdp")
        swap = [(0, 1), (1, 0)]
        own = (w_gate, w_up, w_down)
        weights = [lax.all_gather(w, "fsdp", axis=0) for w in own]
        ids_t = expert_ids.T
        inputs = (me, x_tok, dy_tok, ids_t, route_w.T, weights, own)

        def shard_halves(dws):
            out = []
            for dw, axis in zip(dws, (1, 1, 2)):
                size = dw.shape[axis] // 2
                keep = lax.dynamic_slice_in_dim(dw, part * size, size, axis)
                give = lax.dynamic_slice_in_dim(dw, (1 - part) * size, size, axis)
                out.append(keep + lax.ppermute(give, "fsdp", swap))
            return out

        quick = Plan(72, 48, 4, 8, capacity, n_ep, True)
        safe = Plan(2 * capacity, capacity, 2, 4, capacity, n_ep, False)
        notes, q_t, back, top_out, dws = quick.forward(*inputs)
        halves = shard_halves(dws)
        top_id = top_out[0]
        agree = jnp.all(notes[:, 1] == top_id.astype(f32)) & jnp.all(notes[:, 0] == 0.0)
        note = jnp.where(agree, top_id.astype(f32), -1.0).reshape(1, 1)
        other = lax.ppermute(note, "fsdp", swap)
        good = agree & (other == note)[0, 0]

        def fits():
            grads = []
            for i, half in enumerate(halves):
                rows = half.shape[1]
                extra = top_out[3][i].reshape(-1, rows, LANES).transpose(1, 0, 2).reshape(1, *half.shape[1:])
                pick = (jnp.arange(2) + 2 * me == top_id)[:, None, None]
                grads.append(half + jnp.where(pick, extra, 0.0))
            return (*quick.finish(ids_t, q_t, back, top_out), *grads)

        def general():
            _, q_all, back_all, _, dw_all = safe.forward(*inputs)
            return (*safe.finish(ids_t, q_all, back_all, None), *shard_halves(dw_all))

        return lax.cond(good, fits, general)

    return jax.shard_map(
        per_device, mesh=mesh,
        in_specs=(tok_spec, tok_spec, tok_spec, tok_spec, spec_in, spec_in, spec_out),
        out_specs=(tok_spec, tok_spec, spec_in, spec_in, spec_out),
        check_vma=False)
```

time: 665 us -> 440 us (0.66)
  waiting for transfers between devices: 367 us -> 141 us
  blocking collectives: 34 us -> 0 us
  Pallas kernels: 194 us -> 222 us
    all_to_all x3, waiting for transfers between devices: 322 us -> 97.1 us  [exchange(): return lax.all_to_all(v, 'ep', 0, 0, tiled=True)]
    pallas_call x4 -> x6, Pallas kernels: 112 us -> 177 us  [the longest x1 125 us: top_serve(): pl.pallas_call(top_kernel, out_shape=(jax.ShapeDtypeStruct((rows.shape[0]...]
    pallas_call x1, Pallas kernels: 82.4 us -> 44.4 us  [experts(): pl.pallas_call(functools.partial(expert_kernel, self.depth, span), out_sh...]
    all_to_all x1 -> x0, blocking collectives: 34 us -> none  [exchange(): return lax.all_to_all(v, 'ep', 0, 0, tiled=True)]
  transfers between devices with their start and end apart: 10 -> 10, of which waited for: 6 -> 5; matrix products, arithmetic and copies ran while one was open for 2% -> 2% of each run, Pallas kernels for 16% -> 35%
where the time goes in v2:
time: 440 us; the launch traced here: 437 us
  Pallas kernels  222 us (50%)
  waiting for transfers between devices  141 us (32%)
  starting transfers between devices  29 us (7%)
  between operations  19 us (4%)
  local copies, waits for them, and re-layouts  16.6 us (4%)
  other arithmetic  8.82 us (2%)
    pallas_call x1, Pallas kernels, top_serve(): pl.pallas_call(top_kernel, out_shape=(jax.ShapeDtypeStruct((rows.shape[0]...  125 us
    all_to_all x3, waiting for transfers between devices, exchange(): return lax.all_to_all(v, 'ep', 0, 0, tiled=True)  97.1 us
    pallas_call x1, Pallas kernels, experts(): pl.pallas_call(functools.partial(expert_kernel, self.depth, span), out_sh...  44.4 us
    all_gather x3, waiting for transfers between devices, per_device(): weights = [lax.all_gather(w, 'fsdp', axis=0) for w in own]  41.8 us
    pallas_call x2, Pallas kernels, pack(): pl.pallas_call(functools.partial(pack_kernel, group, rows, first), out_sh...  28.8 us
    all_to_all x3, starting transfers between devices, exchange(): return lax.all_to_all(v, 'ep', 0, 0, tiled=True)  27.5 us
    pallas_call x1, Pallas kernels, finish(): pl.pallas_call(combine_kernel, out_shape=jax.ShapeDtypeStruct((tok_dev, d...  16.6 us
  transfers between devices with their start and end apart: 10, of which 5 were waited for; matrix products, arithmetic and copies ran while one was open for 2% of the time, Pallas kernels for 35%

profile of v2, /device:TPU:32, one launch (start us, length us, event | category | flops | bytes accessed | tf_op | source)
XLA Modules:
  0.0 436.7 jit_solution(402467669475111506)
XLA Ops:
  7.2 3.6 route.3
  10.8 1.6 copy.36
  12.4 11.1 %all-to-all-start.3 = ((f32[64,1,384]{2,1,0:T(1,128)}), f32[64,1,384]{2,1,0:T(1,128)S(1)}, u32[]{:S(2)}, u32[]{:S(2)}) async-start(f32[64,1,384]{2,1,0:T(1,128)} %copy.36), calls=%async_computation.3 | async-start | bytes 196608 | tf_op jit(solution)/shard_map/all_to_all | solution.py:346
  23.5 25.8 %pack.4 = bf16[4608,1024]{1,0:T(8,128)(2,1)} custom-call(s32[2,2048]{1,0:T(2,128)S(1)} %get-tuple-element.115.q_ref, bf16[2048,512]{1,0:T(8,128)(2,1)} %x_ref.3, bf16[2048,512]{1,0:T(8,128)(2,1)} %dy_ref.3), custom_call_target="tpu_custom_call" | custom-call | tf_op jit(solution)/shard_map/pack/pallas_call | solution.py:381
  49.4 3.0 pack.5.rows_ref
  52.4 10.5 %all-to-all-start.4 = ((bf16[64,72,1024]{2,1,0:T(8,128)(2,1)}), bf16[64,72,1024]{2,1,0:T(8,128)(2,1)}, u32[]{:S(2)}, u32[]{:S(2)}) async-start(bf16[64,72,1024]{2,1,0:T(8,128)(2,1)} %bitcast.53), calls=%async_computation.4 | async-start | bytes 18874368 | tf_op jit(solution)/shard_map/all_to_all | solution.py:346
  63.7 0.7 all-gather.9.cloned.1.call-update
  65.8 12.6 %all-gather.7.cloned.1.call-done = bf16[4,256,512]{2,1,0:T(8,128)(2,1)} async-done(((bf16[2,256,512]{2,1,0:T(8,128)(2,1)}), bf16[4,256,512]{2,1,0:T(8,128)(2,1)}) %all-gather.7.cloned.1.call-update) | async-done | bytes 1048592 | tf_op jit(solution)/shard_map/all_gather | solution.py:476
  78.3 14.6 %all-gather.9.cloned.1.call-done = bf16[4,256,512]{2,1,0:T(8,128)(2,1)} async-done(((bf16[2,256,512]{2,1,0:T(8,128)(2,1)}), bf16[4,256,512]{2,1,0:T(8,128)(2,1)}) %all-gather.9.cloned.1.call-update) | async-done | bytes 1048592 | tf_op jit(solution)/shard_map/all_gather | solution.py:476
  92.9 14.6 %all-gather.11.cloned.1.call-done = bf16[4,512,256]{2,1,0:T(8,128)(2,1)} async-done(((bf16[2,512,256]{2,1,0:T(8,128)(2,1)}), bf16[4,512,256]{2,1,0:T(8,128)(2,1)}) %all-gather.11.cloned.1.call-update) | async-done | bytes 1048592 | tf_op jit(solution)/shard_map/all_gather | solution.py:476
  107.6 97.1 %all-to-all-done.4.xdy_ref = bf16[64,72,1024]{2,1,0:T(8,128)(2,1)} async-done(((bf16[64,72,1024]{2,1,0:T(8,128)(2,1)}), bf16[64,72,1024]{2,1,0:T(8,128)(2,1)}, u32[]{:S(2)}, u32[]{:S(2)}) %all-to-all-start.4) | async-done | bytes 9437216 | tf_op jit(solution)/shard_map/all_to_all | solution.py:346
  204.7 44.4 %experts.3 = (bf16[64,80,512]{2,1,0:T(8,128)(2,1)}, f32[2,512,512]{2,1,0:T(8,128)}, f32[2,512,512]{2,1,0:T(8,128)}, f32[2,512,512]{2,1,0:T(8,128)}) custom-call(bf16[64,72,1024]{2,1,0:T(8,128)(2,1)} %all-to-all-done.4.xdy_ref, f32[64,384]{1,0:T(8,128)} %bitcast.69, bf16[2,2,256,512]{3,2,1,0:T(8,128)(2,1)} %bitcast.54, bf16[2,2,256,512]{3,2,1,0:T(8,128)(2,1)} %bitcast.56, ...), custom_call_target="tpu_custom_call" | custom-call | tf_op jit(solution)/shard_map/experts/pallas_call | solution.py:424
  249.1 5.9 %all-to-all-start.5 = ((bf16[64,80,512]{2,1,0:T(8,128)(2,1)}), bf16[64,80,512]{2,1,0:T(8,128)(2,1)}, u32[]{:S(2)}, u32[]{:S(2)}) async-start(bf16[64,80,512]{2,1,0:T(8,128)(2,1)} %get-tuple-element.117), calls=%async_computation.5 | async-start | bytes 10485760 | tf_op jit(solution)/shard_map/all_to_all | solution.py:346
  255.0 1.2 slice.28
  258.8 0.7 dynamic-slice_select_fusion.2
  259.5 1.1 select_n.96
  260.6 0.7 copy.37
  262.4 2.4 constant_dynamic-slice_fusion.5
  264.9 1.0 constant_dynamic-slice_fusion.4
  266.4 1.1 constant_dynamic-slice_fusion.3
  267.5 125.3 %top.1 = (bf16[128,512]{1,0:T(8,128)(2,1)S(1)}, f32[128,128]{1,0:T(8,128)S(1)}, f32[3,1024,128]{2,1,0:T(8,128)}) custom-call(bf16[3,1024,128]{2,1,0:T(8,128)(2,1)S(1)} %pad_maximum_fusion.wm_ref, bf16[128,1024]{1,0:T(8,128)(2,1)S(1)} %copy-done, f32[8,128]{1,0:T(8,128)S(1)} %copy-done.1), custom_call_target="tpu_custom_call" | custom-call | flops 40000000000 | bytes 8000000 | tf_op jit(solution)/shard_map/top/pallas_call | solution.py:360
  393.5 0.7 fusion.1
  395.5 0.9 collective-permute-start.3
  397.3 32.9 %conditional.1 = (bf16[2048,512]{1,0:T(8,128)(2,1)}, f32[2048,2]{0,1:T(2,128)}, f32[2,256,512]{2,1,0:T(8,128)}, f32[2,256,512]{2,1,0:T(8,128)}, f32[2,512,256]{2,1,0:T(8,128)}) conditional(s32[]{:T(128)} %convert_element_type.8, (s32[2,2048]{1,0:T(2,128)S(1)}, f32[2,2048]{1,0:T(2,128)S(1)}, bf16[2048,512]{1,0:T(8,128)(2,1)S(1)}, ...), branch_computations={%region_2.3_spmd, %region_3.4_spmd} | conditional | flops 2359305 | bytes 170590720 | solution.py:512
  397.6 1.6 fusion.2
  399.2 0.9 copy_bitcast_fusion.2
  400.8 4.2 select_add_fusion.1
  405.0 2.5 select_add_fusion
  407.5 1.4 copy.32
  408.8 16.6 %combine.3 = bf16[2048,512]{1,0:T(8,128)(2,1)} custom-call(s32[2048,2]{1,0:T(8,128)} %bitcast.61, bf16[5120,512]{1,0:T(8,128)(2,1)} %bitcast.6.back_ref, bf16[128,512]{1,0:T(8,128)(2,1)S(1)} %get-tuple-element.82.rest_0_), custom_call_target="tpu_custom_call" | custom-call | tf_op jit(solution)/shard_map/cond/branch_1_fun/combine/pallas_call | solution.py:453
  425.4 1.9 slice.20.back_ref
  427.3 2.9 route_grad.3
  (54 shorter events, 4.6 us)
Async XLA Ops:
  12.4 39.9 %all-to-all-start.3 = ((f32[64,1,384]{2,1,0:T(1,128)}), f32[64,1,384]{2,1,0:T(1,128)S(1)}, u32[]{:S(2)}, u32[]{:S(2)}) async-start(f32[64,1,384]{2,1,0:T(1,128)} %copy.36), calls=%async_computation.3 | async-start | bytes 196608 | tf_op jit(solution)/shard_map/all_to_all | solution.py:346
  23.5 25.8 %copy-start.2 = (bf16[2048,512]{1,0:T(8,128)(2,1)S(1)}, bf16[2048,512]{1,0:T(8,128)(2,1)}, u32[]{:S(2)}) copy-start(bf16[2048,512]{1,0:T(8,128)(2,1)} %x_ref.3) | copy-start | bytes 6291460
  52.4 152.3 %all-to-all-start.4 = ((bf16[64,72,1024]{2,1,0:T(8,128)(2,1)}), bf16[64,72,1024]{2,1,0:T(8,128)(2,1)}, u32[]{:S(2)}, u32[]{:S(2)}) async-start(bf16[64,72,1024]{2,1,0:T(8,128)(2,1)} %bitcast.53), calls=%async_computation.4 | async-start | bytes 18874368 | tf_op jit(solution)/shard_map/all_to_all | solution.py:346
  62.9 15.4 %all-gather.7.cloned.1.call-start = ((), (), s32[]{:S(2)}) async-start(), calls=%async_computation.6 | async-start | bytes 1572864 | tf_op jit(solution)/shard_map/all_gather | solution.py:476
  63.6 29.3 %all-gather.9.cloned.1.call-start = ((), (), s32[]{:S(2)}) async-start(), calls=%async_computation.7 | async-start | bytes 1572864 | tf_op jit(solution)/shard_map/all_gather | solution.py:476
  64.4 43.2 %all-gather.11.cloned.1.call-start = ((), (), s32[]{:S(2)}) async-start(), calls=%async_computation.8 | async-start | bytes 1572864 | tf_op jit(solution)/shard_map/all_gather | solution.py:476
  249.1 9.7 %copy-start.12 = (bf16[2,256,512]{2,1,0:T(8,128)(2,1)S(1)}, bf16[2,256,512]{2,1,0:T(8,128)(2,1)}, u32[]{:S(2)}) copy-start(bf16[2,256,512]{2,1,0:T(8,128)(2,1)} %param.13) | copy-start | bytes 1572868
  249.1 12.2 %copy-start.13 = (bf16[2,256,512]{2,1,0:T(8,128)(2,1)S(1)}, bf16[2,256,512]{2,1,0:T(8,128)(2,1)}, u32[]{:S(2)}) copy-start(bf16[2,256,512]{2,1,0:T(8,128)(2,1)} %param.14) | copy-start | bytes 1572868
  249.1 148.2 %all-to-all-start.5 = ((bf16[64,80,512]{2,1,0:T(8,128)(2,1)}), bf16[64,80,512]{2,1,0:T(8,128)(2,1)}, u32[]{:S(2)}, u32[]{:S(2)}) async-start(bf16[64,80,512]{2,1,0:T(8,128)(2,1)} %get-tuple-element.117), calls=%async_computation.5 | async-start | bytes 10485760 | tf_op jit(solution)/shard_map/all_to_all | solution.py:346
  259.5 2.0 copy-start.14
  261.4 1.0 copy-start.15
  261.7 3.2 copy-start.9
  262.4 4.0 copy-start.10
  264.8 132.4 %collective-permute-start.4 = (f32[2,256,512]{2,1,0:T(8,128)}, f32[2,256,512]{2,1,0:T(8,128)}, u32[]{:S(2)}, u32[]{:S(2)}) collective-permute-start(f32[2,256,512]{2,1,0:T(8,128)} %constant_dynamic-slice_fusion.5), channel_id=1, source_target_pairs={{0,64},{64,0},{1,65},{65,1},{2,66},{66,2},{3,67},{67,3},{4,68},{68... | collective-permute-start | bytes 3145736 | tf_op jit(solution)/shard_map/ppermute | solution.py:486
  264.8 2.7 copy-start
  264.8 2.6 copy-start.1
  265.9 131.4 %collective-permute-start.5 = (f32[2,256,512]{2,1,0:T(8,128)}, f32[2,256,512]{2,1,0:T(8,128)}, u32[]{:S(2)}, u32[]{:S(2)}) collective-permute-start(f32[2,256,512]{2,1,0:T(8,128)} %constant_dynamic-slice_fusion.4), channel_id=1, source_target_pairs={{0,64},{64,0},{1,65},{65,1},{2,66},{66,2},{3,67},{67,3},{4,68},{68... | collective-permute-start | bytes 3145736 | tf_op jit(solution)/shard_map/ppermute | solution.py:486
  267.5 129.8 %collective-permute-start.6 = (f32[2,512,256]{2,1,0:T(8,128)}, f32[2,512,256]{2,1,0:T(8,128)}, u32[]{:S(2)}, u32[]{:S(2)}) collective-permute-start(f32[2,512,256]{2,1,0:T(8,128)} %constant_dynamic-slice_fusion.3), channel_id=1, source_target_pairs={{0,64},{64,0},{1,65},{65,1},{2,66},{66,2},{3,67},{67,3},{4,68},{68... | collective-permute-start | bytes 3145736 | tf_op jit(solution)/shard_map/ppermute | solution.py:486
  267.5 126.0 %copy-start.16 = (f32[64,1,384]{2,0,1:T(8,128)S(1)}, f32[64,1,384]{2,0,1:T(8,128)}, u32[]{:S(2)}) copy-start(f32[64,1,384]{2,0,1:T(8,128)} %copy.52) | copy-start | bytes 294916
  267.5 129.8 %copy-start.3 = (bf16[4,256,512]{2,1,0:T(8,128)(2,1)S(1)}, bf16[4,256,512]{2,1,0:T(8,128)(2,1)}, u32[]{:S(2)}) copy-start(bf16[4,256,512]{2,1,0:T(8,128)(2,1)} %all-gather.7.cloned.1.call-done) | copy-start | bytes 3145732
  267.5 129.8 %copy-start.18 = (s32[2048,2]{0,1:T(2,128)S(1)}, s32[2048,2]{0,1:T(2,128)}, u32[]{:S(2)}) copy-start(s32[2048,2]{0,1:T(2,128)} %param.11) | copy-start | bytes 49156
  267.5 129.8 %copy-start.19 = (f32[2048,2]{0,1:T(2,128)S(1)}, f32[2048,2]{0,1:T(2,128)}, u32[]{:S(2)}) copy-start(f32[2048,2]{0,1:T(2,128)} %param.12) | copy-start | bytes 49156
  395.5 1.2 collective-permute-start.3
  397.6 3.2 copy-start.8
  400.8 4.2 copy-start.11
Sparse Core Ops, SparseCore 0:
  65.3 12.9 all-gather.6
  80.0 12.9 all-gather.8
  94.6 12.9 all-gather.10

commit v3 on v2

v3 whole, which is shorter than its diff:
```python
import functools

import jax
import jax.numpy as jnp
from jax import lax
from jax.experimental import pallas as pl
from jax.experimental.pallas import tpu as pltpu
from jax.sharding import PartitionSpec as P

CAP_FACTOR = 3
LANES = 128
FAR = 1 << 20
TAIL = 8
MESH = pl.DeviceIdType.MESH
f32, bf16, i32 = jnp.float32, jnp.bfloat16, jnp.int32


def capacity_of(tok_dev, top_k, experts):
    return max(8, ((CAP_FACTOR * tok_dev * top_k // experts + 7) // 8) * 8)


def iota(shape, dim):
    return lax.broadcasted_iota(i32, shape, dim)


def nn(a, b):
    return jnp.dot(a, b, preferred_element_type=f32)


def nt(a, b):
    return lax.dot_general(a, b, (((1,), (1,)), ((), ())), preferred_element_type=f32)


def tn(a, b):
    return lax.dot_general(a, b, (((0,), (0,)), ((), ())), preferred_element_type=f32)


def split3(v):
    hi = v.astype(bf16)
    rest = v - hi.astype(f32)
    mid = rest.astype(bf16)
    lo = (rest - mid.astype(f32)).astype(bf16)
    return hi, mid, lo


def hot(mask):
    return jnp.where(mask, 1.0, 0.0).astype(bf16)


def only(mask, v):
    return jnp.where(mask, v, jnp.zeros_like(v))


def down(v):
    return jnp.sum(v, axis=0, keepdims=True)


def across(v):
    return jnp.sum(v, axis=1, keepdims=True)


def add3(v, n):
    return v[:, :n] + v[:, n:2 * n] + v[:, 2 * n:]


SIDE = 4
STRIDES = (1, SIDE, SIDE * SIDE)


def coords(me):
    return [me % SIDE, (me // SIDE) % SIDE, me // (SIDE * SIDE)]


def peer_at(me, r, sign):
    o = (r * 23) % SIDE ** 3
    out = 0
    for here, off, stride in zip(coords(me), coords(o), STRIDES):
        out = out + ((here + sign * off + SIDE) % SIDE) * stride
    return out


def meet_all(me, part):
    barrier = pltpu.get_barrier_semaphore()
    n = SIDE ** 3

    @pl.loop(1, n)
    def _(r):
        pl.semaphore_signal(barrier, inc=1, device_id={"ep": peer_at(me, r, 1)}, device_id_type=MESH)

    pl.semaphore_signal(barrier, inc=1, device_id={"fsdp": 1 - part}, device_id_type=MESH)
    pl.semaphore_wait(barrier, n)


def route_kernel(capacity, rows, depth, span, local_top, ids_ref, rw_ref, q_ref, pos_ref, msg_ref, top_ref, topw_ref):
    experts, chunk = LANES, 256
    tokens = ids_ref.shape[1]
    n_dest = msg_ref.shape[0]
    pitch = rows + TAIL
    before = (iota((chunk, chunk), 0) < iota((chunk, chunk), 1)).astype(bf16)
    expert_id = iota((experts, chunk), 0)
    slot_id = iota((span, chunk), 0)
    half_id = iota((n_dest, chunk), 0) * 2
    seen = jnp.zeros((experts, 1), f32)
    for c in range(tokens // chunk):
        at = slice(c * chunk, (c + 1) * chunk)
        hits = [expert_id == ids_ref[j:j + 1, at] for j in range(2)]
        member = jnp.where(hits[0] | hits[1], 1.0, 0.0)
        earlier = nn(member.astype(bf16), before) + seen
        seen = seen + across(member)
        for j in range(2):
            pos_ref[j:j + 1, at] = down(only(hits[j], earlier)).astype(i32)
    expert_col = iota((experts, 1), 0).astype(f32)
    kept = jnp.minimum(seen, float(capacity))
    if local_top:
        most = jnp.max(seen, axis=0, keepdims=True)
        top = jnp.min(jnp.where(seen == most, expert_col, float(experts)), axis=0, keepdims=True)
        kept = jnp.where(expert_col == top, 0.0, kept)
    else:
        top = jnp.full((1, 1), -1.0, f32)
    top_i = top.astype(i32)
    gates = [jnp.zeros((3 * n_dest, span), f32) for _ in range(2)]
    top_gates = jnp.zeros((24, LANES), f32)
    for c in range(tokens // chunk):
        at = slice(c * chunk, (c + 1) * chunk)
        for j in range(2):
            ids = ids_ref[j:j + 1, at]
            place = pos_ref[j:j + 1, at]
            weight = rw_ref[j:j + 1, at]
            keep = place < capacity
            slot = jnp.where(ids % 2 == 0, place, rows - 1 - place)
            q = (ids // 2) * pitch + slot
            if local_top:
                is_top = ids == top_i
                q = jnp.where(is_top, n_dest * pitch + place, q)
                slot = jnp.where(is_top, FAR, slot)
                top_hot = hot((iota((LANES, chunk), 0) == place) & keep & is_top)
                top_parts = [jnp.broadcast_to(p, (8, chunk)) for p in split3(weight)]
                top_gates = top_gates + nt(jnp.concatenate(top_parts, axis=0), top_hot)
            q_ref[j:j + 1, at] = jnp.where(keep, q, FAR)
            slot_hot = hot(slot_id == jnp.where(keep, slot, FAR))
            for par in range(2):
                mine = only(half_id + par == ids, weight)
                gates[par] = gates[par] + nt(jnp.concatenate(split3(mine), axis=0), slot_hot)
    kept_wide = jnp.broadcast_to(kept, (experts, LANES)).astype(bf16)
    owner = (iota((n_dest, experts), 1) // 2 == iota((n_dest, experts), 0)).astype(bf16)
    over = jnp.max(jnp.where(nn(owner, kept_wide) > float(rows), 1.0, 0.0), axis=0, keepdims=True)
    over = jnp.maximum(over, jnp.max(jnp.where(kept > float(depth), 1.0, 0.0), axis=0, keepdims=True))
    for par in range(2):
        g = gates[par]
        msg_ref[:, par * span:(par + 1) * span] = g[:n_dest] + g[n_dest:2 * n_dest] + g[2 * n_dest:]
    note = jnp.where(iota((1, LANES), 1) == 1, top, over)
    msg_ref[:, 2 * span:] = jnp.broadcast_to(note, (n_dest, LANES))
    top_ref[...] = jnp.broadcast_to(top_i, (8, LANES))
    topw_ref[...] = top_gates[:8] + top_gates[8:16] + top_gates[16:]


def pack_kernel(group, rows, first, q_ref, x_ref, dy_ref, out_ref):
    d = x_ref.shape[1]
    count, tokens = group * rows, q_ref.shape[1]
    row = iota((count, tokens), 0)
    slot = row + (row // rows + pl.program_id(0) * group) * TAIL + pl.program_id(0) * count + first
    pick = hot((q_ref[0:1, :] == slot) | (q_ref[1:2, :] == slot))
    out_ref[:, :d] = nn(pick, x_ref[...]).astype(bf16)
    out_ref[:, d:] = nn(pick, dy_ref[...]).astype(bf16)


def swiglu_rows(x, dy, weight, w1, w3, w2):
    h1 = nn(x, w1)
    h3 = nn(x, w3)
    s = jax.nn.sigmoid(h1)
    hidden = (h1 * s * h3).astype(bf16)
    dr = across(dy * nn(hidden, w2))
    g = (weight * dy).astype(bf16)
    da = nt(g, w2)
    dh1 = (da * h3 * s * (1.0 + h1 * (1.0 - s))).astype(bf16)
    dh3 = (da * h1 * s).astype(bf16)
    return hidden, g, dh1, dh3, nt(dh1, w1) + nt(dh3, w3), dr


def expert_body(depth, span, step, xdy_ref, rec_ref, w1_ref, w3_ref, w2_ref, dx_ref, dwg_ref, dwu_ref, dwd_ref):
    group, rows, width = xdy_ref.shape
    n_src = rec_ref.shape[0]
    d = width // 2
    m = group * depth

    local = iota((m, n_src), 0) // depth
    src_hot = hot(local + step * group == iota((m, n_src), 1))
    row_hot = hot(iota((m, LANES), 0) // depth == iota((m, LANES), 1))
    within = iota((m, span), 0) % depth
    outs, dr_slots = [], jnp.zeros((LANES, span), f32)
    for k in range(2):
        first = 0 if k == 0 else rows - depth
        slot_hot = iota((m, span), 1) == within + first
        gate_parts = jnp.concatenate(split3(rec_ref[:, k * span:(k + 1) * span]), axis=1)
        weight = across(only(slot_hot, add3(nn(src_hot, gate_parts), span)))
        x = xdy_ref[:, first:first + depth, :d].reshape(m, d)
        dy = xdy_ref[:, first:first + depth, d:].reshape(m, d).astype(f32)
        hidden, g, dh1, dh3, dx, dr = swiglu_rows(x, dy, weight, w1_ref[k], w3_ref[k], w2_ref[k])
        outs.append(dx.reshape(group, depth, d))
        dwg_ref[k] += tn(x, dh1)
        dwu_ref[k] += tn(x, dh3)
        dwd_ref[k] += tn(hidden, g)
        parts = jnp.concatenate(split3(only(slot_hot & (weight > 0.0), dr)), axis=1)
        dr_slots = dr_slots + add3(tn(row_hot, parts), span)
    low = rows - depth
    dx_ref[:, :low] = outs[0][:, :low].astype(bf16)
    if depth > low:
        dx_ref[:, low:depth] = (outs[0][:, low:] + outs[1][:, :depth - low]).astype(bf16)
    dx_ref[:, depth:rows] = outs[1][:, depth - low:].astype(bf16)
    parts = split3(dr_slots)
    for i in range(group):
        dx_ref[i, rows:, :] = jnp.zeros((TAIL, d), bf16)
        for n in range(3):
            dx_ref[i, rows + n:rows + n + 1, :span] = parts[n][i:i + 1, :]


def gather_weights(part, own, other, full):
    for mine, theirs, whole_ref, by_rows in zip(own, other, full, (True, True, False)):
        size = mine.shape[1] if by_rows else mine.shape[2]
        for ref, at in ((mine, part * size), (theirs, (1 - part) * size)):
            at = pl.ds(pl.multiple_of(at, LANES), size)
            for k in range(2):
                if by_rows:
                    whole_ref[k, at, :] = ref[k]
                else:
                    whole_ref[k, :, at] = ref[k]


def expert_kernel(depth, span, part_ref, xdy_ref, rec_ref, *refs):
    own, other, (dx_ref, dwg_ref, dwu_ref, dwd_ref), full = refs[:3], refs[3:6], refs[6:10], refs[10:]
    step = pl.program_id(0)

    @pl.when(step == 0)
    def _():
        for ref in (dwg_ref, dwu_ref, dwd_ref):
            ref[...] = jnp.zeros_like(ref)
        gather_weights(part_ref[0], own, other, full)

    expert_body(depth, span, step, xdy_ref, rec_ref, *full, dx_ref, dwg_ref, dwu_ref, dwd_ref)


def expert_send_kernel(depth, span, group, xdy_ref, rec_ref, *refs):
    own, other, dws, back_ref, peers, full = refs[:3], refs[3:6], refs[6:9], refs[9], refs[10:13], refs[13:16]
    dx_buf, ssem, rsem, psem, own_sem = refs[16:]
    me, part = lax.axis_index("ep"), lax.axis_index("fsdp")
    n = xdy_ref.shape[0]
    meet_all(me, part)
    for ref in dws:
        ref[...] = jnp.zeros_like(ref)
    gather_weights(part, own, other, full)

    def send(r):
        return pltpu.make_async_remote_copy(
            src_ref=dx_buf.at[r], dst_ref=back_ref.at[me], send_sem=ssem.at[r], recv_sem=rsem.at[r],
            device_id={"ep": peer_at(me, r, -1)}, device_id_type=MESH)

    keep = pltpu.make_async_copy(dx_buf.at[0], back_ref.at[me], own_sem)

    @pl.loop(0, n // group)
    def _(step):
        at = pl.ds(step * group, group)
        expert_body(depth, span, step, xdy_ref.at[at], rec_ref, *full, dx_buf.at[at], *dws)
        for j in range(group):
            if j == 0:
                @pl.when(step == 0)
                def _():
                    keep.start()

                @pl.when(step > 0)
                def _():
                    send(step * group).start()
            else:
                send(step * group + j).start()

    swaps = []
    for i, (dw, peer) in enumerate(zip(dws, peers)):
        size = peer.shape[1] if i < 2 else peer.shape[2]
        at = pl.ds(pl.multiple_of((1 - part) * size, LANES), size)
        swaps.append(pltpu.make_async_remote_copy(
            src_ref=dw.at[:, at, :] if i < 2 else dw.at[:, :, at], dst_ref=peer,
            send_sem=psem.at[0, i], recv_sem=psem.at[1, i], device_id={"fsdp": 1 - part}, device_id_type=MESH))
    for copy in swaps:
        copy.start()
    for copy in swaps:
        copy.wait()
    keep.wait()

    @pl.loop(1, n)
    def _(r):
        send(r).wait()


def dispatch_kernel(group, q_ref, x_ref, dy_ref, msg_ref, wm_ref, gate_ref,
                    xdy_ref, rec_ref, dx_ref, dr_ref, grad_ref,
                    packed, rows_ref, wbuf, wr0, wr1, wr2, wfull, gfull, gbuf, gpeer, gr0, gr1, gr2,
                    bsem, msem, ssem, rsem, own_sem):
    me, part = lax.axis_index("ep"), lax.axis_index("fsdp")
    coord = coords(me)
    n_mat, total = wbuf.shape[0], wbuf.shape[1]
    levels = len(STRIDES)
    n_dest, rows, _ = xdy_ref.shape
    d, tokens = x_ref.shape[1], x_ref.shape[0]
    pitch = rows + TAIL
    meet_all(me, part)

    def pack(slot):
        pick = hot((q_ref[0:1, :] == slot) | (q_ref[1:2, :] == slot))
        return nn(pick, x_ref[...]).astype(bf16), nn(pick, dy_ref[...]).astype(bf16)

    def block_copies(r):
        to = peer_at(me, r, 1)
        return [pltpu.make_async_remote_copy(
                    src_ref=packed.at[r], dst_ref=xdy_ref.at[r], send_sem=bsem.at[0, r], recv_sem=bsem.at[1, r],
                    device_id={"ep": to}, device_id_type=MESH),
                pltpu.make_async_remote_copy(
                    src_ref=msg_ref.at[to], dst_ref=rec_ref.at[r], send_sem=msem.at[0, r], recv_sem=msem.at[1, r],
                    device_id={"ep": to}, device_id_type=MESH)]

    keep = [pltpu.make_async_copy(packed.at[0], xdy_ref.at[0], own_sem.at[0]),
            pltpu.make_async_copy(msg_ref.at[me], rec_ref.at[0], own_sem.at[1])]

    def send_blocks(step):
        line = iota((group * rows, 1), 0)
        slot = line
        for j in range(group):
            inside = (line >= j * rows) & (line < (j + 1) * rows)
            slot = jnp.where(inside, line - j * rows + peer_at(me, step * group + j, 1) * pitch, slot)
        x_rows, dy_rows = pack(slot)
        for j in range(group):
            at = slice(j * rows, (j + 1) * rows)
            packed[step * group + j, :, :d] = x_rows[at]
            packed[step * group + j, :, d:] = dy_rows[at]
        for j in range(group):
            if j == 0:
                @pl.when(step == 0)
                def _():
                    for copy in keep:
                        copy.start()

                @pl.when(step > 0)
                def _():
                    for copy in block_copies(step * group):
                        copy.start()
            else:
                for copy in block_copies(step * group + j):
                    copy.start()

    sizes = [total // SIDE ** (level + 1) for level in range(levels)]

    def base_of(c, level):
        base = 0
        for i in range(level):
            base = base + coord[(c + i) % 3] * sizes[i]
        return base

    def at(base, size):
        return pl.ds(pl.multiple_of(base, 16), size)

    def peer(axis, delta):
        return me + ((coord[axis] + delta) % SIDE - coord[axis]) * STRIDES[axis]

    w_put = lambda c, s: wfull.at[part, c, s]
    g_put = lambda c, s: grad_ref.at[c, s]
    plans = ((wbuf, (wr0, wr1, wr2), w_put), (gbuf, (gr0, gr1, gr2), g_put))

    def scatter_copies(which, level):
        buf, recvs, _ = plans[which]
        out = []
        for c in range(n_mat):
            axis = (c + level) % 3
            for delta in (1, 2, 3):
                to = (coord[axis] + delta) % SIDE
                out.append(pltpu.make_async_remote_copy(
                    src_ref=buf.at[c, at(base_of(c, level) + to * sizes[level], sizes[level])],
                    dst_ref=recvs[level].at[c, 3 - delta],
                    send_sem=ssem.at[which, 0, level, c, delta - 1], recv_sem=rsem.at[which, 0, level, c, 3 - delta],
                    device_id={"ep": peer(axis, delta)}, device_id_type=MESH))
        return out

    def scatter_add(which, level):
        buf, recvs, put = plans[which]
        for c in range(n_mat):
            mine = at(base_of(c, level + 1), sizes[level])
            got = [recvs[level][c, i].astype(f32) for i in range(3)]
            value = (buf[c, mine].astype(f32) + got[0] + got[1] + got[2]).astype(buf.dtype)
            if level == levels - 1:
                put(c, mine)[...] = value
            else:
                buf[c, mine] = value

    def gather_copies(which, level):
        put = plans[which][2]
        out = []
        for c in range(n_mat):
            axis = (c + level) % 3
            mine = at(base_of(c, level + 1), sizes[level])
            for delta in (1, 2, 3):
                out.append(pltpu.make_async_remote_copy(
                    src_ref=put(c, mine), dst_ref=put(c, mine),
                    send_sem=ssem.at[which, 1, level, c, delta - 1], recv_sem=rsem.at[which, 1, level, c, 3 - delta],
                    device_id={"ep": peer(axis, delta)}, device_id_type=MESH))
        return out

    def swap_copies(which):
        src, dst = ((wfull.at[part], wfull.at[part]), (gfull.at[1 - part], gpeer))[which]
        return [pltpu.make_async_remote_copy(
            src_ref=src, dst_ref=dst, send_sem=ssem.at[which, 2, 0, 0, 0], recv_sem=rsem.at[which, 2, 0, 0, 0],
            device_id={"fsdp": 1 - part}, device_id_type=MESH)]

    def serve_top():
        half, wide = d // 2, d // LANES
        mats = []
        for i in range(2):
            mats.append(jnp.concatenate([jnp.concatenate(
                [wfull[f, i, b * half:(b + 1) * half, :] for b in range(wide)], axis=1) for f in range(2)], axis=0))
        w2 = jnp.concatenate([wfull[f, 2, b * d:(b + 1) * d, :] for f in range(2) for b in range(wide // 2)], axis=1)
        n = rows_ref.shape[0]
        x = rows_ref[:, :d]
        dy = rows_ref[:, d:].astype(f32)
        eye = iota((n, n), 0) == iota((n, n), 1)
        weight = across(only(eye, gate_ref[0:1, :]))
        hidden, g, dh1, dh3, dx, dr = swiglu_rows(x, dy, weight, mats[0], mats[1], w2)
        dx_ref[...] = dx.astype(bf16)
        dr_ref[...] = jnp.broadcast_to(dr, dr_ref.shape)
        for i, dh in enumerate((dh1, dh3)):
            dw = tn(x, dh)
            for f in range(2):
                for b in range(wide):
                    gfull[f, i, b * half:(b + 1) * half, :] = dw[f * half:(f + 1) * half, b * LANES:(b + 1) * LANES]
        dw = tn(hidden, g)
        for f in range(2):
            for b in range(wide // 2):
                lane = f * half + b * LANES
                gfull[f, 2, b * d:(b + 1) * d, :] = dw[:, lane:lane + LANES]

    def fold_peer():
        gbuf[...] = gfull[part] + gpeer[...]

    phases = []
    for which in range(2):
        if which == 1:
            phases.append((lambda: swap_copies(1), fold_peer))
        for level in range(levels):
            phases.append((functools.partial(scatter_copies, which, level), functools.partial(scatter_add, which, level)))
        for level in reversed(range(levels)):
            phases.append((functools.partial(gather_copies, which, level), None))
        if which == 0:
            phases.append((lambda: swap_copies(0), serve_top))

    wbuf[...] = wm_ref[...]
    x_rows, dy_rows = pack(iota((rows_ref.shape[0], 1), 0) + n_dest * pitch)
    rows_ref[:, :d] = x_rows
    rows_ref[:, d:] = dy_rows
    steps = n_dest // group

    @pl.loop(0, steps)
    def _(step):
        for i, (copies, _) in enumerate(phases):
            @pl.when(step == i)
            def _(copies=copies):
                for copy in copies():
                    copy.start()

        send_blocks(step)

        for i, (copies, then) in enumerate(phases):
            @pl.when(step == i)
            def _(copies=copies, then=then):
                for copy in copies():
                    copy.wait()
                if then is not None:
                    then()

    for copy in keep:
        copy.wait()

    @pl.loop(1, n_dest)
    def _(r):
        for copy in block_copies(r):
            copy.wait()


def dr_kernel(rows, span, ids_ref, q_ref, pos_ref, back_ref, top_dr_ref, out_ref):
    n_src = back_ref.shape[0]
    tokens = ids_ref.shape[1]
    pitch = rows + TAIL
    chunk = 512
    tables = [back_ref[:, n, :span].T for n in range(3)]
    for c in range(tokens // chunk):
        at = slice(c * chunk, (c + 1) * chunk)
        for j in range(2):
            block = ids_ref[j:j + 1, at] // 2
            q = q_ref[j:j + 1, at]
            owner = hot(iota((n_src, chunk), 0) == block)
            column = nn(tables[0], owner) + nn(tables[1], owner) + nn(tables[2], owner)
            far = q >= n_src * pitch
            want = jnp.where(far, FAR, q - block * pitch)
            picked = down(only(iota((span, chunk), 0) == want, column))
            if top_dr_ref is not None:
                want = jnp.where(far, q - n_src * pitch, FAR)
                picked = picked + down(
                    only(iota((LANES, chunk), 0) == want, top_dr_ref[:, 0:1]))
            out_ref[j:j + 1, at] = picked


def combine_kernel(q_ref, back_ref, *rest):
    top_ref, out_ref = rest if len(rest) == 2 else (None, rest[0])
    rows, slots = q_ref.shape[0], back_ref.shape[0]
    q0, q1 = q_ref[:, 0:1], q_ref[:, 1:2]
    acc = jnp.zeros(out_ref.shape, f32)
    for at in range(0, slots, 512):
        depth = min(512, slots - at)
        column = iota((rows, depth), 1) + at
        pick = hot((q0 == column) | (q1 == column))
        acc = acc + nn(pick, back_ref[at:at + depth, :])
    if top_ref is not None:
        column = iota((rows, LANES), 1) + slots
        pick = hot((q0 == column) | (q1 == column))
        acc = acc + nn(pick, top_ref[...])
    out_ref[...] = acc.astype(bf16)


def vmem():
    return pl.BlockSpec(memory_space=pltpu.VMEM)


def whole(shape):
    return pl.BlockSpec(shape, lambda i: (0,) * len(shape))


PARAMS = pltpu.CompilerParams(vmem_limit_bytes=60 * 1024 * 1024)


def exchange(v):
    return lax.all_to_all(v, "ep", 0, 0, tiled=True)


ANYWHERE = pl.BlockSpec(memory_space=pl.ANY)


def dispatch(q_t, x_tok, dy_tok, msg, w_mine, gate, n_dest, rows):
    d, n_mat, total = x_tok.shape[1], 3, w_mine.shape[1]
    scratch = [pltpu.VMEM((n_dest, rows, 2 * d), bf16), pltpu.VMEM((LANES, 2 * d), bf16)]
    for dtype in (bf16, f32):
        recvs = [pltpu.VMEM((n_mat, 3, total // 4 ** (i + 1), LANES), dtype) for i in range(3)]
        if dtype == bf16:
            scratch += [pltpu.VMEM((n_mat, total, LANES), dtype), *recvs, pltpu.VMEM((2, n_mat, total, LANES), dtype)]
        else:
            scratch += [pltpu.VMEM((2, n_mat, total, LANES), dtype), pltpu.VMEM((n_mat, total, LANES), dtype),
                        pltpu.VMEM((n_mat, total, LANES), dtype), *recvs]
    dma = pltpu.SemaphoreType.DMA
    scratch += [dma((2, n_dest)), dma((2, n_dest)), dma((2, 3, 3, n_mat, 3)), dma((2, 3, 3, n_mat, 3)), dma((2,))]
    return pl.pallas_call(
        functools.partial(dispatch_kernel, 4),
        out_shape=(jax.ShapeDtypeStruct((n_dest, rows, 2 * d), bf16),
                   jax.ShapeDtypeStruct(msg.shape, f32),
                   jax.ShapeDtypeStruct((LANES, d), bf16),
                   jax.ShapeDtypeStruct((LANES, LANES), f32),
                   jax.ShapeDtypeStruct((n_mat, total, LANES), f32)),
        in_specs=[vmem()] * 6, out_specs=(ANYWHERE, vmem(), vmem(), vmem(), vmem()), scratch_shapes=scratch,
        compiler_params=pltpu.CompilerParams(
            vmem_limit_bytes=60 * 1024 * 1024, collective_id=0, has_side_effects=True),
        cost_estimate=pl.CostEstimate(flops=100_000_000_000, bytes_accessed=30_000_000, transcendentals=0),
        name="dispatch",
    )(q_t, x_tok, dy_tok, msg, w_mine, gate)


class Plan:
    def __init__(self, rows, depth, pack_group, group, capacity, n_ep, local_top):
        self.rows, self.depth, self.pack_group, self.group = rows, depth, pack_group, group
        self.capacity, self.n_ep, self.local_top = capacity, n_ep, local_top
        self.span = -(-rows // LANES) * LANES

    def pack(self, q_t, x_tok, dy_tok, group, rows, steps, first):
        tok_dev, d = x_tok.shape
        return pl.pallas_call(
            functools.partial(pack_kernel, group, rows, first),
            out_shape=jax.ShapeDtypeStruct((steps * group * rows, 2 * d), bf16),
            grid=(steps,),
            in_specs=[whole((2, tok_dev)), whole((tok_dev, d)), whole((tok_dev, d))],
            out_specs=pl.BlockSpec((group * rows, 2 * d), lambda i: (i, 0)),
            compiler_params=PARAMS, name="pack",
        )(q_t, x_tok, dy_tok)

    def route(self, ids_t, rw_t):
        n_ep, rows, span, tok_dev = self.n_ep, self.rows, self.span, ids_t.shape[1]
        q_t, _, msg, top, gate = pl.pallas_call(
            functools.partial(route_kernel, self.capacity, rows, self.depth, span, self.local_top),
            out_shape=(jax.ShapeDtypeStruct((2, tok_dev), i32), jax.ShapeDtypeStruct((2, tok_dev), i32),
                       jax.ShapeDtypeStruct((n_ep, 2 * span + LANES), f32),
                       jax.ShapeDtypeStruct((8, LANES), i32), jax.ShapeDtypeStruct((8, LANES), f32)),
            in_specs=[vmem(), vmem()], out_specs=(vmem(),) * 5, compiler_params=PARAMS, name="route",
        )(ids_t, rw_t)
        return q_t, msg, top, gate

    def forward(self, me, part, x_tok, dy_tok, ids_t, rw_t, weights, own):
        d = x_tok.shape[1]
        n_ep, rows = self.n_ep, self.rows
        q_t, msg, _, _ = self.route(ids_t, rw_t)
        rec = exchange(msg)
        packed = self.pack(q_t, x_tok, dy_tok, self.pack_group, rows, n_ep // self.pack_group, 0)
        xdy = exchange(packed.reshape(n_ep, rows, 2 * d))
        dx, *dws = self.experts(part, xdy, rec, weights, own)
        return q_t, exchange(dx), dws

    def forward_top(self, me, part, x_tok, dy_tok, ids_t, rw_t, weights, own):
        n_ep, rows, span = self.n_ep, self.rows, self.span
        q_t, msg, top, gate = self.route(ids_t, rw_t)
        top_id = top[0, 0]
        mine = top_id // 2 == me
        flat = []
        for w in own:
            one = lax.dynamic_index_in_dim(w, top_id % 2, 0, keepdims=False)
            one = jnp.where(mine, one, jnp.zeros_like(one))
            flat.append(one.reshape(one.shape[0], -1, LANES).transpose(1, 0, 2).reshape(-1, LANES))
        xdy, rec, top_dx, top_dr, top_grad = dispatch(
            q_t, x_tok, dy_tok, msg.reshape(n_ep, 1, -1), jnp.stack(flat), gate, n_ep, rows)
        rec = rec.reshape(n_ep, -1)
        dws, back, peers = self.experts_send(xdy, rec, weights, own)
        return rec[:, 2 * span:], q_t, back, (top_id, top_dx, top_dr, top_grad), dws, peers

    def experts(self, part, xdy, rec, weights, own):
        n_ep, rows, width = xdy.shape
        d, group, span = width // 2, self.group, self.span
        ff = own[0].shape[2]
        return pl.pallas_call(
            functools.partial(expert_kernel, self.depth, span),
            out_shape=(jax.ShapeDtypeStruct((n_ep, rows + TAIL, d), bf16),
                       jax.ShapeDtypeStruct((2, d, ff), f32),
                       jax.ShapeDtypeStruct((2, d, ff), f32),
                       jax.ShapeDtypeStruct((2, ff, d), f32)),
            grid=(n_ep // group,),
            in_specs=[pl.BlockSpec(memory_space=pltpu.SMEM), pl.BlockSpec((group, rows, width), lambda i: (i, 0, 0)),
                      whole(rec.shape)] + [whole(w.shape) for w in (*own, *weights)],
            out_specs=(pl.BlockSpec((group, rows + TAIL, d), lambda i: (i, 0, 0)),
                       whole((2, d, ff)), whole((2, d, ff)), whole((2, ff, d))),
            scratch_shapes=[pltpu.VMEM((2, d, ff), bf16), pltpu.VMEM((2, d, ff), bf16), pltpu.VMEM((2, ff, d), bf16)],
            compiler_params=PARAMS, name="experts",
        )(part.reshape(1), xdy, rec, *own, *weights)

    def experts_send(self, xdy, rec, weights, own):
        n_ep, rows, width = xdy.shape
        d, ff = width // 2, own[0].shape[2]
        pitch = rows + TAIL
        dma = pltpu.SemaphoreType.DMA
        out = pl.pallas_call(
            functools.partial(expert_send_kernel, self.depth, self.span, self.group),
            out_shape=(jax.ShapeDtypeStruct((2, d, ff), f32), jax.ShapeDtypeStruct((2, d, ff), f32),
                       jax.ShapeDtypeStruct((2, ff, d), f32), jax.ShapeDtypeStruct((n_ep, pitch, d), bf16),
                       *(jax.ShapeDtypeStruct(w.shape, f32) for w in own)),
            in_specs=[vmem()] * 8, out_specs=(vmem(),) * 3 + (ANYWHERE,) * 4,
            scratch_shapes=[pltpu.VMEM((2, d, ff), bf16), pltpu.VMEM((2, d, ff), bf16), pltpu.VMEM((2, ff, d), bf16),
                            pltpu.VMEM((n_ep, pitch, d), bf16), dma((n_ep,)), dma((n_ep,)), dma((2, 3)), dma],
            compiler_params=pltpu.CompilerParams(
                vmem_limit_bytes=60 * 1024 * 1024, collective_id=1, has_side_effects=True),
            cost_estimate=pl.CostEstimate(flops=60_000_000_000, bytes_accessed=30_000_000, transcendentals=0),
            name="experts_send",
        )(xdy, rec, *own, *weights)
        return out[:3], out[3], out[4:]

    def finish(self, ids_t, q_t, back, top_out):
        tok_dev, (n_ep, pitch, d), tile = q_t.shape[1], back.shape, 256
        tail = back[:, self.rows:, :]
        dr_args = [ids_t, q_t, q_t, tail] + ([top_out[2]] if top_out else [])
        kernel = functools.partial(dr_kernel, self.rows, self.span)
        if not top_out:
            inner = kernel
            kernel = lambda a, b, c, e, out: inner(a, b, c, e, None, out)
        dr_t = pl.pallas_call(
            kernel, out_shape=jax.ShapeDtypeStruct((2, tok_dev), f32),
            in_specs=[vmem()] * len(dr_args), out_specs=vmem(), compiler_params=PARAMS, name="route_grad",
        )(*dr_args)
        slots = n_ep * pitch
        args = [q_t.T, back.reshape(slots, d)] + ([top_out[1]] if top_out else [])
        grad_x = pl.pallas_call(
            combine_kernel,
            out_shape=jax.ShapeDtypeStruct((tok_dev, d), bf16),
            grid=(tok_dev // tile,),
            in_specs=[pl.BlockSpec((tile, 2), lambda i: (i, 0))] + [whole(v.shape) for v in args[1:]],
            out_specs=pl.BlockSpec((tile, d), lambda i: (i, 0)),
            compiler_params=PARAMS, name="combine",
        )(*args)
        return grad_x, dr_t.T


def solution(mesh):
    n_ep = mesh.shape["ep"]
    tok_spec = P(("fsdp", "ep"), None)
    spec_in = P("ep", "fsdp", None)
    spec_out = P("ep", None, "fsdp")

    def per_device(x_tok, dy_tok, expert_ids, route_w, w_gate, w_up, w_down):
        tok_dev, top_k = expert_ids.shape
        capacity = capacity_of(tok_dev, top_k, w_gate.shape[0] * n_ep)
        me, part = lax.axis_index("ep").astype(i32), lax.axis_index("fsdp").astype(i32)
        swap = [(0, 1), (1, 0)]
        own = (w_gate, w_up, w_down)
        weights = [lax.ppermute(w, "fsdp", swap) for w in own]
        ids_t = expert_ids.T
        inputs = (me, part, x_tok, dy_tok, ids_t, route_w.T, weights, own)

        def shard_halves(dws):
            out = []
            for dw, axis in zip(dws, (1, 1, 2)):
                size = dw.shape[axis] // 2
                keep = lax.dynamic_slice_in_dim(dw, part * size, size, axis)
                give = lax.dynamic_slice_in_dim(dw, (1 - part) * size, size, axis)
                out.append(keep + lax.ppermute(give, "fsdp", swap))
            return out

        quick = Plan(72, 48, 4, 8, capacity, n_ep, True)
        safe = Plan(2 * capacity, capacity, 2, 4, capacity, n_ep, False)
        notes, q_t, back, top_out, dws, peers = quick.forward_top(*inputs)
        top_id = top_out[0]
        agree = jnp.all(notes[:, 1] == top_id.astype(f32)) & jnp.all(notes[:, 0] == 0.0)
        note = jnp.where(agree, top_id.astype(f32), -1.0).reshape(1, 1)
        other = lax.ppermute(note, "fsdp", swap)
        good = agree & (other == note)[0, 0]

        def fits():
            grads = []
            for i, (dw, peer) in enumerate(zip(dws, peers)):
                axis = 1 if i < 2 else 2
                size = peer.shape[axis]
                half = lax.dynamic_slice_in_dim(dw, part * size, size, axis) + peer
                rows = half.shape[1]
                extra = top_out[3][i].reshape(-1, rows, LANES).transpose(1, 0, 2).reshape(1, *half.shape[1:])
                pick = (jnp.arange(2) + 2 * me == top_id)[:, None, None]
                grads.append(half + only(pick, extra))
            return (*quick.finish(ids_t, q_t, back, top_out), *grads)

        def general():
            q_all, back_all, dw_all = safe.forward(*inputs)
            return (*safe.finish(ids_t, q_all, back_all, None), *shard_halves(dw_all))

        return lax.cond(good, fits, general)

    return jax.shard_map(
        per_device, mesh=mesh,
        in_specs=(tok_spec, tok_spec, tok_spec, tok_spec, spec_in, spec_in, spec_out),
        out_specs=(tok_spec, tok_spec, spec_in, spec_in, spec_out),
        check_vma=False)
```

time: 440 us -> 335 us (0.76)
  waiting for transfers between devices: 141 us -> 0.29 us
  Pallas kernels: 222 us -> 302 us
  starting transfers between devices: 29 us -> 1.76 us
  between operations: 19 us -> 5.95 us
  local copies, waits for them, and re-layouts: 16.6 us -> 8.18 us
    all_to_all x3 -> x0, waiting for transfers between devices: 97.1 us -> none  [exchange(): return lax.all_to_all(v, 'ep', 0, 0, tiled=True)]
    pallas_call x5 -> x3, Pallas kernels: 202 us -> 283 us  [the longest x1 185 us: dispatch(): pl.pallas_call(functools.partial(dispatch_kernel, 4), out_shape=(jax.Shap...]
    all_gather x3 -> x0, waiting for transfers between devices: 41.8 us -> none  [per_device(): weights = [lax.all_gather(w, 'fsdp', axis=0) for w in own]]
    all_to_all x3 -> x0, starting transfers between devices: 27.5 us -> none  [exchange(): return lax.all_to_all(v, 'ep', 0, 0, tiled=True)]
    dynamic_slice x3 -> x0, local copies, waits for them, and re-layouts: 4.54 us -> none  [shard_halves(): give = lax.dynamic_slice_in_dim(dw, (1 - part) * size, size, axis)]
  transfers between devices with their start and end apart: 10 -> 4, of which waited for: 5 -> 1; matrix products, arithmetic and copies ran while one was open for 2% -> 2% of each run, Pallas kernels for 35% -> 57%
where the time goes in v3:
time: 335 us; the launch traced here: 329 us
  Pallas kernels  302 us (90%)
  other arithmetic  10.6 us (3%)
  local copies, waits for them, and re-layouts  8.18 us (2%)
  between operations  5.95 us (2%)
    pallas_call x1, Pallas kernels, dispatch(): pl.pallas_call(functools.partial(dispatch_kernel, 4), out_shape=(jax.Shap...  185 us
    pallas_call x1, Pallas kernels, experts_send(): pl.pallas_call(functools.partial(expert_send_kernel, self.depth, self.spa...  93.6 us
    pallas_call x1, Pallas kernels, finish(): pl.pallas_call(combine_kernel, out_shape=jax.ShapeDtypeStruct((tok_dev, d...  16.6 us
  transfers between devices with their start and end apart: 4, of which 1 were waited for; matrix products, arithmetic and copies ran while one was open for 2% of the time, Pallas kernels for 57%

profile of v3, /device:TPU:32, one launch (start us, length us, event | category | flops | bytes accessed | tf_op | source)
XLA Modules:
  0.0 329.3 jit_solution(11103225422950162166)
XLA Ops:
  0.6 0.1 collective-permute-start.4
  0.7 0.5 collective-permute-start.5
  1.2 0.1 collective-permute-start.6
  1.3 3.6 %route.3 = (s32[2,2048]{1,0:T(2,128)S(1)}, s32[2,2048]{1,0:T(2,128)}, f32[64,384]{1,0:T(8,128)}, s32[8,128]{1,0:T(8,128)}, f32[8,128]{1,0:T(8,128)}) custom-call(s32[2,2048]{1,0:T(2,128)} %bitcast.62, f32[2,2048]{1,0:T(2,128)} %bitcast.66), custom_call_target="tpu_custom_call" | custom-call | tf_op jit(solution)/shard_map/route/pallas_call | solution.py:587
  5.0 1.3 slice.27
  8.8 1.0 dynamic-slice_select_fusion.2
  9.8 0.0 copy-start.12
  9.8 1.0 dynamic-slice_select_fusion.1
  10.8 1.0 dynamic-slice_select_fusion
  11.8 0.1 select_n.89
  11.8 0.0 copy-start
  11.9 0.1 select_n.91
  12.0 0.1 select_n.94
  12.1 0.7 reshape.63.msg_ref
  12.9 1.0 pad_maximum_fusion.wm_ref
  13.8 185.4 %dispatch.1 = (bf16[64,72,1024]{2,1,0:T(8,128)(2,1)}, f32[64,1,384]{2,1,0:T(1,128)}, bf16[128,512]{1,0:T(8,128)(2,1)S(1)}, f32[128,128]{1,0:T(8,128)S(1)}, f32[3,1024,128]{2,1,0:T(8,128)}) custom-call(s32[2,2048]{1,0:T(2,128)S(1)} %get-tuple-element.105.q_ref, bf16[2048,512]{1,0:T(8,128)(2,1)S(1)} %copy-done, bf16[2048,512]{1,0:T(8,128)(2,1)} %dy_ref.1, ...), custom_call_target="tpu_custom_call" | custom-call | flops 99999997952 | bytes 30000000 | tf_op jit(solution)/shard_map/dispatch/pallas_call | solution.py:553
  199.8 0.9 copy.51
  200.7 0.7 fusion.1
  202.8 1.1 collective-permute-start.3
  203.8 0.3 collective-permute-done.3
  204.8 0.0 copy-start.13
  204.8 93.6 %experts_send.1 = (f32[2,512,512]{2,1,0:T(8,128)}, f32[2,512,512]{2,1,0:T(8,128)}, f32[2,512,512]{2,1,0:T(8,128)}, bf16[64,80,512]{2,1,0:T(8,128)(2,1)}, f32[2,2...) custom-call(bf16[64,72,1024]{2,1,0:T(8,128)(2,1)} %get-tuple-element.110.xdy_ref, ...), custom_call_target="tpu_custom_call" | custom-call | flops 60000002048 | bytes 30000000 | tf_op jit(solution)/shard_map/experts_send/pallas_call | solution.py:646
  298.5 30.7 %conditional.1 = (bf16[2048,512]{1,0:T(8,128)(2,1)}, f32[2048,2]{0,1:T(2,128)}, f32[2,256,512]{2,1,0:T(8,128)}, f32[2,256,512]{2,1,0:T(8,128)}, f32[2,512,256]{2,1,0:T(8,128)}) conditional(s32[]{:T(128)} %convert_element_type.8, (s32[2,2048]{1,0:T(2,128)S(1)}, f32[2,2048]{1,0:T(2,128)S(1)}, s32[]{:T(128)}, bf16[2048,512]{1,0:T(8,128)(2,1)S(1)}, ...), branch_computations={%region_2.3_spmd, %region_3.4_spmd} | conditional | flops 2359305 | bytes 164299200 | solution.py:736
  298.8 1.5 fusion.2
  300.4 0.1 copy_bitcast_fusion.2
  300.5 0.6 add_compare_fusion
  301.2 4.0 %select_add_fusion.1 = (f32[2,256,512]{2,1,0:T(8,128)}, f32[2,256,512]{2,1,0:T(8,128)}) fusion(f32[2,256,512]{2,1,0:T(8,128)} %get-tuple-element.81, f32[2,512,512]{2,1,0:T(8,128)} %get-tuple-element.80, s32[]{:T(128)S(6)} %select_n.68, f32[256,512]{1,0:T(8,128)S(1)} %get-tuple-element.133, pred[2]{0:T(512)(128)(4,1)S(1)} %add_compare_fusion, ...), kind=kLoop, calls=%fused_computation.8 | loop fusion | flops 1572864 | bytes 7340038 | tf_op jit(solution)/shard_map/cond/branch_1_fun/add | solution.py:729
  305.3 1.3 select_add_fusion
  306.5 1.4 copy.32
  307.9 16.6 %combine.3 = bf16[2048,512]{1,0:T(8,128)(2,1)} custom-call(s32[2048,2]{1,0:T(8,128)} %bitcast.51, bf16[5120,512]{1,0:T(8,128)(2,1)} %bitcast.49, bf16[128,512]{1,0:T(8,128)(2,1)S(1)} %get-tuple-element.71.rest_0_), custom_call_target="tpu_custom_call" | custom-call | tf_op jit(solution)/shard_map/cond/branch_1_fun/combine/pallas_call | solution.py:675
  324.4 1.9 slice.20.back_ref
  326.3 2.9 route_grad.3
  (24 shorter events, 0.2 us)
Async XLA Ops:
  0.6 204.1 %collective-permute-start.4 = (bf16[2,256,512]{2,1,0:T(8,128)(2,1)}, bf16[2,256,512]{2,1,0:T(8,128)(2,1)}, u32[]{:S(2)}, u32[]{:S(2)}) collective-permute-start(bf16[2,256,512]{2,1,0:T(8,128)(2,1)} %refs_0_.1), channel_id=1, source_target_pairs={{0,64},{64,0},{1,65},{65,1},{2,66},{66,2},{3,67},{67,3},{4,68},{68... | collective-permute-start | bytes 1572872 | tf_op jit(solution)/shard_map/ppermute | solution.py:698
  0.7 204.0 %collective-permute-start.5 = (bf16[2,256,512]{2,1,0:T(8,128)(2,1)}, bf16[2,256,512]{2,1,0:T(8,128)(2,1)}, u32[]{:S(2)}, u32[]{:S(2)}) collective-permute-start(bf16[2,256,512]{2,1,0:T(8,128)(2,1)} %refs_1_.1), channel_id=1, source_target_pairs={{0,64},{64,0},{1,65},{65,1},{2,66},{66,2},{3,67},{67,3},{4,68},{68... | collective-permute-start | bytes 1572872 | tf_op jit(solution)/shard_map/ppermute | solution.py:698
  1.2 203.6 %collective-permute-start.6 = (bf16[2,512,256]{2,1,0:T(8,128)(2,1)}, bf16[2,512,256]{2,1,0:T(8,128)(2,1)}, u32[]{:S(2)}, u32[]{:S(2)}) collective-permute-start(bf16[2,512,256]{2,1,0:T(8,128)(2,1)} %refs_2_.1), channel_id=1, source_target_pairs={{0,64},{64,0},{1,65},{65,1},{2,66},{66,2},{3,67},{67,3},{4,68},{68... | collective-permute-start | bytes 1572872 | tf_op jit(solution)/shard_map/ppermute | solution.py:698
  9.8 2.4 copy-start.12
  11.8 2.0 copy-start
  13.8 191.0 %copy-start.3 = (bf16[2,512,256]{2,1,0:T(8,128)(2,1)S(1)}, bf16[2,512,256]{2,1,0:T(8,128)(2,1)}, u32[]{:S(2)}) copy-start(bf16[2,512,256]{2,1,0:T(8,128)(2,1)} %refs_2_.1) | copy-start | bytes 1572868
  13.8 191.0 %copy-start.4 = (bf16[2,256,512]{2,1,0:T(8,128)(2,1)S(1)}, bf16[2,256,512]{2,1,0:T(8,128)(2,1)}, u32[]{:S(2)}) copy-start(bf16[2,256,512]{2,1,0:T(8,128)(2,1)} %refs_1_.1) | copy-start | bytes 1572868
  200.7 4.1 %copy-start.9 = (f32[64,1,384]{2,0,1:T(8,128)}, f32[64,1,384]{2,0,1:T(8,128)S(1)}, u32[]{:S(2)}) copy-start(f32[64,1,384]{2,0,1:T(8,128)S(1)} %copy.51) | copy-start | bytes 294916
  202.8 1.4 collective-permute-start.3
  204.8 93.7 %copy-start.11 = (s32[2048,2]{0,1:T(2,128)S(1)}, s32[2048,2]{0,1:T(2,128)}, u32[]{:S(2)}) copy-start(s32[2048,2]{0,1:T(2,128)} %param.11) | copy-start | bytes 49156
  204.8 93.7 %copy-start.13 = (f32[2048,2]{0,1:T(2,128)S(1)}, f32[2048,2]{0,1:T(2,128)}, u32[]{:S(2)}) copy-start(f32[2048,2]{0,1:T(2,128)} %param.12) | copy-start | bytes 49156
  298.8 2.4 copy-start.6
  301.2 4.1 %copy-start.7 = (f32[2,512,256]{2,1,0:T(8,128)S(1)}, f32[2,512,256]{2,1,0:T(8,128)}, u32[]{:S(2)}) copy-start(f32[2,512,256]{2,1,0:T(8,128)} %get-tuple-element.83) | copy-start | bytes 3145732 | tf_op jit(solution)/shard_map/cond
  301.2 4.1 %copy-start.8 = (f32[2,512,512]{2,1,0:T(8,128)S(1)}, f32[2,512,512]{2,1,0:T(8,128)}, u32[]{:S(2)}) copy-start(f32[2,512,512]{2,1,0:T(8,128)} %get-tuple-element.82) | copy-start | bytes 6291460 | tf_op jit(solution)/shard_map/cond

commit v4 on v3

v4 whole, which is shorter than its diff:
```python
import functools

import jax
import jax.numpy as jnp
from jax import lax
from jax.experimental import pallas as pl
from jax.experimental.pallas import tpu as pltpu
from jax.sharding import PartitionSpec as P

CAP_FACTOR = 3
LANES = 128
FAR = 1 << 20
MESH = pl.DeviceIdType.MESH
f32, bf16, i32 = jnp.float32, jnp.bfloat16, jnp.int32


def capacity_of(tok_dev, top_k, experts):
    return max(8, ((CAP_FACTOR * tok_dev * top_k // experts + 7) // 8) * 8)


def iota(shape, dim):
    return lax.broadcasted_iota(i32, shape, dim)


def nn(a, b):
    return jnp.dot(a, b, preferred_element_type=f32)


def nt(a, b):
    return lax.dot_general(a, b, (((1,), (1,)), ((), ())), preferred_element_type=f32)


def tn(a, b):
    return lax.dot_general(a, b, (((0,), (0,)), ((), ())), preferred_element_type=f32)


def split3(v):
    hi = v.astype(bf16)
    rest = v - hi.astype(f32)
    mid = rest.astype(bf16)
    lo = (rest - mid.astype(f32)).astype(bf16)
    return hi, mid, lo


def hot(mask):
    return jnp.where(mask, 1.0, 0.0).astype(bf16)


def only(mask, v):
    return jnp.where(mask, v, jnp.zeros_like(v))


def down(v):
    return jnp.sum(v, axis=0, keepdims=True)


def across(v):
    return jnp.sum(v, axis=1, keepdims=True)


def add3(v, n):
    return v[:, :n] + v[:, n:2 * n] + v[:, 2 * n:]


SIDE = 4
STRIDES = (1, SIDE, SIDE * SIDE)


def coords(me):
    return [me % SIDE, (me // SIDE) % SIDE, me // (SIDE * SIDE)]


def peer_at(me, r, sign):
    o = (r * 23) % SIDE ** 3
    out = 0
    for here, off, stride in zip(coords(me), coords(o), STRIDES):
        out = out + ((here + sign * off + SIDE) % SIDE) * stride
    return out


def meet_all(me, part):
    barrier = pltpu.get_barrier_semaphore()
    n = SIDE ** 3

    @pl.loop(1, n)
    def _(r):
        pl.semaphore_signal(barrier, inc=1, device_id={"ep": peer_at(me, r, 1)}, device_id_type=MESH)

    pl.semaphore_signal(barrier, inc=1, device_id={"fsdp": 1 - part}, device_id_type=MESH)
    pl.semaphore_wait(barrier, n)


def remote(src, dst, sems, at, to, back=None):
    return pltpu.make_async_remote_copy(
        src_ref=src, dst_ref=dst, send_sem=sems.at[(0, *at)], recv_sem=sems.at[(1, *(back or at))],
        device_id=to, device_id_type=MESH)


def start_blocks(step, group, copies, keep):
    for j in range(group):
        if j == 0:
            @pl.when(step == 0)
            def _():
                for copy in keep:
                    copy.start()

            @pl.when(step > 0)
            def _():
                for copy in copies(step * group):
                    copy.start()
        else:
            for copy in copies(step * group + j):
                copy.start()


def wait_blocks(n, copies, keep):
    for copy in keep:
        copy.wait()

    @pl.loop(1, n)
    def _(r):
        for copy in copies(r):
            copy.wait()


def in_step(steps, phases, work):
    @pl.loop(0, steps)
    def _(step):
        for i, (copies, _) in enumerate(phases):
            @pl.when(step == i)
            def _(copies=copies):
                for copy in copies():
                    copy.start()

        work(step)

        for i, (copies, then) in enumerate(phases):
            @pl.when(step == i)
            def _(copies=copies, then=then):
                for copy in copies():
                    copy.wait()
                if then is not None:
                    then()


def all_reduce(me, buf, recvs, put, sems_out, sems_in):
    coord = coords(me)
    n_mat, total = buf.shape[0], buf.shape[1]
    levels = len(STRIDES)
    sizes = [total // SIDE ** (level + 1) for level in range(levels)]

    def at(base, size):
        return pl.ds(pl.multiple_of(base, 16), size)

    def base_of(c, level):
        base = 0
        for i in range(level):
            base = base + coord[(c + i) % levels] * sizes[i]
        return base

    def lines(level):
        for c in range(n_mat):
            axis = (c + level) % levels
            for delta in range(1, SIDE):
                to = (coord[axis] + delta) % SIDE
                yield c, delta, to, {"ep": me + (to - coord[axis]) * STRIDES[axis]}

    def scatter(level):
        return [remote(buf.at[c, at(base_of(c, level) + to * sizes[level], sizes[level])], recvs[level].at[c, 3 - delta],
                       sems_out, (level, c, delta - 1), peer, (level, c, 3 - delta))
                for c, delta, to, peer in lines(level)]

    def gather(level):
        out = []
        for c, delta, _, peer in lines(level):
            mine = put(c, at(base_of(c, level + 1), sizes[level]))
            out.append(remote(mine, mine, sems_in, (level, c, delta - 1), peer, (level, c, 3 - delta)))
        return out

    def add(level):
        for c in range(n_mat):
            mine = at(base_of(c, level + 1), sizes[level])
            value = buf[c, mine].astype(f32)
            for i in range(SIDE - 1):
                value = value + recvs[level][c, i].astype(f32)
            if level == levels - 1:
                put(c, mine)[...] = value.astype(buf.dtype)
            else:
                buf[c, mine] = value.astype(buf.dtype)

    return ([(functools.partial(scatter, level), functools.partial(add, level)) for level in range(levels)]
            + [(functools.partial(gather, level), None) for level in reversed(range(levels))])


def route_kernel(capacity, rows, depth, span, local_top, ids_ref, rw_ref, q_ref, pos_ref, msg_ref, top_ref, topw_ref):
    experts, chunk = LANES, 256
    tokens = ids_ref.shape[1]
    n_dest = msg_ref.shape[0]
    before = (iota((chunk, chunk), 0) < iota((chunk, chunk), 1)).astype(bf16)
    expert_id = iota((experts, chunk), 0)
    slot_id = iota((span, chunk), 0)
    half_id = iota((n_dest, chunk), 0) * 2
    seen = jnp.zeros((experts, 1), f32)
    for c in range(tokens // chunk):
        at = slice(c * chunk, (c + 1) * chunk)
        hits = [expert_id == ids_ref[j:j + 1, at] for j in range(2)]
        member = jnp.where(hits[0] | hits[1], 1.0, 0.0)
        earlier = nn(member.astype(bf16), before) + seen
        seen = seen + across(member)
        for j in range(2):
            pos_ref[j:j + 1, at] = down(only(hits[j], earlier)).astype(i32)
    expert_col = iota((experts, 1), 0).astype(f32)
    kept = jnp.minimum(seen, float(capacity))
    if local_top:
        most = jnp.max(seen, axis=0, keepdims=True)
        top = jnp.min(jnp.where(seen == most, expert_col, float(experts)), axis=0, keepdims=True)
        kept = jnp.where(expert_col == top, 0.0, kept)
    else:
        top = jnp.full((1, 1), -1.0, f32)
    top_i = top.astype(i32)
    gates = [jnp.zeros((3 * n_dest, span), f32) for _ in range(2)]
    top_gates = jnp.zeros((24, LANES), f32)
    for c in range(tokens // chunk):
        at = slice(c * chunk, (c + 1) * chunk)
        for j in range(2):
            ids = ids_ref[j:j + 1, at]
            place = pos_ref[j:j + 1, at]
            weight = rw_ref[j:j + 1, at]
            keep = place < capacity
            slot = jnp.where(ids % 2 == 0, place, rows - 1 - place)
            q = (ids // 2) * rows + slot
            if local_top:
                is_top = ids == top_i
                q = jnp.where(is_top, n_dest * rows + place, q)
                slot = jnp.where(is_top, FAR, slot)
                top_hot = hot((iota((LANES, chunk), 0) == place) & keep & is_top)
                top_parts = [jnp.broadcast_to(p, (8, chunk)) for p in split3(weight)]
                top_gates = top_gates + nt(jnp.concatenate(top_parts, axis=0), top_hot)
            q_ref[j:j + 1, at] = jnp.where(keep, q, FAR)
            slot_hot = hot(slot_id == jnp.where(keep, slot, FAR))
            for par in range(2):
                mine = only(half_id + par == ids, weight)
                gates[par] = gates[par] + nt(jnp.concatenate(split3(mine), axis=0), slot_hot)
    kept_wide = jnp.broadcast_to(kept, (experts, LANES)).astype(bf16)
    owner = (iota((n_dest, experts), 1) // 2 == iota((n_dest, experts), 0)).astype(bf16)
    over = jnp.max(jnp.where(nn(owner, kept_wide) > float(rows), 1.0, 0.0), axis=0, keepdims=True)
    over = jnp.maximum(over, jnp.max(jnp.where(kept > float(depth), 1.0, 0.0), axis=0, keepdims=True))
    for par in range(2):
        g = gates[par]
        msg_ref[:, par * span:(par + 1) * span] = g[:n_dest] + g[n_dest:2 * n_dest] + g[2 * n_dest:]
    note = jnp.where(iota((1, LANES), 1) == 1, top, over)
    msg_ref[:, 2 * span:] = jnp.broadcast_to(note, (n_dest, LANES))
    top_ref[...] = jnp.broadcast_to(top_i, (8, LANES))
    topw_ref[...] = top_gates[:8] + top_gates[8:16] + top_gates[16:]


def pack_kernel(q_ref, x_ref, dy_ref, out_ref):
    d, count = x_ref.shape[1], out_ref.shape[0]
    slot = iota((count, 1), 0) + pl.program_id(0) * count
    pick = hot((q_ref[0:1, :] == slot) | (q_ref[1:2, :] == slot))
    out_ref[:, :d] = nn(pick, x_ref[...]).astype(bf16)
    out_ref[:, d:] = nn(pick, dy_ref[...]).astype(bf16)


def swiglu_rows(x, dy, weight, w1, w3, w2):
    h1 = nn(x, w1)
    h3 = nn(x, w3)
    s = jax.nn.sigmoid(h1)
    hidden = (h1 * s * h3).astype(bf16)
    dr = across(dy * nn(hidden, w2))
    g = (weight * dy).astype(bf16)
    da = nt(g, w2)
    dh1 = (da * h3 * s * (1.0 + h1 * (1.0 - s))).astype(bf16)
    dh3 = (da * h1 * s).astype(bf16)
    return hidden, g, dh1, dh3, nt(dh1, w1) + nt(dh3, w3), dr


def expert_body(depth, span, step, xdy_ref, rec_ref, w1_ref, w3_ref, w2_ref, dx_ref, dr_ref, dwg_ref, dwu_ref, dwd_ref):
    group, rows, width = xdy_ref.shape
    n_src = rec_ref.shape[0]
    d = width // 2
    m = group * depth

    local = iota((m, n_src), 0) // depth
    src_hot = hot(local + step * group == iota((m, n_src), 1))
    row_hot = hot(iota((m, LANES), 0) // depth == iota((m, LANES), 1))
    within = iota((m, span), 0) % depth
    outs, dr_slots = [], jnp.zeros((LANES, span), f32)
    for k in range(2):
        first = 0 if k == 0 else rows - depth
        slot_hot = iota((m, span), 1) == within + first
        gate_parts = jnp.concatenate(split3(rec_ref[:, k * span:(k + 1) * span]), axis=1)
        weight = across(only(slot_hot, add3(nn(src_hot, gate_parts), span)))
        x = xdy_ref[:, first:first + depth, :d].reshape(m, d)
        dy = xdy_ref[:, first:first + depth, d:].reshape(m, d).astype(f32)
        hidden, g, dh1, dh3, dx, dr = swiglu_rows(x, dy, weight, w1_ref[k], w3_ref[k], w2_ref[k])
        outs.append(dx.reshape(group, depth, d))
        dwg_ref[k] += tn(x, dh1)
        dwu_ref[k] += tn(x, dh3)
        dwd_ref[k] += tn(hidden, g)
        parts = jnp.concatenate(split3(only(slot_hot & (weight > 0.0), dr)), axis=1)
        dr_slots = dr_slots + add3(tn(row_hot, parts), span)
    low = rows - depth
    dx_ref[:, :low] = outs[0][:, :low].astype(bf16)
    if depth > low:
        dx_ref[:, low:depth] = (outs[0][:, low:] + outs[1][:, :depth - low]).astype(bf16)
    dx_ref[:, depth:] = outs[1][:, depth - low:].astype(bf16)
    for i in range(group):
        dr_ref[i] = dr_slots[i:i + 1]


def gather_weights(part, own, other, full):
    for mine, theirs, whole_ref, by_rows in zip(own, other, full, (True, True, False)):
        size = mine.shape[1] if by_rows else mine.shape[2]
        for ref, at in ((mine, part * size), (theirs, (1 - part) * size)):
            at = pl.ds(pl.multiple_of(at, LANES), size)
            for k in range(2):
                if by_rows:
                    whole_ref[k, at, :] = ref[k]
                else:
                    whole_ref[k, :, at] = ref[k]


def expert_kernel(depth, span, part_ref, xdy_ref, rec_ref, *refs):
    own, other, (dx_ref, dr_ref), dws, full = refs[:3], refs[3:6], refs[6:8], refs[8:11], refs[11:]
    step = pl.program_id(0)

    @pl.when(step == 0)
    def _():
        for ref in dws:
            ref[...] = jnp.zeros_like(ref)
        gather_weights(part_ref[0], own, other, full)

    expert_body(depth, span, step, xdy_ref, rec_ref, *full, dx_ref, dr_ref, *dws)


def expert_send_kernel(depth, span, group, xdy_ref, rec_ref, top_ref, gfull, *refs):
    own, other, back_ref, dr_back, outs = refs[:3], refs[3:6], refs[6], refs[7], refs[8:11]
    full, dws, peers = refs[11:14], refs[14:17], refs[17:20]
    dx_buf, dr_buf, gbuf, gpeer, gr0, gr1, gr2, gout, bsem, dsem, psem, ssem, rsem, own_sem = refs[20:]
    me, part = lax.axis_index("ep"), lax.axis_index("fsdp")
    n = xdy_ref.shape[0]
    meet_all(me, part)
    for ref in dws:
        ref[...] = jnp.zeros_like(ref)
    gather_weights(part, own, other, full)

    def block_copies(r):
        to = peer_at(me, r, -1)
        return [remote(buf.at[r], ref.at[me], sem, (r,), {"ep": to})
                for buf, ref, sem in ((dx_buf, back_ref, bsem), (dr_buf, dr_back, dsem))]

    keep = [pltpu.make_async_copy(buf.at[0], ref.at[me], own_sem.at[i])
            for i, (buf, ref) in enumerate(((dx_buf, back_ref), (dr_buf, dr_back)))]

    def fold_peer():
        gbuf[...] = gfull[part] + gpeer[...]

    phases = [(lambda: [remote(gfull.at[1 - part], gpeer, psem, (3,), {"fsdp": 1 - part})], fold_peer)]
    phases += all_reduce(me, gbuf, (gr0, gr1, gr2), lambda c, s: gout.at[c, s], ssem, rsem)

    def work(step):
        at = pl.ds(step * group, group)
        expert_body(depth, span, step, xdy_ref.at[at], rec_ref, *full, dx_buf.at[at], dr_buf.at[at], *dws)
        start_blocks(step, group, block_copies, keep)

    in_step(n // group, phases, work)

    size = LANES * 2
    here, there = (pl.ds(pl.multiple_of(p * size, LANES), size) for p in (part, 1 - part))
    swaps = [remote(dw.at[:, there, :] if i < 2 else dw.at[:, :, there], peer, psem, (i,), {"fsdp": 1 - part})
             for i, (dw, peer) in enumerate(zip(dws, peers))]
    for copy in swaps:
        copy.start()
    for copy in swaps:
        copy.wait()
    for i, (dw, peer, out) in enumerate(zip(dws, peers, outs)):
        rows, wide = out.shape[1:]
        for k in range(2):
            mine = top_ref[0:1, :] == 2 * me + k
            for b in range(wide // LANES):
                lanes = slice(b * LANES, (b + 1) * LANES)
                if i < 2:
                    total = dw[k, here, lanes]
                else:
                    total = dw[k, :, pl.ds(pl.multiple_of(part * size + b * LANES, LANES), LANES)]
                out[k, :, lanes] = total + peer[k, :, lanes] + only(mine, gout[i, b * rows:(b + 1) * rows, :])
    wait_blocks(n, block_copies, keep)


def dispatch_kernel(group, q_ref, x_ref, dy_ref, msg_ref, gate_ref, top_ref, wg_ref, wu_ref, wd_ref,
                    xdy_ref, rec_ref, dx_ref, dr_ref, gfull,
                    packed, rows_ref, wbuf, wr0, wr1, wr2, wfull, bsem, msem, psem, ssem, rsem, own_sem):
    me, part = lax.axis_index("ep"), lax.axis_index("fsdp")
    n_dest, rows, _ = xdy_ref.shape
    d = x_ref.shape[1]
    meet_all(me, part)

    def pack(slot):
        pick = hot((q_ref[0:1, :] == slot) | (q_ref[1:2, :] == slot))
        return nn(pick, x_ref[...]).astype(bf16), nn(pick, dy_ref[...]).astype(bf16)

    def block_copies(r):
        to = peer_at(me, r, 1)
        return [remote(packed.at[r], xdy_ref.at[r], bsem, (r,), {"ep": to}),
                remote(msg_ref.at[to], rec_ref.at[r], msem, (r,), {"ep": to})]

    keep = [pltpu.make_async_copy(packed.at[0], xdy_ref.at[0], own_sem.at[0]),
            pltpu.make_async_copy(msg_ref.at[me], rec_ref.at[0], own_sem.at[1])]

    def work(step):
        line = iota((group * rows, 1), 0)
        slot = line
        for j in range(group):
            inside = (line >= j * rows) & (line < (j + 1) * rows)
            slot = jnp.where(inside, line - j * rows + peer_at(me, step * group + j, 1) * rows, slot)
        x_rows, dy_rows = pack(slot)
        for j in range(group):
            at = slice(j * rows, (j + 1) * rows)
            packed[step * group + j, :, :d] = x_rows[at]
            packed[step * group + j, :, d:] = dy_rows[at]
        start_blocks(step, group, block_copies, keep)

    def serve_top():
        half, wide = d // 2, d // LANES
        mats = []
        for i in range(2):
            mats.append(jnp.concatenate([jnp.concatenate(
                [wfull[f, i, b * half:(b + 1) * half, :] for b in range(wide)], axis=1) for f in range(2)], axis=0))
        w2 = jnp.concatenate([wfull[f, 2, b * d:(b + 1) * d, :] for f in range(2) for b in range(wide // 2)], axis=1)
        n = rows_ref.shape[0]
        x = rows_ref[:, :d]
        dy = rows_ref[:, d:].astype(f32)
        eye = iota((n, n), 0) == iota((n, n), 1)
        weight = across(only(eye, gate_ref[0:1, :]))
        hidden, g, dh1, dh3, dx, dr = swiglu_rows(x, dy, weight, mats[0], mats[1], w2)
        dx_ref[...] = dx.astype(bf16)
        dr_ref[...] = jnp.broadcast_to(dr, dr_ref.shape)
        for i, dh in enumerate((dh1, dh3)):
            dw = tn(x, dh)
            for f in range(2):
                for b in range(wide):
                    gfull[f, i, b * half:(b + 1) * half, :] = dw[f * half:(f + 1) * half, b * LANES:(b + 1) * LANES]
        dw = tn(hidden, g)
        for f in range(2):
            for b in range(wide // 2):
                lane = f * half + b * LANES
                gfull[f, 2, b * d:(b + 1) * d, :] = dw[:, lane:lane + LANES]

    for i, w in enumerate((wg_ref, wu_ref, wd_ref)):
        n = w.shape[1]
        for b in range(w.shape[2] // LANES):
            lanes = slice(b * LANES, (b + 1) * LANES)
            mine = [only(top_ref[0:1, :] == 2 * me + k, w[k, :, lanes].astype(f32)) for k in range(2)]
            wbuf[i, b * n:(b + 1) * n, :] = (mine[0] + mine[1]).astype(bf16)
    phases = all_reduce(me, wbuf, (wr0, wr1, wr2), lambda c, s: wfull.at[part, c, s], ssem, rsem)
    phases += [(lambda: [remote(wfull.at[part], wfull.at[part], psem, (0,), {"fsdp": 1 - part})], serve_top)]
    x_rows, dy_rows = pack(iota((rows_ref.shape[0], 1), 0) + n_dest * rows)
    rows_ref[:, :d] = x_rows
    rows_ref[:, d:] = dy_rows
    in_step(n_dest // group, phases, work)
    wait_blocks(n_dest, block_copies, keep)


def dr_kernel(rows, span, ids_ref, q_ref, back_ref, *rest):
    top_dr_ref, out_ref = rest if len(rest) == 2 else (None, rest[0])
    n_src = back_ref.shape[0]
    tokens = ids_ref.shape[1]
    chunk = 512
    tables = split3(back_ref[...].T)
    for c in range(tokens // chunk):
        at = slice(c * chunk, (c + 1) * chunk)
        for j in range(2):
            block = ids_ref[j:j + 1, at] // 2
            q = q_ref[j:j + 1, at]
            owner = hot(iota((n_src, chunk), 0) == block)
            column = nn(tables[0], owner) + nn(tables[1], owner) + nn(tables[2], owner)
            far = q >= n_src * rows
            want = jnp.where(far, FAR, q - block * rows)
            picked = down(only(iota((span, chunk), 0) == want, column))
            if top_dr_ref is not None:
                want = jnp.where(far, q - n_src * rows, FAR)
                picked = picked + down(
                    only(iota((LANES, chunk), 0) == want, top_dr_ref[:, 0:1]))
            out_ref[j:j + 1, at] = picked


def combine_kernel(q_ref, back_ref, *rest):
    top_ref, out_ref = rest if len(rest) == 2 else (None, rest[0])
    rows, slots = q_ref.shape[0], back_ref.shape[0]
    q0, q1 = q_ref[:, 0:1], q_ref[:, 1:2]
    acc = jnp.zeros(out_ref.shape, f32)
    for at in range(0, slots, 512):
        depth = min(512, slots - at)
        column = iota((rows, depth), 1) + at
        pick = hot((q0 == column) | (q1 == column))
        acc = acc + nn(pick, back_ref[at:at + depth, :])
    if top_ref is not None:
        column = iota((rows, LANES), 1) + slots
        pick = hot((q0 == column) | (q1 == column))
        acc = acc + nn(pick, top_ref[...])
    out_ref[...] = acc.astype(bf16)


def vmem():
    return pl.BlockSpec(memory_space=pltpu.VMEM)


def whole(shape):
    return pl.BlockSpec(shape, lambda i: (0,) * len(shape))


PARAMS = pltpu.CompilerParams(vmem_limit_bytes=60 * 1024 * 1024)


def exchange(v):
    return lax.all_to_all(v, "ep", 0, 0, tiled=True)


ANYWHERE = pl.BlockSpec(memory_space=pl.ANY)


def reduce_scratch(dtype, total, n_mat=3):
    sizes = [total // SIDE ** (i + 1) for i in range(len(STRIDES))]
    sems = pltpu.SemaphoreType.DMA((2, len(STRIDES), n_mat, SIDE - 1))
    return [pltpu.VMEM((n_mat, SIDE - 1, size, LANES), dtype) for size in sizes], [sems, sems]


def comm_params(index):
    return pltpu.CompilerParams(vmem_limit_bytes=60 * 1024 * 1024, collective_id=index, has_side_effects=True)


def dispatch(q_t, x_tok, dy_tok, msg, gate, top, own, n_dest, rows):
    d, total = x_tok.shape[1], own[0].shape[1] * own[0].shape[2] // LANES
    part, both = (len(own), total, LANES), (2, len(own), total, LANES)
    recvs, sems = reduce_scratch(bf16, total)
    dma = pltpu.SemaphoreType.DMA
    return pl.pallas_call(
        functools.partial(dispatch_kernel, 8),
        out_shape=(jax.ShapeDtypeStruct((n_dest, rows, 2 * d), bf16),
                   jax.ShapeDtypeStruct(msg.shape, f32),
                   jax.ShapeDtypeStruct((LANES, d), bf16),
                   jax.ShapeDtypeStruct((LANES, LANES), f32),
                   jax.ShapeDtypeStruct(both, f32)),
        in_specs=[vmem()] * 9, out_specs=(ANYWHERE,) + (vmem(),) * 4,
        scratch_shapes=[pltpu.VMEM((n_dest, rows, 2 * d), bf16), pltpu.VMEM((LANES, 2 * d), bf16),
                        pltpu.VMEM(part, bf16), *recvs, pltpu.VMEM(both, bf16),
                        dma((2, n_dest)), dma((2, n_dest)), dma((2, 1)), *sems, dma((2,))],
        compiler_params=comm_params(0), name="dispatch",
    )(q_t, x_tok, dy_tok, msg, gate, top, *own)


class Plan:
    def __init__(self, rows, depth, pack_group, group, capacity, n_ep, local_top):
        self.rows, self.depth, self.pack_group, self.group = rows, depth, pack_group, group
        self.capacity, self.n_ep, self.local_top = capacity, n_ep, local_top
        self.span = -(-rows // LANES) * LANES

    def pack(self, q_t, x_tok, dy_tok, group, rows, steps):
        tok_dev, d = x_tok.shape
        return pl.pallas_call(
            pack_kernel,
            out_shape=jax.ShapeDtypeStruct((steps * group * rows, 2 * d), bf16),
            grid=(steps,),
            in_specs=[whole((2, tok_dev)), whole((tok_dev, d)), whole((tok_dev, d))],
            out_specs=pl.BlockSpec((group * rows, 2 * d), lambda i: (i, 0)),
            compiler_params=PARAMS, name="pack",
        )(q_t, x_tok, dy_tok)

    def route(self, ids_t, rw_t):
        n_ep, rows, span, tok_dev = self.n_ep, self.rows, self.span, ids_t.shape[1]
        q_t, _, msg, top, gate = pl.pallas_call(
            functools.partial(route_kernel, self.capacity, rows, self.depth, span, self.local_top),
            out_shape=(jax.ShapeDtypeStruct((2, tok_dev), i32), jax.ShapeDtypeStruct((2, tok_dev), i32),
                       jax.ShapeDtypeStruct((n_ep, 2 * span + LANES), f32),
                       jax.ShapeDtypeStruct((8, LANES), i32), jax.ShapeDtypeStruct((8, LANES), f32)),
            in_specs=[vmem(), vmem()], out_specs=(vmem(),) * 5, compiler_params=PARAMS, name="route",
        )(ids_t, rw_t)
        return q_t, msg, top, gate

    def forward(self, part, x_tok, dy_tok, ids_t, rw_t, weights, own):
        d = x_tok.shape[1]
        n_ep, rows = self.n_ep, self.rows
        q_t, msg, _, _ = self.route(ids_t, rw_t)
        rec = exchange(msg)
        packed = self.pack(q_t, x_tok, dy_tok, self.pack_group, rows, n_ep // self.pack_group)
        xdy = exchange(packed.reshape(n_ep, rows, 2 * d))
        dx, dr, *dws = self.experts(part, xdy, rec, weights, own)
        return q_t, exchange(dx), exchange(dr), dws

    def forward_top(self, x_tok, dy_tok, ids_t, rw_t, weights, own):
        n_ep, rows, span = self.n_ep, self.rows, self.span
        q_t, msg, top, gate = self.route(ids_t, rw_t)
        xdy, rec, top_dx, top_dr, top_grad = dispatch(
            q_t, x_tok, dy_tok, msg.reshape(n_ep, 1, -1), gate, top, own, n_ep, rows)
        rec = rec.reshape(n_ep, -1)
        back, dr, *grads = self.experts_send(xdy, rec, top, top_grad, weights, own)
        return rec[:, 2 * span:], top[0, 0], (q_t, back, dr, (top_dx, top_dr)), grads

    def experts(self, part, xdy, rec, weights, own):
        n_ep, rows, width = xdy.shape
        d, group, span = width // 2, self.group, self.span
        ff = own[0].shape[2]
        return pl.pallas_call(
            functools.partial(expert_kernel, self.depth, span),
            out_shape=(jax.ShapeDtypeStruct((n_ep, rows, d), bf16), jax.ShapeDtypeStruct((n_ep, 1, span), f32),
                       jax.ShapeDtypeStruct((2, d, ff), f32),
                       jax.ShapeDtypeStruct((2, d, ff), f32),
                       jax.ShapeDtypeStruct((2, ff, d), f32)),
            grid=(n_ep // group,),
            in_specs=[pl.BlockSpec(memory_space=pltpu.SMEM), pl.BlockSpec((group, rows, width), lambda i: (i, 0, 0)),
                      whole(rec.shape)] + [whole(w.shape) for w in (*own, *weights)],
            out_specs=(pl.BlockSpec((group, rows, d), lambda i: (i, 0, 0)),
                       pl.BlockSpec((group, 1, span), lambda i: (i, 0, 0)),
                       whole((2, d, ff)), whole((2, d, ff)), whole((2, ff, d))),
            scratch_shapes=[pltpu.VMEM((2, d, ff), bf16), pltpu.VMEM((2, d, ff), bf16), pltpu.VMEM((2, ff, d), bf16)],
            compiler_params=PARAMS, name="experts",
        )(part.reshape(1), xdy, rec, *own, *weights)

    def experts_send(self, xdy, rec, top, top_grad, weights, own):
        n_ep, rows, width = xdy.shape
        d, ff, span = width // 2, own[0].shape[2], self.span
        dma = pltpu.SemaphoreType.DMA
        full = [(2, d, ff), (2, d, ff), (2, ff, d)]
        part = top_grad.shape[1:]
        recvs, sems = reduce_scratch(f32, part[1])
        sum_refs = [pltpu.VMEM(part, f32), pltpu.VMEM(part, f32), *recvs, pltpu.VMEM(part, f32)]
        return pl.pallas_call(
            functools.partial(expert_send_kernel, self.depth, span, self.group),
            out_shape=(jax.ShapeDtypeStruct((n_ep, rows, d), bf16), jax.ShapeDtypeStruct((n_ep, 1, span), f32),
                       *(jax.ShapeDtypeStruct(w.shape, f32) for w in own)),
            in_specs=[vmem()] * 10, out_specs=(ANYWHERE,) + (vmem(),) * 4,
            scratch_shapes=[*(pltpu.VMEM(v, bf16) for v in full), *(pltpu.VMEM(v, f32) for v in full),
                            *(pltpu.VMEM(w.shape, f32) for w in own),
                            pltpu.VMEM((n_ep, rows, d), bf16), pltpu.VMEM((n_ep, 1, span), f32), *sum_refs,
                            dma((2, n_ep)), dma((2, n_ep)), dma((2, 4)), *sems, dma((2,))],
            compiler_params=comm_params(1), name="experts_send",
        )(xdy, rec, top, top_grad, *own, *weights)

    def finish(self, ids_t, q_t, back, dr, top_out):
        tok_dev, (n_ep, rows, d), tile = q_t.shape[1], back.shape, 256
        dr_args = [ids_t, q_t, dr.reshape(n_ep, -1)] + ([top_out[1]] if top_out else [])
        dr_t = pl.pallas_call(
            functools.partial(dr_kernel, self.rows, self.span), out_shape=jax.ShapeDtypeStruct((2, tok_dev), f32),
            in_specs=[vmem()] * len(dr_args), out_specs=vmem(), compiler_params=PARAMS, name="route_grad",
        )(*dr_args)
        args = [q_t.T, back.reshape(n_ep * rows, d)] + ([top_out[0]] if top_out else [])
        grad_x = pl.pallas_call(
            combine_kernel,
            out_shape=jax.ShapeDtypeStruct((tok_dev, d), bf16),
            grid=(tok_dev // tile,),
            in_specs=[pl.BlockSpec((tile, 2), lambda i: (i, 0))] + [whole(v.shape) for v in args[1:]],
            out_specs=pl.BlockSpec((tile, d), lambda i: (i, 0)),
            compiler_params=PARAMS, name="combine",
        )(*args)
        return grad_x, dr_t.T


def solution(mesh):
    n_ep = mesh.shape["ep"]
    tok_spec = P(("fsdp", "ep"), None)
    spec_in = P("ep", "fsdp", None)
    spec_out = P("ep", None, "fsdp")

    def per_device(x_tok, dy_tok, expert_ids, route_w, w_gate, w_up, w_down):
        tok_dev, top_k = expert_ids.shape
        capacity = capacity_of(tok_dev, top_k, w_gate.shape[0] * n_ep)
        part = lax.axis_index("fsdp").astype(i32)
        swap = [(0, 1), (1, 0)]
        own = (w_gate, w_up, w_down)
        weights = [lax.ppermute(w, "fsdp", swap) for w in own]
        ids_t = expert_ids.T
        inputs = (x_tok, dy_tok, ids_t, route_w.T, weights, own)

        def shard_halves(dws):
            out = []
            for dw, axis in zip(dws, (1, 1, 2)):
                size = dw.shape[axis] // 2
                keep = lax.dynamic_slice_in_dim(dw, part * size, size, axis)
                give = lax.dynamic_slice_in_dim(dw, (1 - part) * size, size, axis)
                out.append(keep + lax.ppermute(give, "fsdp", swap))
            return out

        quick = Plan(72, 48, 4, 8, capacity, n_ep, True)
        safe = Plan(2 * capacity, capacity, 2, 4, capacity, n_ep, False)
        notes, top_id, mine, grads = quick.forward_top(*inputs)
        agree = jnp.all(notes[:, 1] == top_id.astype(f32)) & jnp.all(notes[:, 0] == 0.0)
        note = jnp.where(agree, top_id.astype(f32), -1.0).reshape(1, 1)
        other = lax.ppermute(note, "fsdp", swap)
        good = agree & (other == note)[0, 0]

        def fits():
            return (*quick.finish(ids_t, *mine), *grads)

        def general():
            q_all, back_all, dr_all, dws = safe.forward(part, *inputs)
            return (*safe.finish(ids_t, q_all, back_all, dr_all, None), *shard_halves(dws))

        return lax.cond(good, fits, general)

    return jax.shard_map(
        per_device, mesh=mesh,
        in_specs=(tok_spec, tok_spec, tok_spec, tok_spec, spec_in, spec_in, spec_out),
        out_specs=(tok_spec, tok_spec, spec_in, spec_in, spec_out),
        check_vma=False)
```

time: 335 us -> 316 us (0.943); the launches traced: 329 us -> 314 us
  Pallas kernels: 302 us -> 291 us
  other arithmetic: 10.6 us -> 0.71 us
  starting transfers between devices: 1.76 us -> 7.43 us
    pallas_call x3, Pallas kernels: 282 us -> 273 us  [the longest x1 155 us: dispatch(): pl.pallas_call(functools.partial(dispatch_kernel, 8), out_shape=(jax.Shap...]
    unnamed x15 -> x30, local copies, waits for them, and re-layouts: 0.94 us -> 7.04 us
    ppermute x1, starting transfers between devices: 1.09 us -> 6.75 us  [per_device(): other = lax.ppermute(note, 'fsdp', swap)]
    add x2 -> x0, other arithmetic: 5.27 us -> none  [fits(): grads.append(half + only(pick, extra))]
    slice x3 -> x1, local copies, waits for them, and re-layouts: 4.7 us -> 1.2 us  [forward_top(): top[0, 0]]
  transfers between devices with their start and end apart: 4 -> 4, of which waited for: 1 -> 0; matrix products, arithmetic and copies ran while one was open for 2% -> 1% of each run, Pallas kernels for 57% -> 50%
where the time goes in v4:
time: 316 us; the launch traced here: 314 us
  Pallas kernels  291 us (92%)
  local copies, waits for them, and re-layouts  11.2 us (4%)
  starting transfers between devices  7.43 us (2%)
  between operations  3.38 us (1%)
    pallas_call x1, Pallas kernels, dispatch(): pl.pallas_call(functools.partial(dispatch_kernel, 8), out_shape=(jax.Shap...  155 us
    pallas_call x1, Pallas kernels, experts_send(): pl.pallas_call(functools.partial(expert_send_kernel, self.depth, span, se...  117 us
    pallas_call x1, Pallas kernels, finish(): pl.pallas_call(combine_kernel, out_shape=jax.ShapeDtypeStruct((tok_dev, d...  14.6 us
    unnamed x30, local copies, waits for them, and re-layouts  7.04 us
    ppermute x1, starting transfers between devices, per_device(): other = lax.ppermute(note, 'fsdp', swap)  6.75 us
  transfers between devices with their start and end apart: 4, of which 0 were waited for; matrix products, arithmetic and copies ran while one was open for 1% of the time, Pallas kernels for 50%

profile of v4, /device:TPU:32, one launch (start us, length us, event | category | flops | bytes accessed | tf_op | source)
XLA Modules:
  0.0 314.0 jit_solution(13263692939281531563)
XLA Ops:
  0.6 0.1 collective-permute-start.4
  0.7 0.5 collective-permute-start.5
  1.2 0.1 collective-permute-start.6
  1.3 3.6 %route.3 = (s32[2,2048]{1,0:T(2,128)S(1)}, s32[2,2048]{1,0:T(2,128)}, f32[64,384]{1,0:T(8,128)}, s32[8,128]{1,0:T(8,128)}, f32[8,128]{1,0:T(8,128)}) custom-call(s32[2,2048]{1,0:T(2,128)} %bitcast.32, f32[2,2048]{1,0:T(2,128)} %bitcast.37), custom_call_target="tpu_custom_call" | custom-call | tf_op jit(solution)/shard_map/route/pallas_call | solution.py:572
  4.9 1.6 reshape.44.msg_ref
  6.5 1.2 slice.13
  7.7 154.7 %dispatch.1 = (bf16[64,72,1024]{2,1,0:T(8,128)(2,1)}, f32[64,1,384]{2,1,0:T(1,128)}, bf16[128,512]{1,0:T(8,128)(2,1)S(1)}, f32[128,128]{1,0:T(8,128)S(1)}, f32[2,3,1024,128]{3,2,1,0:T(8,128)}) custom-call(s32[2,2048]{1,0:T(2,128)S(1)} %get-tuple-element.86.q_ref, bf16[2048,512]{1,0:T(8,128)(2,1)} %x_ref.1, bf16[2048,512]{1,0:T(8,128)(2,1)} %dy_ref.1, ...), custom_call_target="tpu_custom_call" | custom-call | tf_op jit(solution)/shard_map/dispatch/pallas_call | solution.py:538
  162.5 0.9 copy.38
  164.0 0.7 fusion.1
  166.0 6.8 %collective-permute-start.3 = (f32[1,1]{1,0:T(1,128)}, f32[1,1]{1,0:T(1,128)}, u32[]{:S(2)}, u32[]{:S(2)}) collective-permute-start(f32[1,1]{1,0:T(1,128)} %bitcast.14), channel_id=1, source_target_pairs={{0,64},{64,0},{1,65},{65,1},{2,66},{66,2},{3,67},{67,3},{4,68},{68... | collective-permute-start | bytes 20 | tf_op jit(solution)/shard_map/ppermute | solution.py:689
  173.4 0.0 collective-permute-done.4.refs_3_
  173.4 0.0 collective-permute-done.5.refs_4_
  173.5 0.0 collective-permute-done.6.refs_5_
  173.5 0.0 copy-start.9
  173.5 0.8 copy-done.5
  174.3 0.1 copy-done.7
  174.4 0.2 copy-done.9
  174.6 0.0 copy-start.16
  174.6 0.0 copy-start.18
  174.6 116.8 %experts_send.1 = (bf16[64,72,512]{2,1,0:T(8,128)(2,1)}, f32[64,1,128]{2,1,0:T(1,128)}, f32[2,256,512]{2,1,0:T(8,128)}, f32[2,256,512]{2,1,0:T(8,128)}, f32[2,512,256]{2,1,0:T(8,128)}) custom-call(bf16[64,72,1024]{2,1,0:T(8,128)(2,1)} %get-tuple-element.91.xdy_ref, f32[64,384]{1,0:T(8,128)} %bitcast.30, s32[8,128]{1,0:T(8,128)} %get-tuple-element.89.top_ref, ...), custom_call_target="tpu_custom_call" | custom-call | tf_op jit(solution)/shard_map/experts_send/pallas_call | solution.py:628
  291.4 0.0 copy-done
  291.4 0.0 copy-done.16
  291.5 0.0 copy-done.18
  291.5 17.5 %conditional.1 = (bf16[2048,512]{1,0:T(8,128)(2,1)S(1)}, f32[2048,2]{0,1:T(2,128)S(1)}, f32[2,256,512]{2,1,0:T(8,128)}, f32[2,256,512]{2,1,0:T(8,128)}, f32[2,512,256]{2,1,0:T(8,128)}) conditional(s32[]{:T(128)} %convert_element_type.12, (s32[2,2048]{1,0:T(2,128)S(1)}, f32[2,2048]{1,0:T(2,128)S(1)}, s32[]{:T(128)}, bf16[2048,512]{1,0:T(8,128)(2,1)S(1)}, ...), branch_computations={%region_2.3_spmd, %region_3.4_spmd} | conditional | flops 786441 | bytes 168231488 | solution.py:699
  291.7 1.3 copy.28
  293.1 14.6 %combine.3 = bf16[2048,512]{1,0:T(8,128)(2,1)S(1)} custom-call(s32[2048,2]{1,0:T(8,128)} %bitcast.27, bf16[4608,512]{1,0:T(8,128)(2,1)} %bitcast.26, bf16[128,512]{1,0:T(8,128)(2,1)S(1)} %get-tuple-element.60.rest_0_), custom_call_target="tpu_custom_call" | custom-call | tf_op jit(solution)/shard_map/cond/branch_1_fun/combine/pallas_call | solution.py:648
  307.7 1.3 route_grad.3
  309.0 0.0 copy-start.4
  309.0 0.0 copy-start.20
  309.0 3.1 copy.52
  312.1 1.0 copy.53
  313.1 1.0 copy.54
  (18 shorter events, 0.0 us)
Async XLA Ops:
  0.6 172.8 %collective-permute-start.4 = (bf16[2,256,512]{2,1,0:T(8,128)(2,1)}, bf16[2,256,512]{2,1,0:T(8,128)(2,1)S(1)}, u32[]{:S(2)}, u32[]{:S(2)}) collective-permute-start(bf16[2,256,512]{2,1,0:T(8,128)(2,1)} %refs_0_.1), channel_id=1, source_target_pairs={{0,64},{64,0},{1,65},{65,1},{2,66},{66,2},{3,67},{67,3},{4,68},{68... | collective-permute-start | bytes 1572872 | tf_op jit(solution)/shard_map/ppermute | solution.py:671
  0.7 172.7 %collective-permute-start.5 = (bf16[2,256,512]{2,1,0:T(8,128)(2,1)}, bf16[2,256,512]{2,1,0:T(8,128)(2,1)S(1)}, u32[]{:S(2)}, u32[]{:S(2)}) collective-permute-start(bf16[2,256,512]{2,1,0:T(8,128)(2,1)} %refs_1_.1), channel_id=1, source_target_pairs={{0,64},{64,0},{1,65},{65,1},{2,66},{66,2},{3,67},{67,3},{4,68},{68... | collective-permute-start | bytes 1572872 | tf_op jit(solution)/shard_map/ppermute | solution.py:671
  1.2 172.2 %collective-permute-start.6 = (bf16[2,512,256]{2,1,0:T(8,128)(2,1)}, bf16[2,512,256]{2,1,0:T(8,128)(2,1)S(1)}, u32[]{:S(2)}, u32[]{:S(2)}) collective-permute-start(bf16[2,512,256]{2,1,0:T(8,128)(2,1)} %refs_2_.1), channel_id=1, source_target_pairs={{0,64},{64,0},{1,65},{65,1},{2,66},{66,2},{3,67},{67,3},{4,68},{68... | collective-permute-start | bytes 1572872 | tf_op jit(solution)/shard_map/ppermute | solution.py:671
  7.7 166.8 %copy-start.1 = (bf16[2,256,512]{2,1,0:T(8,128)(2,1)S(1)}, bf16[2,256,512]{2,1,0:T(8,128)(2,1)}, u32[]{:S(2)}) copy-start(bf16[2,256,512]{2,1,0:T(8,128)(2,1)} %refs_0_.1) | copy-start | bytes 1572868
  7.7 166.8 %copy-start.2 = (bf16[2,256,512]{2,1,0:T(8,128)(2,1)S(1)}, bf16[2,256,512]{2,1,0:T(8,128)(2,1)}, u32[]{:S(2)}) copy-start(bf16[2,256,512]{2,1,0:T(8,128)(2,1)} %refs_1_.1) | copy-start | bytes 1572868
  163.4 11.2 %copy-start.15 = (f32[64,1,384]{2,0,1:T(8,128)}, f32[64,1,384]{2,0,1:T(8,128)S(1)}, u32[]{:S(2)}) copy-start(f32[64,1,384]{2,0,1:T(8,128)S(1)} %copy.38) | copy-start | bytes 294916
  166.0 6.8 %collective-permute-start.3 = (f32[1,1]{1,0:T(1,128)}, f32[1,1]{1,0:T(1,128)}, u32[]{:S(2)}, u32[]{:S(2)}) collective-permute-start(f32[1,1]{1,0:T(1,128)} %bitcast.14), channel_id=1, source_target_pairs={{0,64},{64,0},{1,65},{65,1},{2,66},{66,2},{3,67},{67,3},{4,68},{68... | collective-permute-start | bytes 20 | tf_op jit(solution)/shard_map/ppermute | solution.py:689
  173.4 0.8 copy-start.5
  173.4 0.9 copy-start.7
  173.5 1.1 copy-start.9
  174.6 116.9 %copy-start = (bf16[2048,512]{1,0:T(8,128)(2,1)S(1)}, bf16[2048,512]{1,0:T(8,128)(2,1)}, u32[]{:S(2)}) copy-start(bf16[2048,512]{1,0:T(8,128)(2,1)} %x_ref.1) | copy-start | bytes 6291460
  174.6 116.9 %copy-start.16 = (s32[2048,2]{0,1:T(2,128)S(1)}, s32[2048,2]{0,1:T(2,128)}, u32[]{:S(2)}) copy-start(s32[2048,2]{0,1:T(2,128)} %param.11) | copy-start | bytes 49156
  174.6 116.9 %copy-start.18 = (f32[2048,2]{0,1:T(2,128)S(1)}, f32[2048,2]{0,1:T(2,128)}, u32[]{:S(2)}) copy-start(f32[2048,2]{0,1:T(2,128)} %param.12) | copy-start | bytes 49156
  293.1 14.6 %copy-start.19 = (f32[64,1,128]{2,1,0:T(1,128)S(1)}, f32[64,1,128]{2,1,0:T(1,128)}, u32[]{:S(2)}) copy-start(f32[64,1,128]{2,1,0:T(1,128)} %get-tuple-element.117) | copy-start | bytes 98308 | tf_op jit(solution)/shard_map/cond
  309.0 4.1 %copy-start.4 = (bf16[2048,512]{1,0:T(8,128)(2,1)}, bf16[2048,512]{1,0:T(8,128)(2,1)S(1)}, u32[]{:S(2)}) copy-start(bf16[2048,512]{1,0:T(8,128)(2,1)S(1)} %get-tuple-element.140) | copy-start | bytes 6291460
  309.0 4.1 %copy-start.20 = (f32[2048,2]{0,1:T(2,128)}, f32[2048,2]{0,1:T(2,128)S(1)}, u32[]{:S(2)}) copy-start(f32[2048,2]{0,1:T(2,128)S(1)} %get-tuple-element.141) | copy-start | bytes 49156
  309.0 3.1 copy-start.13
  309.0 4.0 %copy-start.14 = (f32[2,512,256]{2,1,0:T(8,128)S(1)}, f32[2,512,256]{2,1,0:T(8,128)}, u32[]{:S(2)}) copy-start(f32[2,512,256]{2,1,0:T(8,128)} %get-tuple-element.144) | copy-start | bytes 3145732

commit v5 on v4

--- a/solution.py
+++ b/solution.py
@@ -11,6 +11,7 @@
 LANES = 128
 FAR = 1 << 20
 MESH = pl.DeviceIdType.MESH
+LAG = 2
 f32, bf16, i32 = jnp.float32, jnp.bfloat16, jnp.int32
 
 
@@ -73,7 +74,7 @@
 def peer_at(me, r, sign):
     o = (r * 23) % SIDE ** 3
     out = 0
-    for here, off, stride in zip(coords(me), coords(o), STRIDES):
+    for here, off, stride in zip(coords(me), coords(o)[::-1], STRIDES):
         out = out + ((here + sign * off + SIDE) % SIDE) * stride
     return out
 
@@ -124,7 +125,7 @@
 
 
 def in_step(steps, phases, work):
-    @pl.loop(0, steps)
+    @pl.loop(0, max(steps, len(phases)))
     def _(step):
         for i, (copies, _) in enumerate(phases):
             @pl.when(step == i)
@@ -132,7 +133,9 @@
                 for copy in copies():
                     copy.start()
 
-        work(step)
+        @pl.when(step < steps)
+        def _():
+            work(step)
 
         for i, (copies, then) in enumerate(phases):
             @pl.when(step == i)
@@ -247,9 +250,9 @@
     over = jnp.maximum(over, jnp.max(jnp.where(kept > float(depth), 1.0, 0.0), axis=0, keepdims=True))
     for par in range(2):
         g = gates[par]
-        msg_ref[:, par * span:(par + 1) * span] = g[:n_dest] + g[n_dest:2 * n_dest] + g[2 * n_dest:]
+        msg_ref[:, 0, par * span:(par + 1) * span] = g[:n_dest] + g[n_dest:2 * n_dest] + g[2 * n_dest:]
     note = jnp.where(iota((1, LANES), 1) == 1, top, over)
-    msg_ref[:, 2 * span:] = jnp.broadcast_to(note, (n_dest, LANES))
+    msg_ref[:, 0, 2 * span:] = jnp.broadcast_to(note, (n_dest, LANES))
     top_ref[...] = jnp.broadcast_to(top_i, (8, LANES))
     topw_ref[...] = top_gates[:8] + top_gates[8:16] + top_gates[16:]
 
@@ -334,10 +337,10 @@
     expert_body(depth, span, step, xdy_ref, rec_ref, *full, dx_ref, dr_ref, *dws)
 
 
-def expert_send_kernel(depth, span, group, xdy_ref, rec_ref, top_ref, gfull, *refs):
-    own, other, back_ref, dr_back, outs = refs[:3], refs[3:6], refs[6], refs[7], refs[8:11]
+def expert_send_kernel(depth, span, group, q_ref, top_dx_ref, xdy_ref, rec_ref, top_ref, gfull, *refs):
+    own, other, gx_ref, dr_back, outs = refs[:3], refs[3:6], refs[6], refs[7], refs[8:11]
     full, dws, peers = refs[11:14], refs[14:17], refs[17:20]
-    dx_buf, dr_buf, gbuf, gpeer, gr0, gr1, gr2, gout, bsem, dsem, psem, ssem, rsem, own_sem = refs[20:]
+    back_ref, acc_ref, dx_buf, dr_buf, gbuf, gpeer, gr0, gr1, gr2, gout, bsem, dsem, psem, ssem, rsem, own_sem = refs[20:]
     me, part = lax.axis_index("ep"), lax.axis_index("fsdp")
     n = xdy_ref.shape[0]
     meet_all(me, part)
@@ -347,22 +350,65 @@
 
     def block_copies(r):
         to = peer_at(me, r, -1)
-        return [remote(buf.at[r], ref.at[me], sem, (r,), {"ep": to})
-                for buf, ref, sem in ((dx_buf, back_ref, bsem), (dr_buf, dr_back, dsem))]
-
-    keep = [pltpu.make_async_copy(buf.at[0], ref.at[me], own_sem.at[i])
-            for i, (buf, ref) in enumerate(((dx_buf, back_ref), (dr_buf, dr_back)))]
+        return [remote(dx_buf.at[r], back_ref.at[r], bsem, (r,), {"ep": to}),
+                remote(dr_buf.at[r], dr_back.at[me], dsem, (r,), {"ep": to})]
+
+    keep = [pltpu.make_async_copy(dx_buf.at[0], back_ref.at[0], own_sem.at[0]),
+            pltpu.make_async_copy(dr_buf.at[0], dr_back.at[me], own_sem.at[1])]
 
     def fold_peer():
         gbuf[...] = gfull[part] + gpeer[...]
 
     phases = [(lambda: [remote(gfull.at[1 - part], gpeer, psem, (3,), {"fsdp": 1 - part})], fold_peer)]
     phases += all_reduce(me, gbuf, (gr0, gr1, gr2), lambda c, s: gout.at[c, s], ssem, rsem)
+
+    rows, tile = xdy_ref.shape[1], LANES * 2
+
+    def combine(slot, block, fresh):
+        @pl.loop(0, gx_ref.shape[0] // tile)
+        def _(i):
+            at = pl.ds(pl.multiple_of(i * tile, tile), tile)
+            q = q_ref[at, :]
+            value = nn(hot((q[:, 0:1] == slot) | (q[:, 1:2] == slot)), block)
+            acc_ref[at, :] = value if fresh else acc_ref[at, :] + value
+
+    def take(step):
+        for j in range(group):
+            r = step * group + j
+            if j > 0:
+                copies = block_copies(r)
+                for copy in copies:
+                    copy.wait()
+            else:
+                @pl.when(step == 0)
+                def _():
+                    for copy in keep:
+                        copy.wait()
+
+                @pl.when(step > 0)
+                def _(r=r):
+                    for copy in block_copies(r):
+                        copy.wait()
+        line = iota((1, group * rows), 1)
+        slot = line
+        for j in range(group):
+            inside = (line >= j * rows) & (line < (j + 1) * rows)
+            slot = jnp.where(inside, line - j * rows + peer_at(me, step * group + j, 1) * rows, slot)
+        block = jnp.concatenate([back_ref[step * group + j].astype(f32) for j in range(group)], axis=0)
+        combine(slot, block.astype(bf16), False)
 
     def work(step):
         at = pl.ds(step * group, group)
         expert_body(depth, span, step, xdy_ref.at[at], rec_ref, *full, dx_buf.at[at], dr_buf.at[at], *dws)
         start_blocks(step, group, block_copies, keep)
+
+        @pl.when(step == 0)
+        def _():
+            combine(iota((1, LANES), 1) + n * rows, top_dx_ref[...], True)
+
+        @pl.when(step >= LAG)
+        def _():
+            take(step - LAG)
 
     in_step(n // group, phases, work)
 
@@ -372,6 +418,9 @@
              for i, (dw, peer) in enumerate(zip(dws, peers))]
     for copy in swaps:
         copy.start()
+    for step in range(n // group - LAG, n // group):
+        take(step)
+    gx_ref[...] = acc_ref[...].astype(bf16)
     for copy in swaps:
         copy.wait()
     for i, (dw, peer, out) in enumerate(zip(dws, peers, outs)):
@@ -385,12 +434,11 @@
                 else:
                     total = dw[k, :, pl.ds(pl.multiple_of(part * size + b * LANES, LANES), LANES)]
                 out[k, :, lanes] = total + peer[k, :, lanes] + only(mine, gout[i, b * rows:(b + 1) * rows, :])
-    wait_blocks(n, block_copies, keep)
 
 
 def dispatch_kernel(group, q_ref, x_ref, dy_ref, msg_ref, gate_ref, top_ref, wg_ref, wu_ref, wd_ref,
                     xdy_ref, rec_ref, dx_ref, dr_ref, gfull,
-                    packed, rows_ref, wbuf, wr0, wr1, wr2, wfull, bsem, msem, psem, ssem, rsem, own_sem):
+                    packed, wbuf, wr0, wr1, wr2, wfull, bsem, msem, psem, ssem, rsem, own_sem):
     me, part = lax.axis_index("ep"), lax.axis_index("fsdp")
     n_dest, rows, _ = xdy_ref.shape
     d = x_ref.shape[1]
@@ -428,9 +476,9 @@
             mats.append(jnp.concatenate([jnp.concatenate(
                 [wfull[f, i, b * half:(b + 1) * half, :] for b in range(wide)], axis=1) for f in range(2)], axis=0))
         w2 = jnp.concatenate([wfull[f, 2, b * d:(b + 1) * d, :] for f in range(2) for b in range(wide // 2)], axis=1)
-        n = rows_ref.shape[0]
-        x = rows_ref[:, :d]
-        dy = rows_ref[:, d:].astype(f32)
+        n = dx_ref.shape[0]
+        x, dy = pack(iota((n, 1), 0) + n_dest * rows)
+        dy = dy.astype(f32)
         eye = iota((n, n), 0) == iota((n, n), 1)
         weight = across(only(eye, gate_ref[0:1, :]))
         hidden, g, dh1, dh3, dx, dr = swiglu_rows(x, dy, weight, mats[0], mats[1], w2)
@@ -455,9 +503,6 @@
             wbuf[i, b * n:(b + 1) * n, :] = (mine[0] + mine[1]).astype(bf16)
     phases = all_reduce(me, wbuf, (wr0, wr1, wr2), lambda c, s: wfull.at[part, c, s], ssem, rsem)
     phases += [(lambda: [remote(wfull.at[part], wfull.at[part], psem, (0,), {"fsdp": 1 - part})], serve_top)]
-    x_rows, dy_rows = pack(iota((rows_ref.shape[0], 1), 0) + n_dest * rows)
-    rows_ref[:, :d] = x_rows
-    rows_ref[:, d:] = dy_rows
     in_step(n_dest // group, phases, work)
     wait_blocks(n_dest, block_copies, keep)
 
@@ -485,21 +530,17 @@
             out_ref[j:j + 1, at] = picked
 
 
-def combine_kernel(q_ref, back_ref, *rest):
-    top_ref, out_ref = rest if len(rest) == 2 else (None, rest[0])
+def combine_kernel(q_ref, back_ref, out_ref):
     rows, slots = q_ref.shape[0], back_ref.shape[0]
     q0, q1 = q_ref[:, 0:1], q_ref[:, 1:2]
-    acc = jnp.zeros(out_ref.shape, f32)
-    for at in range(0, slots, 512):
-        depth = min(512, slots - at)
+    depth = 512
+
+    def body(i, acc):
+        at = i * depth
         column = iota((rows, depth), 1) + at
-        pick = hot((q0 == column) | (q1 == column))
-        acc = acc + nn(pick, back_ref[at:at + depth, :])
-    if top_ref is not None:
-        column = iota((rows, LANES), 1) + slots
-        pick = hot((q0 == column) | (q1 == column))
-        acc = acc + nn(pick, top_ref[...])
-    out_ref[...] = acc.astype(bf16)
+        return acc + nn(hot((q0 == column) | (q1 == column)), back_ref[pl.ds(pl.multiple_of(at, depth), depth), :])
+
+    out_ref[...] = lax.fori_loop(0, slots // depth, body, jnp.zeros(out_ref.shape, f32)).astype(bf16)
 
 
 def vmem():
@@ -527,7 +568,7 @@
 
 
 def comm_params(index):
-    return pltpu.CompilerParams(vmem_limit_bytes=60 * 1024 * 1024, collective_id=index, has_side_effects=True)
+    return pltpu.CompilerParams(vmem_limit_bytes=63 * 1024 * 1024, collective_id=index, has_side_effects=True)
 
 
 def dispatch(q_t, x_tok, dy_tok, msg, gate, top, own, n_dest, rows):
@@ -543,7 +584,7 @@
                    jax.ShapeDtypeStruct((LANES, LANES), f32),
                    jax.ShapeDtypeStruct(both, f32)),
         in_specs=[vmem()] * 9, out_specs=(ANYWHERE,) + (vmem(),) * 4,
-        scratch_shapes=[pltpu.VMEM((n_dest, rows, 2 * d), bf16), pltpu.VMEM((LANES, 2 * d), bf16),
+        scratch_shapes=[pltpu.VMEM((n_dest, rows, 2 * d), bf16),
                         pltpu.VMEM(part, bf16), *recvs, pltpu.VMEM(both, bf16),
                         dma((2, n_dest)), dma((2, n_dest)), dma((2, 1)), *sems, dma((2,))],
         compiler_params=comm_params(0), name="dispatch",
@@ -572,7 +613,7 @@
         q_t, _, msg, top, gate = pl.pallas_call(
             functools.partial(route_kernel, self.capacity, rows, self.depth, span, self.local_top),
             out_shape=(jax.ShapeDtypeStruct((2, tok_dev), i32), jax.ShapeDtypeStruct((2, tok_dev), i32),
-                       jax.ShapeDtypeStruct((n_ep, 2 * span + LANES), f32),
+                       jax.ShapeDtypeStruct((n_ep, 1, 2 * span + LANES), f32),
                        jax.ShapeDtypeStruct((8, LANES), i32), jax.ShapeDtypeStruct((8, LANES), f32)),
             in_specs=[vmem(), vmem()], out_specs=(vmem(),) * 5, compiler_params=PARAMS, name="route",
         )(ids_t, rw_t)
@@ -582,7 +623,7 @@
         d = x_tok.shape[1]
         n_ep, rows = self.n_ep, self.rows
         q_t, msg, _, _ = self.route(ids_t, rw_t)
-        rec = exchange(msg)
+        rec = exchange(msg).reshape(n_ep, -1)
         packed = self.pack(q_t, x_tok, dy_tok, self.pack_group, rows, n_ep // self.pack_group)
         xdy = exchange(packed.reshape(n_ep, rows, 2 * d))
         dx, dr, *dws = self.experts(part, xdy, rec, weights, own)
@@ -592,10 +633,10 @@
         n_ep, rows, span = self.n_ep, self.rows, self.span
         q_t, msg, top, gate = self.route(ids_t, rw_t)
         xdy, rec, top_dx, top_dr, top_grad = dispatch(
-            q_t, x_tok, dy_tok, msg.reshape(n_ep, 1, -1), gate, top, own, n_ep, rows)
+            q_t, x_tok, dy_tok, msg, gate, top, own, n_ep, rows)
         rec = rec.reshape(n_ep, -1)
-        back, dr, *grads = self.experts_send(xdy, rec, top, top_grad, weights, own)
-        return rec[:, 2 * span:], top[0, 0], (q_t, back, dr, (top_dx, top_dr)), grads
+        grad_x, dr, *grads = self.experts_send(q_t, top_dx, xdy, rec, top, top_grad, weights, own)
+        return rec[:, 2 * span:], top[0, 0], (q_t, dr, top_dr), grad_x, grads
 
     def experts(self, part, xdy, rec, weights, own):
         n_ep, rows, width = xdy.shape
@@ -617,7 +658,7 @@
             compiler_params=PARAMS, name="experts",
         )(part.reshape(1), xdy, rec, *own, *weights)
 
-    def experts_send(self, xdy, rec, top, top_grad, weights, own):
+    def experts_send(self, q_t, top_dx, xdy, rec, top, top_grad, weights, own):
         n_ep, rows, width = xdy.shape
         d, ff, span = width // 2, own[0].shape[2], self.span
         dma = pltpu.SemaphoreType.DMA
@@ -627,33 +668,33 @@
         sum_refs = [pltpu.VMEM(part, f32), pltpu.VMEM(part, f32), *recvs, pltpu.VMEM(part, f32)]
         return pl.pallas_call(
             functools.partial(expert_send_kernel, self.depth, span, self.group),
-            out_shape=(jax.ShapeDtypeStruct((n_ep, rows, d), bf16), jax.ShapeDtypeStruct((n_ep, 1, span), f32),
+            out_shape=(jax.ShapeDtypeStruct((q_t.shape[1], d), bf16), jax.ShapeDtypeStruct((n_ep, 1, span), f32),
                        *(jax.ShapeDtypeStruct(w.shape, f32) for w in own)),
-            in_specs=[vmem()] * 10, out_specs=(ANYWHERE,) + (vmem(),) * 4,
+            in_specs=[vmem()] * 12, out_specs=(vmem(),) * 5,
             scratch_shapes=[*(pltpu.VMEM(v, bf16) for v in full), *(pltpu.VMEM(v, f32) for v in full),
                             *(pltpu.VMEM(w.shape, f32) for w in own),
+                            pltpu.VMEM((n_ep, rows, d), bf16), pltpu.VMEM((q_t.shape[1], d), f32),
                             pltpu.VMEM((n_ep, rows, d), bf16), pltpu.VMEM((n_ep, 1, span), f32), *sum_refs,
                             dma((2, n_ep)), dma((2, n_ep)), dma((2, 4)), *sems, dma((2,))],
             compiler_params=comm_params(1), name="experts_send",
-        )(xdy, rec, top, top_grad, *own, *weights)
-
-    def finish(self, ids_t, q_t, back, dr, top_out):
+        )(q_t.T, top_dx, xdy, rec, top, top_grad, *own, *weights)
+
+    def route_grad(self, ids_t, q_t, dr, *top_dr):
+        return pl.pallas_call(
+            functools.partial(dr_kernel, self.rows, self.span), out_shape=jax.ShapeDtypeStruct(q_t.shape, f32),
+            in_specs=[vmem()] * (3 + len(top_dr)), out_specs=vmem(), compiler_params=PARAMS, name="route_grad",
+        )(ids_t, q_t, dr.reshape(self.n_ep, -1), *top_dr).T
+
+    def combine(self, q_t, back):
         tok_dev, (n_ep, rows, d), tile = q_t.shape[1], back.shape, 256
-        dr_args = [ids_t, q_t, dr.reshape(n_ep, -1)] + ([top_out[1]] if top_out else [])
-        dr_t = pl.pallas_call(
-            functools.partial(dr_kernel, self.rows, self.span), out_shape=jax.ShapeDtypeStruct((2, tok_dev), f32),
-            in_specs=[vmem()] * len(dr_args), out_specs=vmem(), compiler_params=PARAMS, name="route_grad",
-        )(*dr_args)
-        args = [q_t.T, back.reshape(n_ep * rows, d)] + ([top_out[0]] if top_out else [])
-        grad_x = pl.pallas_call(
+        return pl.pallas_call(
             combine_kernel,
             out_shape=jax.ShapeDtypeStruct((tok_dev, d), bf16),
             grid=(tok_dev // tile,),
-            in_specs=[pl.BlockSpec((tile, 2), lambda i: (i, 0))] + [whole(v.shape) for v in args[1:]],
+            in_specs=[pl.BlockSpec((tile, 2), lambda i: (i, 0)), whole((n_ep * rows, d))],
             out_specs=pl.BlockSpec((tile, d), lambda i: (i, 0)),
             compiler_params=PARAMS, name="combine",
-        )(*args)
-        return grad_x, dr_t.T
+        )(q_t.T, back.reshape(n_ep * rows, d))
 
 
 def solution(mesh):
@@ -682,19 +723,19 @@
             return out
 
         quick = Plan(72, 48, 4, 8, capacity, n_ep, True)
-        safe = Plan(2 * capacity, capacity, 2, 4, capacity, n_ep, False)
-        notes, top_id, mine, grads = quick.forward_top(*inputs)
+        safe = Plan(2 * capacity, capacity, 1, 1, capacity, n_ep, False)
+        notes, top_id, mine, grad_x, grads = quick.forward_top(*inputs)
         agree = jnp.all(notes[:, 1] == top_id.astype(f32)) & jnp.all(notes[:, 0] == 0.0)
         note = jnp.where(agree, top_id.astype(f32), -1.0).reshape(1, 1)
         other = lax.ppermute(note, "fsdp", swap)
         good = agree & (other == note)[0, 0]
 
         def fits():
-            return (*quick.finish(ids_t, *mine), *grads)
+            return (grad_x, quick.route_grad(ids_t, *mine), *grads)
 
         def general():
             q_all, back_all, dr_all, dws = safe.forward(part, *inputs)
-            return (*safe.finish(ids_t, q_all, back_all, dr_all, None), *shard_halves(dws))
+            return (safe.combine(q_all, back_all), safe.route_grad(ids_t, q_all, dr_all), *shard_halves(dws))
 
         return lax.cond(good, fits, general)
 

time: 316 us -> 312 us (0.987)
  starting transfers between devices: 7.43 us -> 2.91 us
    pallas_call x2 -> x1, Pallas kernels: 15.9 us -> 1.26 us  [route_grad(): pl.pallas_call(functools.partial(dr_kernel, self.rows, self.span), out_sh...]
    pallas_call x1, Pallas kernels: 155 us -> 165 us  [dispatch(): pl.pallas_call(functools.partial(dispatch_kernel, 8), out_shape=(jax.Shap...]
    pallas_call x1, Pallas kernels: 117 us -> 124 us  [experts_send(): pl.pallas_call(functools.partial(expert_send_kernel, self.depth, span, se...]
    ppermute x1, starting transfers between devices: 6.75 us -> 2.23 us  [per_device(): other = lax.ppermute(note, 'fsdp', swap)]
    unnamed x30 -> x21, local copies, waits for them, and re-layouts: 7.04 us -> 7.6 us
  transfers between devices with their start and end apart: 4 -> 4, of which waited for: 0 -> 0; matrix products, arithmetic and copies ran while one was open for 1% -> 1% of each run, Pallas kernels for 50% -> 54%
where the time goes in v5:
time: 312 us; the launch traced here: 311 us
  Pallas kernels  293 us (94%)
  local copies, waits for them, and re-layouts  10.1 us (3%)
  between operations  3.35 us (1%)
    pallas_call x1, Pallas kernels, dispatch(): pl.pallas_call(functools.partial(dispatch_kernel, 8), out_shape=(jax.Shap...  165 us
    pallas_call x1, Pallas kernels, experts_send(): pl.pallas_call(functools.partial(expert_send_kernel, self.depth, span, se...  124 us
    unnamed x21, local copies, waits for them, and re-layouts  7.6 us
  transfers between devices with their start and end apart: 4, of which 0 were waited for; matrix products, arithmetic and copies ran while one was open for 1% of the time, Pallas kernels for 54%

profile of v5, /device:TPU:32, one launch (start us, length us, event | category | flops | bytes accessed | tf_op | source)
XLA Modules:
  0.0 310.6 jit_solution(859441871929700279)
XLA Ops:
  0.6 0.1 collective-permute-start.4
  0.7 0.5 collective-permute-start.5
  1.2 0.1 collective-permute-start.6
  1.3 3.7 %route.3 = (s32[2,2048]{1,0:T(2,128)S(1)}, s32[2,2048]{1,0:T(2,128)}, f32[64,1,384]{2,1,0:T(1,128)}, s32[8,128]{1,0:T(8,128)}, f32[8,128]{1,0:T(8,128)}) custom-call(s32[2,2048]{1,0:T(2,128)} %bitcast.29, f32[2,2048]{1,0:T(2,128)} %bitcast.33), custom_call_target="tpu_custom_call" | custom-call | tf_op jit(solution)/shard_map/route/pallas_call | solution.py:613
  5.0 1.2 slice.13
  6.2 164.7 %dispatch.1 = (bf16[64,72,1024]{2,1,0:T(8,128)(2,1)}, f32[64,1,384]{2,1,0:T(1,128)}, bf16[128,512]{1,0:T(8,128)(2,1)}, f32[128,128]{1,0:T(8,128)S(1)}, f32[2,3,1024,128]{3,2,1,0:T(8,128)}) custom-call(s32[2,2048]{1,0:T(2,128)S(1)} %get-tuple-element.83.q_ref, bf16[2048,512]{1,0:T(8,128)(2,1)} %x_ref.1, bf16[2048,512]{1,0:T(8,128)(2,1)} %dy_ref.1, ...), custom_call_target="tpu_custom_call" | custom-call | tf_op jit(solution)/shard_map/dispatch/pallas_call | solution.py:579
  170.9 0.9 copy.38
  172.5 0.7 fusion.1
  174.5 2.2 collective-permute-start.3
  176.7 1.3 copy.28
  178.7 0.0 collective-permute-done.4.refs_3_
  178.7 0.0 collective-permute-done.5.refs_4_
  178.7 0.0 collective-permute-done.6.refs_5_
  178.7 0.0 copy-done.8
  178.8 0.0 copy-done
  178.8 0.0 copy-start.9
  178.8 0.0 copy-start.11
  178.8 123.8 %experts_send.1 = (bf16[2048,512]{1,0:T(8,128)(2,1)}, f32[64,1,128]{2,1,0:T(1,128)S(1)}, f32[2,256,512]{2,1,0:T(8,128)}, f32[2,256,512]{2,1,0:T(8,128)}, f32[2,512,256]{2,1,0:T(8,128)}) custom-call(s32[2048,2]{1,0:T(8,128)} %bitcast.24, bf16[128,512]{1,0:T(8,128)(2,1)} %get-tuple-element.88.top_dx_ref, bf16[64,72,1024]{2,1,0:T(8,128)(2,1)} %get-tuple-element.89.xdy_ref, ...), custom_call_target="tpu_custom_call" | custom-call | tf_op jit(solution)/shard_map/experts_send/pallas_call | solution.py:669
  302.6 0.0 copy-done.9
  302.6 0.0 copy-done.11
  302.6 1.3 conditional.1
  302.6 1.3 route_grad.3
  303.9 0.0 copy-start.12
  303.9 0.0 copy-start.5
  303.9 3.1 %copy.53 = bf16[2048,512]{1,0:T(8,128)(2,1)} copy(bf16[2048,512]{1,0:T(8,128)(2,1)} %get-tuple-element.135) | data formatting | bytes 4194304
  307.0 0.0 copy-done.12
  307.0 0.0 copy-done.5
  307.1 1.0 copy.54
  308.0 0.6 copy-done.6
  308.6 1.0 copy.55
  309.6 0.0 copy-done.7
  309.6 1.0 copy.56
  (5 shorter events, 0.0 us)
Async XLA Ops:
  0.6 178.1 %collective-permute-start.4 = (bf16[2,256,512]{2,1,0:T(8,128)(2,1)}, bf16[2,256,512]{2,1,0:T(8,128)(2,1)}, u32[]{:S(2)}, u32[]{:S(2)}) collective-permute-start(bf16[2,256,512]{2,1,0:T(8,128)(2,1)} %refs_0_.1), channel_id=1, source_target_pairs={{0,64},{64,0},{1,65},{65,1},{2,66},{66,2},{3,67},{67,3},{4,68},{68... | collective-permute-start | bytes 1572872 | tf_op jit(solution)/shard_map/ppermute | solution.py:712
  0.7 178.0 %collective-permute-start.5 = (bf16[2,256,512]{2,1,0:T(8,128)(2,1)}, bf16[2,256,512]{2,1,0:T(8,128)(2,1)}, u32[]{:S(2)}, u32[]{:S(2)}) collective-permute-start(bf16[2,256,512]{2,1,0:T(8,128)(2,1)} %refs_1_.1), channel_id=1, source_target_pairs={{0,64},{64,0},{1,65},{65,1},{2,66},{66,2},{3,67},{67,3},{4,68},{68... | collective-permute-start | bytes 1572872 | tf_op jit(solution)/shard_map/ppermute | solution.py:712
  1.2 177.5 %collective-permute-start.6 = (bf16[2,512,256]{2,1,0:T(8,128)(2,1)}, bf16[2,512,256]{2,1,0:T(8,128)(2,1)}, u32[]{:S(2)}, u32[]{:S(2)}) collective-permute-start(bf16[2,512,256]{2,1,0:T(8,128)(2,1)} %refs_2_.1), channel_id=1, source_target_pairs={{0,64},{64,0},{1,65},{65,1},{2,66},{66,2},{3,67},{67,3},{4,68},{68... | collective-permute-start | bytes 1572872 | tf_op jit(solution)/shard_map/ppermute | solution.py:712
  6.2 172.6 %copy-start = (bf16[2,256,512]{2,1,0:T(8,128)(2,1)S(1)}, bf16[2,256,512]{2,1,0:T(8,128)(2,1)}, u32[]{:S(2)}) copy-start(bf16[2,256,512]{2,1,0:T(8,128)(2,1)} %refs_0_.1) | copy-start | bytes 1572868
  171.8 6.9 %copy-start.8 = (f32[64,1,384]{2,0,1:T(8,128)}, f32[64,1,384]{2,0,1:T(8,128)S(1)}, u32[]{:S(2)}) copy-start(f32[64,1,384]{2,0,1:T(8,128)S(1)} %copy.38) | copy-start | bytes 294916
  174.5 3.6 %collective-permute-start.3 = (f32[1,1]{1,0:T(1,128)}, f32[1,1]{1,0:T(1,128)}, u32[]{:S(2)}, u32[]{:S(2)}) collective-permute-start(f32[1,1]{1,0:T(1,128)} %bitcast.11), channel_id=1, source_target_pairs={{0,64},{64,0},{1,65},{65,1},{2,66},{66,2},{3,67},{67,3},{4,68},{68... | collective-permute-start | bytes 20 | tf_op jit(solution)/shard_map/ppermute | solution.py:730
  178.8 123.8 %copy-start.9 = (s32[2048,2]{0,1:T(2,128)S(1)}, s32[2048,2]{0,1:T(2,128)}, u32[]{:S(2)}) copy-start(s32[2048,2]{0,1:T(2,128)} %param.11) | copy-start | bytes 49156
  178.8 123.8 %copy-start.11 = (f32[2048,2]{0,1:T(2,128)S(1)}, f32[2048,2]{0,1:T(2,128)}, u32[]{:S(2)}) copy-start(f32[2048,2]{0,1:T(2,128)} %param.12) | copy-start | bytes 49156
  303.9 3.2 %copy-start.12 = (f32[2048,2]{0,1:T(2,128)}, f32[2048,2]{0,1:T(2,128)S(1)}, u32[]{:S(2)}) copy-start(f32[2048,2]{0,1:T(2,128)S(1)} %get-tuple-element.136) | copy-start | bytes 49156
  303.9 3.1 %copy-start.5 = (f32[2,256,512]{2,1,0:T(8,128)S(1)}, f32[2,256,512]{2,1,0:T(8,128)}, u32[]{:S(2)}) copy-start(f32[2,256,512]{2,1,0:T(8,128)} %get-tuple-element.137) | copy-start | bytes 3145732
  307.0 1.6 copy-start.6
  307.0 2.6 copy-start.7
